TPU v7x, 32 devices: a whole 2x2x4 slice. The times are simulated.
32 devices in a mesh: gx: 16 (over z, y, core), gy: 2 (over x).
Axes of the slice: x: 2, y: 2, z: 4, core: 2. Of those that a mesh axis runs over, the one named last changes fastest.
Arguments:
- forcing: float32 [128, 16, 128], P('gx', 'gy'), may hold values from -12 to 12
- kappa: float32 [16, 2, 16], P('gx', 'gy'), may hold values from 0.25 to 4
- sigma: float32 [16, 2, 16], P('gx', 'gy'), may hold values from 0.5 to 8
Outputs:
- solution: float32 [128, 16, 128], P('gx', 'gy')
- residual: float32 [128, 16, 128], P('gx', 'gy')
- rel_residual: float32 [], replicated
All inputs are finite; a program needn't handle non-finite values.
Results may differ from a plain program's by a relative error of at most 0.0003.
Values sent between devices are 32-bit elements; how exact they have to be, the bound alone decides.
No kernel may reach another device: no remote copies, remote signals or barrier semaphores. Data moves between devices by JAX's collectives and lax.ppermute only.
A program may use at most 64 MiB of HBM per device.

v0:
```python
import jax
import jax.numpy as jnp
import numpy as np
from jax import lax
from jax.sharding import PartitionSpec as P


def with_halo(cells, sides, width):
    for axis, dim in sides:
        count = lax.axis_size(axis)
        head = lax.slice_in_dim(cells, 0, width, axis=dim)
        tail = lax.slice_in_dim(cells, cells.shape[dim] - width, cells.shape[dim], axis=dim)
        cells = jnp.concatenate(
            [
                lax.ppermute(tail, axis, [(i, (i + 1) % count) for i in range(count)]),
                cells,
                lax.ppermute(head, axis, [((i + 1) % count, i) for i in range(count)]),
            ],
            axis=dim,
        )
    return cells


def legendre_table(points, order):
    columns = [points * 0.0 + 1.0, points]
    for degree in range(2, order + 1):
        columns.append(
            ((2 * degree - 1) * points * columns[-1] - (degree - 1) * columns[-2]) / degree
        )
    return np.stack(columns, axis=1)


def lobatto(count):
    order = count - 1
    points = np.cos(np.pi * np.arange(count) / order)
    for sweep in range(60):
        table = legendre_table(points, order)
        points = points - (points * table[:, order] - table[:, order - 1]) / (
            count * table[:, order]
        )
    table = legendre_table(points, order)
    weights = 2.0 / (order * count * table[:, order] ** 2)
    values = table[:, order]
    points, weights, values = (points[::-1], weights[::-1], values[::-1])
    spread = points[:, None] - points[None, :] + np.eye(count)
    deriv = values[:, None] / values[None, :] / spread * (1.0 - np.eye(count))
    corner = order * (order + 1) / 4.0
    ends = np.array([-corner] + [0.0] * (count - 2) + [corner])
    return (points, weights, deriv + np.eye(count) * ends[None, :])


def lagrange(fine_points, coarse_points):
    columns = []
    for column in range(len(coarse_points)):
        value = fine_points * 0.0 + 1.0
        for other in range(len(coarse_points)):
            if other != column:
                value = (
                    value
                    * (fine_points - coarse_points[other])
                    / (coarse_points[column] - coarse_points[other])
                )
        columns.append(value)
    return np.stack(columns, axis=1)


def edge_factor(count, blocks):
    index = jnp.arange(count)
    single = jnp.where((index == 0) | (index == count - 1), 0.5, 1.0).astype(jnp.float32)
    return jnp.tile(single, blocks)


def multiplicity(count, blocks):
    first = edge_factor(count, blocks[0])
    second = edge_factor(count, blocks[1])
    third = edge_factor(count, blocks[2])
    return first[:, None, None] * second[None, :, None] * third[None, None, :]


def element_apply(field, kappa, sigma, deriv, weights):
    count = deriv.shape[0]
    ex, ey, ez = kappa.shape
    high = lax.Precision.HIGHEST
    block = field.reshape(ex, count, ey, count, ez, count)
    mass = (weights[:, None, None] * weights[None, :, None] * weights[None, None, :])[
        None, :, None, :, None, :
    ]
    first = jnp.einsum("ai,eifjgk->eafjgk", deriv, block, precision=high)
    total = jnp.einsum("ai,eafjgk->eifjgk", deriv, first * mass, precision=high)
    second = jnp.einsum("aj,eifjgk->eifagk", deriv, block, precision=high)
    total = total + jnp.einsum("aj,eifagk->eifjgk", deriv, second * mass, precision=high)
    third = jnp.einsum("ak,eifjgk->eifjga", deriv, block, precision=high)
    total = total + jnp.einsum("ak,eifjga->eifjgk", deriv, third * mass, precision=high)
    coeff = kappa[:, None, :, None, :, None]
    shift = sigma[:, None, :, None, :, None]
    return (coeff * total + shift * mass * block).reshape(field.shape)


def element_diagonal(kappa, sigma, deriv, weights):
    count = deriv.shape[0]
    ex, ey, ez = kappa.shape
    stiff = jnp.sum(deriv * deriv * weights[:, None], axis=0)
    term = stiff[:, None, None] * weights[None, :, None] * weights[None, None, :]
    term = term + weights[:, None, None] * stiff[None, :, None] * weights[None, None, :]
    term = term + weights[:, None, None] * weights[None, :, None] * stiff[None, None, :]
    mass = weights[:, None, None] * weights[None, :, None] * weights[None, None, :]
    coeff = kappa[:, None, :, None, :, None]
    shift = sigma[:, None, :, None, :, None]
    full = coeff * term[None, :, None, :, None, :] + shift * mass[None, :, None, :, None, :]
    return full.reshape(ex * count, ey * count, ez * count)


def fold_axis(field, dim, count):
    size = field.shape[dim]
    position = jnp.arange(size) % count
    shape = [1, 1, 1]
    shape[dim] = size
    first = (position == 0).reshape(shape)
    last = (position == count - 1).reshape(shape)
    before = jnp.roll(field, 1, dim)
    after = jnp.roll(field, -1, dim)
    return field + jnp.where(first, before, 0.0) + jnp.where(last, after, 0.0)


def fold_padded(padded, dim, count):
    size = padded.shape[dim] - 2
    center = lax.slice_in_dim(padded, 1, size + 1, axis=dim)
    before = lax.slice_in_dim(padded, 0, size, axis=dim)
    after = lax.slice_in_dim(padded, 2, size + 2, axis=dim)
    position = jnp.arange(size) % count
    shape = [1, 1, 1]
    shape[dim] = size
    first = (position == 0).reshape(shape)
    last = (position == count - 1).reshape(shape)
    return center + jnp.where(first, before, 0.0) + jnp.where(last, after, 0.0)


def assemble(field, count, finest):
    if finest:
        padded = with_halo(field, (("gx", 0), ("gy", 1)), 1)
        field = fold_padded(fold_padded(padded, 0, count), 1, count)
    else:
        padded = with_halo(field, (("gx", 0), ("gy", 1)), 1)
        field = fold_padded(fold_padded(padded, 0, count), 1, count)
    return fold_axis(field, 2, count)


def restrict(field, interp, blocks, fine_count, coarse_count):
    high = lax.Precision.HIGHEST
    block = field.reshape(blocks[0], fine_count, blocks[1], fine_count, blocks[2], fine_count)
    one = jnp.einsum("ia,eifjgk->eafjgk", interp, block, precision=high)
    two = jnp.einsum("jb,eafjgk->eafbgk", interp, one, precision=high)
    three = jnp.einsum("kc,eafbgk->eafbgc", interp, two, precision=high)
    return three.reshape(
        blocks[0] * coarse_count, blocks[1] * coarse_count, blocks[2] * coarse_count
    )


def prolong(field, interp, blocks, fine_count, coarse_count):
    high = lax.Precision.HIGHEST
    block = field.reshape(blocks[0], coarse_count, blocks[1], coarse_count, blocks[2], coarse_count)
    one = jnp.einsum("ia,eafbgc->eifbgc", interp, block, precision=high)
    two = jnp.einsum("jb,eifbgc->eifjgc", interp, one, precision=high)
    three = jnp.einsum("kc,eifjgc->eifjgk", interp, two, precision=high)
    return three.reshape(blocks[0] * fine_count, blocks[1] * fine_count, blocks[2] * fine_count)


def local(forcing, kappa, sigma):
    blocks = kappa.shape
    counts = [8, 4, 2]
    tables = [lobatto(count) for count in counts]
    derivs = [jnp.asarray(table[2], jnp.float32) for table in tables]
    weights = [jnp.asarray(table[1], jnp.float32) for table in tables]
    interps = [
        jnp.asarray(lagrange(tables[level][0], tables[level + 1][0]), jnp.float32)
        for level in range(2)
    ]
    mults = [multiplicity(count, blocks) for count in counts]
    diags = [
        assemble(
            element_diagonal(kappa, sigma, derivs[level], weights[level]), counts[level], level == 0
        )
        for level in range(3)
    ]
    center = 1.65
    half = 1.35
    ratio = center / half

    def operate(field, level):
        return assemble(
            element_apply(field, kappa, sigma, derivs[level], weights[level]),
            counts[level],
            level == 0,
        )

    def smooth(resid, level, steps, keep_last):
        rho = 1.0 / ratio
        direction = resid / (center * diags[level])
        iterate = direction
        for step in range(steps):
            if step > 0:
                rho_next = 1.0 / (2.0 * ratio - rho)
                direction = (
                    rho_next * rho * direction + 2.0 * rho_next / half * resid / diags[level]
                )
                iterate = iterate + direction
                rho = rho_next
            if step < steps - 1 or keep_last:
                resid = resid - operate(direction, level)
        return (iterate, resid)

    def vcycle(resid, level):
        if level == 2:
            iterate, unused = smooth(resid, level, 2, False)
            return iterate
        iterate, resid = smooth(resid, level, 2, True)
        coarse = assemble(
            restrict(
                mults[level] * resid, interps[level], blocks, counts[level], counts[level + 1]
            ),
            counts[level + 1],
            False,
        )
        correction = prolong(
            vcycle(coarse, level + 1), interps[level], blocks, counts[level], counts[level + 1]
        )
        iterate = iterate + correction
        resid = resid - operate(correction, level)
        return iterate + resid / (center * diags[level])

    load = assemble(forcing, 8, True)
    first = vcycle(load, 0)
    image_first = operate(first, 0)
    second = vcycle(load - image_first, 0)
    combined = first + second
    image = operate(combined, 0)
    weight = mults[0]
    load_sq, load_image, image_sq = lax.psum(
        (
            jnp.sum(weight * load * load),
            jnp.sum(weight * load * image),
            jnp.sum(weight * image * image),
        ),
        ("gx", "gy"),
    )
    coef = load_image / image_sq
    solution = coef * combined
    residual = load - coef * image
    rel_residual = jnp.sqrt((load_sq - load_image * load_image / image_sq) / load_sq)
    return (solution, residual, rel_residual)


def solution(mesh):
    in_specs = (P("gx", "gy", None), P("gx", "gy", None), P("gx", "gy", None))
    out_specs = (P("gx", "gy", None), P("gx", "gy", None), P())
    return jax.shard_map(local, mesh=mesh, in_specs=in_specs, out_specs=out_specs, check_vma=False)
```

profile of v0, /device:TPU:0, one launch (start us, length us, event | category | flops | bytes accessed | tf_op | source)
XLA Modules:
  0.0 398.1 jit_solution(3525151297120584496)
XLA Ops:
  1.5 5.5 %collective-permute-start.37 = (f32[1,2,32]{2,1,0:T(2,128)S(1)}, f32[1,2,32]{2,1,0:T(2,128)S(1)}, u32[]{:S(2)}, u32[]{:S(2)}) collective-permute-start(f32[1,2,32]{2,1,0:T(2,128)S(1)} %slice.1301), channel_id=1, source_target_pairs={{2,0},{4,2},{6,4},{8,6},{10,8},{12,10},{14,12},{16,14},{18,16},{20... | collective-permute-start | bytes 776 | tf_op jit(solution)/shard_map/ppermute | solution.py:17
  7.0 4.5 %collective-permute-start.1 = (f32[1,8,128]{2,1,0:T(8,128)S(1)}, f32[1,8,128]{2,1,0:T(8,128)S(1)}, u32[]{:S(2)}, u32[]{:S(2)}) collective-permute-start(f32[1,8,128]{2,1,0:T(8,128)S(1)} %get-tuple-element.133), channel_id=1, source_target_pairs={{2,0},{4,2},{6,4},{8,6},{10,8},{12,10},{14,12},{16,14},{18,16},{20... | collective-permute-start | bytes 12296 | tf_op jit(solution)/shard_map/ppermute | solution.py:17
  17.3 4.5 %collective-permute-start.5 = (f32[1,8,128]{2,1,0:T(8,128)S(1)}, f32[1,8,128]{2,1,0:T(8,128)S(1)}, u32[]{:S(2)}, u32[]{:S(2)}) collective-permute-start(f32[1,8,128]{2,1,0:T(8,128)S(1)} %slice.1175), channel_id=1, source_target_pairs={{2,0},{4,2},{6,4},{8,6},{10,8},{12,10},{14,12},{16,14},{18,16},{20... | collective-permute-start | bytes 12296 | tf_op jit(solution)/shard_map/ppermute | solution.py:17
  23.0 1.5 collective-permute-start.2
  25.0 1.6 collective-permute-done.2
  26.6 1.5 collective-permute-start.6
  28.6 1.6 collective-permute-done.6
  30.2 1.5 collective-permute-done.7
  33.8 3.7 fusion.486
  41.2 4.6 %collective-permute-start.9 = (f32[1,8,128]{2,1,0:T(8,128)S(1)}, f32[1,8,128]{2,1,0:T(8,128)S(1)}, u32[]{:S(2)}, u32[]{:S(2)}) collective-permute-start(f32[1,8,128]{2,1,0:T(8,128)S(1)} %slice.1191), channel_id=1, source_target_pairs={{2,0},{4,2},{6,4},{8,6},{10,8},{12,10},{14,12},{16,14},{18,16},{20... | collective-permute-start | bytes 12296 | tf_op jit(solution)/shard_map/ppermute | solution.py:17
  47.8 1.5 collective-permute-start.11
  49.4 1.5 collective-permute-done.10
  52.2 3.7 fusion.488
  60.3 4.5 %collective-permute-start.13 = (f32[1,8,128]{2,1,0:T(8,128)S(1)}, f32[1,8,128]{2,1,0:T(8,128)S(1)}, u32[]{:S(2)}, u32[]{:S(2)}) collective-permute-start(f32[1,8,128]{2,1,0:T(8,128)S(1)} %slice.1207), channel_id=1, source_target_pairs={{2,0},{4,2},{6,4},{8,6},{10,8},{12,10},{14,12},{16,14},{18,16},{20... | collective-permute-start | bytes 12296 | tf_op jit(solution)/shard_map/ppermute | solution.py:17
  66.2 1.6 collective-permute-start.14
  69.9 3.3 collective-permute-start.21
  75.7 1.6 collective-permute-start.22
  78.3 3.1 collective-permute-done.16
  83.5 1.5 collective-permute-start.18
  85.7 1.5 collective-permute-done.18
  87.2 1.5 collective-permute-done.19
  93.6 4.5 %collective-permute-start.25 = (f32[1,4,64]{2,1,0:T(4,128)S(1)}, f32[1,4,64]{2,1,0:T(4,128)S(1)}, u32[]{:S(2)}, u32[]{:S(2)}) collective-permute-start(f32[1,4,64]{2,1,0:T(4,128)S(1)} %slice.1255), channel_id=1, source_target_pairs={{2,0},{4,2},{6,4},{8,6},{10,8},{12,10},{14,12},{16,14},{18,16},{20... | collective-permute-start | bytes 3080 | tf_op jit(solution)/shard_map/ppermute | solution.py:17
  107.9 4.7 %collective-permute-start.29 = (f32[1,4,64]{2,1,0:T(4,128)S(1)}, f32[1,4,64]{2,1,0:T(4,128)S(1)}, u32[]{:S(2)}, u32[]{:S(2)}) collective-permute-start(f32[1,4,64]{2,1,0:T(4,128)S(1)} %slice.1271), channel_id=1, source_target_pairs={{2,0},{4,2},{6,4},{8,6},{10,8},{12,10},{14,12},{16,14},{18,16},{20... | collective-permute-start | bytes 3080 | tf_op jit(solution)/shard_map/ppermute | solution.py:17
  113.9 1.5 collective-permute-start.30
  116.0 1.5 collective-permute-start.38
  121.3 4.5 %collective-permute-start.33 = (f32[1,2,32]{2,1,0:T(2,128)S(1)}, f32[1,2,32]{2,1,0:T(2,128)S(1)}, u32[]{:S(2)}, u32[]{:S(2)}) collective-permute-start(f32[1,2,32]{2,1,0:T(2,128)S(1)} %slice.1287), channel_id=1, source_target_pairs={{2,0},{4,2},{6,4},{8,6},{10,8},{12,10},{14,12},{16,14},{18,16},{20... | collective-permute-start | bytes 776 | tf_op jit(solution)/shard_map/ppermute | solution.py:17
  127.7 1.5 collective-permute-start.35
  129.2 1.5 collective-permute-done.34
  134.7 4.5 %collective-permute-start.41 = (f32[1,2,32]{2,1,0:T(2,128)S(1)}, f32[1,2,32]{2,1,0:T(2,128)S(1)}, u32[]{:S(2)}, u32[]{:S(2)}) collective-permute-start(f32[1,2,32]{2,1,0:T(2,128)S(1)} %slice.1319), channel_id=1, source_target_pairs={{2,0},{4,2},{6,4},{8,6},{10,8},{12,10},{14,12},{16,14},{18,16},{20... | collective-permute-start | bytes 776 | tf_op jit(solution)/shard_map/ppermute | solution.py:17
  140.5 1.5 collective-permute-start.42
  142.6 1.6 collective-permute-done.42
  149.1 4.5 %collective-permute-start.45 = (f32[1,4,64]{2,1,0:T(4,128)S(1)}, f32[1,4,64]{2,1,0:T(4,128)S(1)}, u32[]{:S(2)}, u32[]{:S(2)}) collective-permute-start(f32[1,4,64]{2,1,0:T(4,128)S(1)} %slice.1335), channel_id=1, source_target_pairs={{2,0},{4,2},{6,4},{8,6},{10,8},{12,10},{14,12},{16,14},{18,16},{20... | collective-permute-start | bytes 3080 | tf_op jit(solution)/shard_map/ppermute | solution.py:17
  164.9 4.9 %collective-permute-start.49 = (f32[1,8,128]{2,1,0:T(8,128)S(1)}, f32[1,8,128]{2,1,0:T(8,128)S(1)}, u32[]{:S(2)}, u32[]{:S(2)}) collective-permute-start(f32[1,8,128]{2,1,0:T(8,128)S(1)} %slice.1351), channel_id=1, source_target_pairs={{2,0},{4,2},{6,4},{8,6},{10,8},{12,10},{14,12},{16,14},{18,16},{20... | collective-permute-start | bytes 12296 | tf_op jit(solution)/shard_map/ppermute | solution.py:17
  171.1 1.5 collective-permute-start.50
  177.1 3.7 fusion.497
  185.2 4.5 %collective-permute-start.53 = (f32[1,8,128]{2,1,0:T(8,128)S(1)}, f32[1,8,128]{2,1,0:T(8,128)S(1)}, u32[]{:S(2)}, u32[]{:S(2)}) collective-permute-start(f32[1,8,128]{2,1,0:T(8,128)S(1)} %slice.1367), channel_id=1, source_target_pairs={{2,0},{4,2},{6,4},{8,6},{10,8},{12,10},{14,12},{16,14},{18,16},{20... | collective-permute-start | bytes 12296 | tf_op jit(solution)/shard_map/ppermute | solution.py:17
  193.1 1.6 collective-permute-done.54
  196.0 3.7 fusion.499
  204.2 4.7 %collective-permute-start.57 = (f32[1,8,128]{2,1,0:T(8,128)S(1)}, f32[1,8,128]{2,1,0:T(8,128)S(1)}, u32[]{:S(2)}, u32[]{:S(2)}) collective-permute-start(f32[1,8,128]{2,1,0:T(8,128)S(1)} %slice.1383), channel_id=1, source_target_pairs={{2,0},{4,2},{6,4},{8,6},{10,8},{12,10},{14,12},{16,14},{18,16},{20... | collective-permute-start | bytes 12296 | tf_op jit(solution)/shard_map/ppermute | solution.py:17
  210.2 1.5 collective-permute-start.58
  212.3 1.6 collective-permute-done.58
  216.1 3.7 fusion.501
  224.3 4.5 %collective-permute-start.61 = (f32[1,8,128]{2,1,0:T(8,128)S(1)}, f32[1,8,128]{2,1,0:T(8,128)S(1)}, u32[]{:S(2)}, u32[]{:S(2)}) collective-permute-start(f32[1,8,128]{2,1,0:T(8,128)S(1)} %slice.1399), channel_id=1, source_target_pairs={{2,0},{4,2},{6,4},{8,6},{10,8},{12,10},{14,12},{16,14},{18,16},{20... | collective-permute-start | bytes 12296 | tf_op jit(solution)/shard_map/ppermute | solution.py:17
  232.2 1.6 collective-permute-done.62
  236.8 4.5 %collective-permute-start.65 = (f32[1,4,64]{2,1,0:T(4,128)S(1)}, f32[1,4,64]{2,1,0:T(4,128)S(1)}, u32[]{:S(2)}, u32[]{:S(2)}) collective-permute-start(f32[1,4,64]{2,1,0:T(4,128)S(1)} %slice.1415), channel_id=1, source_target_pairs={{2,0},{4,2},{6,4},{8,6},{10,8},{12,10},{14,12},{16,14},{18,16},{20... | collective-permute-start | bytes 3080 | tf_op jit(solution)/shard_map/ppermute | solution.py:17
  242.6 1.5 collective-permute-start.66
  244.7 1.6 collective-permute-done.66
  251.9 4.5 %collective-permute-start.69 = (f32[1,4,64]{2,1,0:T(4,128)S(1)}, f32[1,4,64]{2,1,0:T(4,128)S(1)}, u32[]{:S(2)}, u32[]{:S(2)}) collective-permute-start(f32[1,4,64]{2,1,0:T(4,128)S(1)} %slice.1431), channel_id=1, source_target_pairs={{2,0},{4,2},{6,4},{8,6},{10,8},{12,10},{14,12},{16,14},{18,16},{20... | collective-permute-start | bytes 3080 | tf_op jit(solution)/shard_map/ppermute | solution.py:17
  259.8 1.6 collective-permute-done.70
  266.1 4.7 %collective-permute-start.73 = (f32[1,4,64]{2,1,0:T(4,128)S(1)}, f32[1,4,64]{2,1,0:T(4,128)S(1)}, u32[]{:S(2)}, u32[]{:S(2)}) collective-permute-start(f32[1,4,64]{2,1,0:T(4,128)S(1)} %slice.1447), channel_id=1, source_target_pairs={{2,0},{4,2},{6,4},{8,6},{10,8},{12,10},{14,12},{16,14},{18,16},{20... | collective-permute-start | bytes 3080 | tf_op jit(solution)/shard_map/ppermute | solution.py:17
  272.2 1.5 collective-permute-start.74
  274.3 1.6 collective-permute-done.74
  279.1 4.5 %collective-permute-start.77 = (f32[1,2,32]{2,1,0:T(2,128)S(1)}, f32[1,2,32]{2,1,0:T(2,128)S(1)}, u32[]{:S(2)}, u32[]{:S(2)}) collective-permute-start(f32[1,2,32]{2,1,0:T(2,128)S(1)} %slice.1463), channel_id=1, source_target_pairs={{2,0},{4,2},{6,4},{8,6},{10,8},{12,10},{14,12},{16,14},{18,16},{20... | collective-permute-start | bytes 776 | tf_op jit(solution)/shard_map/ppermute | solution.py:17
  286.9 1.6 collective-permute-done.78
  291.7 4.5 %collective-permute-start.81 = (f32[1,2,32]{2,1,0:T(2,128)S(1)}, f32[1,2,32]{2,1,0:T(2,128)S(1)}, u32[]{:S(2)}, u32[]{:S(2)}) collective-permute-start(f32[1,2,32]{2,1,0:T(2,128)S(1)} %slice.1479), channel_id=1, source_target_pairs={{2,0},{4,2},{6,4},{8,6},{10,8},{12,10},{14,12},{16,14},{18,16},{20... | collective-permute-start | bytes 776 | tf_op jit(solution)/shard_map/ppermute | solution.py:17
  297.5 1.5 collective-permute-start.82
  299.6 1.6 collective-permute-done.82
  306.1 4.5 %collective-permute-start.85 = (f32[1,4,64]{2,1,0:T(4,128)S(1)}, f32[1,4,64]{2,1,0:T(4,128)S(1)}, u32[]{:S(2)}, u32[]{:S(2)}) collective-permute-start(f32[1,4,64]{2,1,0:T(4,128)S(1)} %slice.1495), channel_id=1, source_target_pairs={{2,0},{4,2},{6,4},{8,6},{10,8},{12,10},{14,12},{16,14},{18,16},{20... | collective-permute-start | bytes 3080 | tf_op jit(solution)/shard_map/ppermute | solution.py:17
  322.0 4.7 %collective-permute-start.89 = (f32[1,8,128]{2,1,0:T(8,128)S(1)}, f32[1,8,128]{2,1,0:T(8,128)S(1)}, u32[]{:S(2)}, u32[]{:S(2)}) collective-permute-start(f32[1,8,128]{2,1,0:T(8,128)S(1)} %slice.1511), channel_id=1, source_target_pairs={{2,0},{4,2},{6,4},{8,6},{10,8},{12,10},{14,12},{16,14},{18,16},{20... | collective-permute-start | bytes 12296 | tf_op jit(solution)/shard_map/ppermute | solution.py:17
  328.1 1.5 collective-permute-start.90
  334.0 3.7 fusion.510
  342.1 4.5 %collective-permute-start.93 = (f32[1,8,128]{2,1,0:T(8,128)S(1)}, f32[1,8,128]{2,1,0:T(8,128)S(1)}, u32[]{:S(2)}, u32[]{:S(2)}) collective-permute-start(f32[1,8,128]{2,1,0:T(8,128)S(1)} %slice.1527), channel_id=1, source_target_pairs={{2,0},{4,2},{6,4},{8,6},{10,8},{12,10},{14,12},{16,14},{18,16},{20... | collective-permute-start | bytes 12296 | tf_op jit(solution)/shard_map/ppermute | solution.py:17
  350.1 1.6 collective-permute-done.94
  353.3 37.5 %all-reduce = (f32[]{:T(128)}, f32[]{:T(128)}, f32[]{:T(128)}) all-reduce(f32[]{:T(128)} %get-tuple-element.4, f32[]{:T(128)} %get-tuple-element.5, f32[]{:T(128)} %get-tuple-element.3), channel_id=1, replica_groups=mesh['gx'=16,'gy'=2] {'gx','gy'}, use_global_device_ids=true, to_apply=%region_4.5 | all-reduce | flops 3 | bytes 24 | tf_op jit(solution)/shard_map/psum | solution.py:238
  (809 shorter events, 170.7 us)
Async XLA Ops:
  1.5 106.0 %collective-permute-start.37 = (f32[1,2,32]{2,1,0:T(2,128)S(1)}, f32[1,2,32]{2,1,0:T(2,128)S(1)}, u32[]{:S(2)}, u32[]{:S(2)}) collective-permute-start(f32[1,2,32]{2,1,0:T(2,128)S(1)} %slice.1301), channel_id=1, source_target_pairs={{2,0},{4,2},{6,4},{8,6},{10,8},{12,10},{14,12},{16,14},{18,16},{20... | collective-permute-start | bytes 776 | tf_op jit(solution)/shard_map/ppermute | solution.py:17
  7.0 100.5 %collective-permute-start.36 = (f32[1,2,32]{2,1,0:T(2,128)S(1)}, f32[1,2,32]{2,1,0:T(2,128)S(1)}, u32[]{:S(2)}, u32[]{:S(2)}) collective-permute-start(f32[1,2,32]{2,1,0:T(2,128)S(1)} %slice.1301), channel_id=1, source_target_pairs={{0,2},{2,4},{4,6},{6,8},{8,10},{10,12},{12,14},{14,16},{16,18},{18... | collective-permute-start | bytes 776 | tf_op jit(solution)/shard_map/ppermute | solution.py:15
  7.0 10.2 %collective-permute-start.1 = (f32[1,8,128]{2,1,0:T(8,128)S(1)}, f32[1,8,128]{2,1,0:T(8,128)S(1)}, u32[]{:S(2)}, u32[]{:S(2)}) collective-permute-start(f32[1,8,128]{2,1,0:T(8,128)S(1)} %get-tuple-element.133), channel_id=1, source_target_pairs={{2,0},{4,2},{6,4},{8,6},{10,8},{12,10},{14,12},{16,14},{18,16},{20... | collective-permute-start | bytes 12296 | tf_op jit(solution)/shard_map/ppermute | solution.py:17
  11.5 5.7 %collective-permute-start = (f32[1,8,128]{2,1,0:T(8,128)S(1)}, f32[1,8,128]{2,1,0:T(8,128)S(1)}, u32[]{:S(2)}, u32[]{:S(2)}) collective-permute-start(f32[1,8,128]{2,1,0:T(8,128)S(1)} %get-tuple-element.134), channel_id=1, source_target_pairs={{0,2},{2,4},{4,6},{6,8},{8,10},{10,12},{12,14},{14,16},{16,18},{18... | collective-permute-start | bytes 12296 | tf_op jit(solution)/shard_map/ppermute | solution.py:15
  12.7 63.0 %collective-permute-start.20 = (f32[1,4,64]{2,1,0:T(4,128)S(1)}, f32[1,4,64]{2,1,0:T(4,128)S(1)}, u32[]{:S(2)}, u32[]{:S(2)}) collective-permute-start(f32[1,4,64]{2,1,0:T(4,128)S(1)} %slice.1237), channel_id=1, source_target_pairs={{0,2},{2,4},{4,6},{6,8},{8,10},{10,12},{12,14},{14,16},{16,18},{18... | collective-permute-start | bytes 3080 | tf_op jit(solution)/shard_map/ppermute | solution.py:15
  17.2 5.7 %collective-permute-start.4 = (f32[1,8,128]{2,1,0:T(8,128)S(1)}, f32[1,8,128]{2,1,0:T(8,128)S(1)}, u32[]{:S(2)}, u32[]{:S(2)}) collective-permute-start(f32[1,8,128]{2,1,0:T(8,128)S(1)} %slice.1173), channel_id=1, source_target_pairs={{0,2},{2,4},{4,6},{6,8},{8,10},{10,12},{12,14},{14,16},{16,18},{18... | collective-permute-start | bytes 12296 | tf_op jit(solution)/shard_map/ppermute | solution.py:15
  17.3 7.2 %collective-permute-start.5 = (f32[1,8,128]{2,1,0:T(8,128)S(1)}, f32[1,8,128]{2,1,0:T(8,128)S(1)}, u32[]{:S(2)}, u32[]{:S(2)}) collective-permute-start(f32[1,8,128]{2,1,0:T(8,128)S(1)} %slice.1175), channel_id=1, source_target_pairs={{2,0},{4,2},{6,4},{8,6},{10,8},{12,10},{14,12},{16,14},{18,16},{20... | collective-permute-start | bytes 12296 | tf_op jit(solution)/shard_map/ppermute | solution.py:17
  40.7 5.8 %collective-permute-start.8 = (f32[1,8,128]{2,1,0:T(8,128)S(1)}, f32[1,8,128]{2,1,0:T(8,128)S(1)}, u32[]{:S(2)}, u32[]{:S(2)}) collective-permute-start(f32[1,8,128]{2,1,0:T(8,128)S(1)} %slice.1189), channel_id=1, source_target_pairs={{0,2},{2,4},{4,6},{6,8},{8,10},{10,12},{12,14},{14,16},{16,18},{18... | collective-permute-start | bytes 12296 | tf_op jit(solution)/shard_map/ppermute | solution.py:15
  41.2 6.0 %collective-permute-start.9 = (f32[1,8,128]{2,1,0:T(8,128)S(1)}, f32[1,8,128]{2,1,0:T(8,128)S(1)}, u32[]{:S(2)}, u32[]{:S(2)}) collective-permute-start(f32[1,8,128]{2,1,0:T(8,128)S(1)} %slice.1191), channel_id=1, source_target_pairs={{2,0},{4,2},{6,4},{8,6},{10,8},{12,10},{14,12},{16,14},{18,16},{20... | collective-permute-start | bytes 12296 | tf_op jit(solution)/shard_map/ppermute | solution.py:17
  47.2 3.7 collective-permute-start.10
  59.8 5.8 %collective-permute-start.12 = (f32[1,8,128]{2,1,0:T(8,128)S(1)}, f32[1,8,128]{2,1,0:T(8,128)S(1)}, u32[]{:S(2)}, u32[]{:S(2)}) collective-permute-start(f32[1,8,128]{2,1,0:T(8,128)S(1)} %slice.1205), channel_id=1, source_target_pairs={{0,2},{2,4},{4,6},{6,8},{8,10},{10,12},{12,14},{14,16},{16,18},{18... | collective-permute-start | bytes 12296 | tf_op jit(solution)/shard_map/ppermute | solution.py:15
  60.3 5.8 %collective-permute-start.13 = (f32[1,8,128]{2,1,0:T(8,128)S(1)}, f32[1,8,128]{2,1,0:T(8,128)S(1)}, u32[]{:S(2)}, u32[]{:S(2)}) collective-permute-start(f32[1,8,128]{2,1,0:T(8,128)S(1)} %slice.1207), channel_id=1, source_target_pairs={{2,0},{4,2},{6,4},{8,6},{10,8},{12,10},{14,12},{16,14},{18,16},{20... | collective-permute-start | bytes 12296 | tf_op jit(solution)/shard_map/ppermute | solution.py:17
  66.2 3.7 collective-permute-start.14
  67.7 5.4 %collective-permute-start.15 = (f32[10,1,128]{2,1,0:T(1,128)S(1)}, f32[10,1,128]{2,1,0:T(1,128)S(1)}, u32[]{:S(2)}, u32[]{:S(2)}) collective-permute-start(f32[10,1,128]{2,1,0:T(1,128)S(1)} %get-tuple-element.72), channel_id=1, source_target_pairs={{1,0},{0,1},{3,2},{2,3},{5,4},{4,5},{7,6},{6,7},{9,8},{8,9},{11,10... | collective-permute-start | bytes 15368 | tf_op jit(solution)/shard_map/ppermute | solution.py:17
  69.9 5.9 %collective-permute-start.21 = (f32[1,4,64]{2,1,0:T(4,128)S(1)}, f32[1,4,64]{2,1,0:T(4,128)S(1)}, u32[]{:S(2)}, u32[]{:S(2)}) collective-permute-start(f32[1,4,64]{2,1,0:T(4,128)S(1)} %slice.1239), channel_id=1, source_target_pairs={{2,0},{4,2},{6,4},{8,6},{10,8},{12,10},{14,12},{16,14},{18,16},{20... | collective-permute-start | bytes 3080 | tf_op jit(solution)/shard_map/ppermute | solution.py:17
  75.6 5.8 %collective-permute-start.16 = (f32[1,4,64]{2,1,0:T(4,128)S(1)}, f32[1,4,64]{2,1,0:T(4,128)S(1)}, u32[]{:S(2)}, u32[]{:S(2)}) collective-permute-start(f32[1,4,64]{2,1,0:T(4,128)S(1)} %slice.1221), channel_id=1, source_target_pairs={{0,2},{2,4},{4,6},{6,8},{8,10},{10,12},{12,14},{14,16},{16,18},{18... | collective-permute-start | bytes 3080 | tf_op jit(solution)/shard_map/ppermute | solution.py:15
  75.7 9.4 %collective-permute-start.22 = (f32[6,1,64]{2,1,0:T(1,128)S(1)}, f32[6,1,64]{2,1,0:T(1,128)S(1)}, u32[]{:S(2)}, u32[]{:S(2)}) collective-permute-start(f32[6,1,64]{2,1,0:T(1,128)S(1)} %get-tuple-element.155), channel_id=1, source_target_pairs={{0,1},{1,0},{2,3},{3,2},{4,5},{5,4},{6,7},{7,6},{8,9},{9,8},{10,11... | collective-permute-start | bytes 4616 | tf_op jit(solution)/shard_map/ppermute | solution.py:15
  77.3 8.3 %collective-permute-start.23 = (f32[6,1,64]{2,1,0:T(1,128)S(1)}, f32[6,1,64]{2,1,0:T(1,128)S(1)}, u32[]{:S(2)}, u32[]{:S(2)}) collective-permute-start(f32[6,1,64]{2,1,0:T(1,128)S(1)} %get-tuple-element.156), channel_id=1, source_target_pairs={{1,0},{0,1},{3,2},{2,3},{5,4},{4,5},{7,6},{6,7},{9,8},{8,9},{11,10... | collective-permute-start | bytes 4616 | tf_op jit(solution)/shard_map/ppermute | solution.py:17
  83.5 3.7 collective-permute-start.18
  93.2 5.8 %collective-permute-start.24 = (f32[1,4,64]{2,1,0:T(4,128)S(1)}, f32[1,4,64]{2,1,0:T(4,128)S(1)}, u32[]{:S(2)}, u32[]{:S(2)}) collective-permute-start(f32[1,4,64]{2,1,0:T(4,128)S(1)} %slice.1253), channel_id=1, source_target_pairs={{0,2},{2,4},{4,6},{6,8},{8,10},{10,12},{12,14},{14,16},{16,18},{18... | collective-permute-start | bytes 3080 | tf_op jit(solution)/shard_map/ppermute | solution.py:15
  93.6 5.8 %collective-permute-start.25 = (f32[1,4,64]{2,1,0:T(4,128)S(1)}, f32[1,4,64]{2,1,0:T(4,128)S(1)}, u32[]{:S(2)}, u32[]{:S(2)}) collective-permute-start(f32[1,4,64]{2,1,0:T(4,128)S(1)} %slice.1255), channel_id=1, source_target_pairs={{2,0},{4,2},{6,4},{8,6},{10,8},{12,10},{14,12},{16,14},{18,16},{20... | collective-permute-start | bytes 3080 | tf_op jit(solution)/shard_map/ppermute | solution.py:17
  99.4 3.7 collective-permute-start.26
  107.4 5.8 %collective-permute-start.28 = (f32[1,4,64]{2,1,0:T(4,128)S(1)}, f32[1,4,64]{2,1,0:T(4,128)S(1)}, u32[]{:S(2)}, u32[]{:S(2)}) collective-permute-start(f32[1,4,64]{2,1,0:T(4,128)S(1)} %slice.1269), channel_id=1, source_target_pairs={{0,2},{2,4},{4,6},{6,8},{8,10},{10,12},{12,14},{14,16},{16,18},{18... | collective-permute-start | bytes 3080 | tf_op jit(solution)/shard_map/ppermute | solution.py:15
  107.9 6.0 %collective-permute-start.29 = (f32[1,4,64]{2,1,0:T(4,128)S(1)}, f32[1,4,64]{2,1,0:T(4,128)S(1)}, u32[]{:S(2)}, u32[]{:S(2)}) collective-permute-start(f32[1,4,64]{2,1,0:T(4,128)S(1)} %slice.1271), channel_id=1, source_target_pairs={{2,0},{4,2},{6,4},{8,6},{10,8},{12,10},{14,12},{16,14},{18,16},{20... | collective-permute-start | bytes 3080 | tf_op jit(solution)/shard_map/ppermute | solution.py:17
  113.9 4.1 %collective-permute-start.30 = (f32[6,1,64]{2,1,0:T(1,128)S(1)}, f32[6,1,64]{2,1,0:T(1,128)S(1)}, u32[]{:S(2)}, u32[]{:S(2)}) collective-permute-start(f32[6,1,64]{2,1,0:T(1,128)S(1)} %get-tuple-element.149), channel_id=1, source_target_pairs={{0,1},{1,0},{2,3},{3,2},{4,5},{5,4},{6,7},{7,6},{8,9},{9,8},{10,11... | collective-permute-start | bytes 4616 | tf_op jit(solution)/shard_map/ppermute | solution.py:15
  116.0 13.2 %collective-permute-start.38 = (f32[4,1,32]{2,1,0:T(1,128)S(1)}, f32[4,1,32]{2,1,0:T(1,128)S(1)}, u32[]{:S(2)}, u32[]{:S(2)}) collective-permute-start(f32[4,1,32]{2,1,0:T(1,128)S(1)} %get-tuple-element.207), channel_id=1, source_target_pairs={{0,1},{1,0},{2,3},{3,2},{4,5},{5,4},{6,7},{7,6},{8,9},{9,8},{10,11... | collective-permute-start | bytes 1544 | tf_op jit(solution)/shard_map/ppermute | solution.py:15
  117.4 11.7 %collective-permute-start.39 = (f32[4,1,32]{2,1,0:T(1,128)S(1)}, f32[4,1,32]{2,1,0:T(1,128)S(1)}, u32[]{:S(2)}, u32[]{:S(2)}) collective-permute-start(f32[4,1,32]{2,1,0:T(1,128)S(1)} %get-tuple-element.208), channel_id=1, source_target_pairs={{1,0},{0,1},{3,2},{2,3},{5,4},{4,5},{7,6},{6,7},{9,8},{8,9},{11,10... | collective-permute-start | bytes 1544 | tf_op jit(solution)/shard_map/ppermute | solution.py:17
  121.0 5.7 %collective-permute-start.32 = (f32[1,2,32]{2,1,0:T(2,128)S(1)}, f32[1,2,32]{2,1,0:T(2,128)S(1)}, u32[]{:S(2)}, u32[]{:S(2)}) collective-permute-start(f32[1,2,32]{2,1,0:T(2,128)S(1)} %slice.1285), channel_id=1, source_target_pairs={{0,2},{2,4},{4,6},{6,8},{8,10},{10,12},{12,14},{14,16},{16,18},{18... | collective-permute-start | bytes 776 | tf_op jit(solution)/shard_map/ppermute | solution.py:15
  121.3 5.8 %collective-permute-start.33 = (f32[1,2,32]{2,1,0:T(2,128)S(1)}, f32[1,2,32]{2,1,0:T(2,128)S(1)}, u32[]{:S(2)}, u32[]{:S(2)}) collective-permute-start(f32[1,2,32]{2,1,0:T(2,128)S(1)} %slice.1287), channel_id=1, source_target_pairs={{2,0},{4,2},{6,4},{8,6},{10,8},{12,10},{14,12},{16,14},{18,16},{20... | collective-permute-start | bytes 776 | tf_op jit(solution)/shard_map/ppermute | solution.py:17
  134.4 5.7 %collective-permute-start.40 = (f32[1,2,32]{2,1,0:T(2,128)S(1)}, f32[1,2,32]{2,1,0:T(2,128)S(1)}, u32[]{:S(2)}, u32[]{:S(2)}) collective-permute-start(f32[1,2,32]{2,1,0:T(2,128)S(1)} %slice.1317), channel_id=1, source_target_pairs={{0,2},{2,4},{4,6},{6,8},{8,10},{10,12},{12,14},{14,16},{16,18},{18... | collective-permute-start | bytes 776 | tf_op jit(solution)/shard_map/ppermute | solution.py:15
  134.7 5.8 %collective-permute-start.41 = (f32[1,2,32]{2,1,0:T(2,128)S(1)}, f32[1,2,32]{2,1,0:T(2,128)S(1)}, u32[]{:S(2)}, u32[]{:S(2)}) collective-permute-start(f32[1,2,32]{2,1,0:T(2,128)S(1)} %slice.1319), channel_id=1, source_target_pairs={{2,0},{4,2},{6,4},{8,6},{10,8},{12,10},{14,12},{16,14},{18,16},{20... | collective-permute-start | bytes 776 | tf_op jit(solution)/shard_map/ppermute | solution.py:17
  148.7 5.8 %collective-permute-start.44 = (f32[1,4,64]{2,1,0:T(4,128)S(1)}, f32[1,4,64]{2,1,0:T(4,128)S(1)}, u32[]{:S(2)}, u32[]{:S(2)}) collective-permute-start(f32[1,4,64]{2,1,0:T(4,128)S(1)} %slice.1333), channel_id=1, source_target_pairs={{0,2},{2,4},{4,6},{6,8},{8,10},{10,12},{12,14},{14,16},{16,18},{18... | collective-permute-start | bytes 3080 | tf_op jit(solution)/shard_map/ppermute | solution.py:15
  149.1 5.8 %collective-permute-start.45 = (f32[1,4,64]{2,1,0:T(4,128)S(1)}, f32[1,4,64]{2,1,0:T(4,128)S(1)}, u32[]{:S(2)}, u32[]{:S(2)}) collective-permute-start(f32[1,4,64]{2,1,0:T(4,128)S(1)} %slice.1335), channel_id=1, source_target_pairs={{2,0},{4,2},{6,4},{8,6},{10,8},{12,10},{14,12},{16,14},{18,16},{20... | collective-permute-start | bytes 3080 | tf_op jit(solution)/shard_map/ppermute | solution.py:17
  154.9 3.7 collective-permute-start.46
  164.4 5.8 %collective-permute-start.48 = (f32[1,8,128]{2,1,0:T(8,128)S(1)}, f32[1,8,128]{2,1,0:T(8,128)S(1)}, u32[]{:S(2)}, u32[]{:S(2)}) collective-permute-start(f32[1,8,128]{2,1,0:T(8,128)S(1)} %slice.1349), channel_id=1, source_target_pairs={{0,2},{2,4},{4,6},{6,8},{8,10},{10,12},{12,14},{14,16},{16,18},{18... | collective-permute-start | bytes 12296 | tf_op jit(solution)/shard_map/ppermute | solution.py:15
  164.9 6.2 %collective-permute-start.49 = (f32[1,8,128]{2,1,0:T(8,128)S(1)}, f32[1,8,128]{2,1,0:T(8,128)S(1)}, u32[]{:S(2)}, u32[]{:S(2)}) collective-permute-start(f32[1,8,128]{2,1,0:T(8,128)S(1)} %slice.1351), channel_id=1, source_target_pairs={{2,0},{4,2},{6,4},{8,6},{10,8},{12,10},{14,12},{16,14},{18,16},{20... | collective-permute-start | bytes 12296 | tf_op jit(solution)/shard_map/ppermute | solution.py:17
  171.1 3.7 collective-permute-start.50
  184.7 5.8 %collective-permute-start.52 = (f32[1,8,128]{2,1,0:T(8,128)S(1)}, f32[1,8,128]{2,1,0:T(8,128)S(1)}, u32[]{:S(2)}, u32[]{:S(2)}) collective-permute-start(f32[1,8,128]{2,1,0:T(8,128)S(1)} %slice.1365), channel_id=1, source_target_pairs={{0,2},{2,4},{4,6},{6,8},{8,10},{10,12},{12,14},{14,16},{16,18},{18... | collective-permute-start | bytes 12296 | tf_op jit(solution)/shard_map/ppermute | solution.py:15
  185.2 5.8 %collective-permute-start.53 = (f32[1,8,128]{2,1,0:T(8,128)S(1)}, f32[1,8,128]{2,1,0:T(8,128)S(1)}, u32[]{:S(2)}, u32[]{:S(2)}) collective-permute-start(f32[1,8,128]{2,1,0:T(8,128)S(1)} %slice.1367), channel_id=1, source_target_pairs={{2,0},{4,2},{6,4},{8,6},{10,8},{12,10},{14,12},{16,14},{18,16},{20... | collective-permute-start | bytes 12296 | tf_op jit(solution)/shard_map/ppermute | solution.py:17
  191.1 3.7 collective-permute-start.54
  203.7 5.8 %collective-permute-start.56 = (f32[1,8,128]{2,1,0:T(8,128)S(1)}, f32[1,8,128]{2,1,0:T(8,128)S(1)}, u32[]{:S(2)}, u32[]{:S(2)}) collective-permute-start(f32[1,8,128]{2,1,0:T(8,128)S(1)} %slice.1381), channel_id=1, source_target_pairs={{0,2},{2,4},{4,6},{6,8},{8,10},{10,12},{12,14},{14,16},{16,18},{18... | collective-permute-start | bytes 12296 | tf_op jit(solution)/shard_map/ppermute | solution.py:15
  204.2 6.0 %collective-permute-start.57 = (f32[1,8,128]{2,1,0:T(8,128)S(1)}, f32[1,8,128]{2,1,0:T(8,128)S(1)}, u32[]{:S(2)}, u32[]{:S(2)}) collective-permute-start(f32[1,8,128]{2,1,0:T(8,128)S(1)} %slice.1383), channel_id=1, source_target_pairs={{2,0},{4,2},{6,4},{8,6},{10,8},{12,10},{14,12},{16,14},{18,16},{20... | collective-permute-start | bytes 12296 | tf_op jit(solution)/shard_map/ppermute | solution.py:17
  210.2 3.7 collective-permute-start.58
  223.8 5.8 %collective-permute-start.60 = (f32[1,8,128]{2,1,0:T(8,128)S(1)}, f32[1,8,128]{2,1,0:T(8,128)S(1)}, u32[]{:S(2)}, u32[]{:S(2)}) collective-permute-start(f32[1,8,128]{2,1,0:T(8,128)S(1)} %slice.1397), channel_id=1, source_target_pairs={{0,2},{2,4},{4,6},{6,8},{8,10},{10,12},{12,14},{14,16},{16,18},{18... | collective-permute-start | bytes 12296 | tf_op jit(solution)/shard_map/ppermute | solution.py:15
  224.3 5.8 %collective-permute-start.61 = (f32[1,8,128]{2,1,0:T(8,128)S(1)}, f32[1,8,128]{2,1,0:T(8,128)S(1)}, u32[]{:S(2)}, u32[]{:S(2)}) collective-permute-start(f32[1,8,128]{2,1,0:T(8,128)S(1)} %slice.1399), channel_id=1, source_target_pairs={{2,0},{4,2},{6,4},{8,6},{10,8},{12,10},{14,12},{16,14},{18,16},{20... | collective-permute-start | bytes 12296 | tf_op jit(solution)/shard_map/ppermute | solution.py:17
  230.1 3.7 collective-permute-start.62
  236.4 5.8 %collective-permute-start.64 = (f32[1,4,64]{2,1,0:T(4,128)S(1)}, f32[1,4,64]{2,1,0:T(4,128)S(1)}, u32[]{:S(2)}, u32[]{:S(2)}) collective-permute-start(f32[1,4,64]{2,1,0:T(4,128)S(1)} %slice.1413), channel_id=1, source_target_pairs={{0,2},{2,4},{4,6},{6,8},{8,10},{10,12},{12,14},{14,16},{16,18},{18... | collective-permute-start | bytes 3080 | tf_op jit(solution)/shard_map/ppermute | solution.py:15
  236.8 5.8 %collective-permute-start.65 = (f32[1,4,64]{2,1,0:T(4,128)S(1)}, f32[1,4,64]{2,1,0:T(4,128)S(1)}, u32[]{:S(2)}, u32[]{:S(2)}) collective-permute-start(f32[1,4,64]{2,1,0:T(4,128)S(1)} %slice.1415), channel_id=1, source_target_pairs={{2,0},{4,2},{6,4},{8,6},{10,8},{12,10},{14,12},{16,14},{18,16},{20... | collective-permute-start | bytes 3080 | tf_op jit(solution)/shard_map/ppermute | solution.py:17
  251.5 5.8 %collective-permute-start.68 = (f32[1,4,64]{2,1,0:T(4,128)S(1)}, f32[1,4,64]{2,1,0:T(4,128)S(1)}, u32[]{:S(2)}, u32[]{:S(2)}) collective-permute-start(f32[1,4,64]{2,1,0:T(4,128)S(1)} %slice.1429), channel_id=1, source_target_pairs={{0,2},{2,4},{4,6},{6,8},{8,10},{10,12},{12,14},{14,16},{16,18},{18... | collective-permute-start | bytes 3080 | tf_op jit(solution)/shard_map/ppermute | solution.py:15
  251.9 5.8 %collective-permute-start.69 = (f32[1,4,64]{2,1,0:T(4,128)S(1)}, f32[1,4,64]{2,1,0:T(4,128)S(1)}, u32[]{:S(2)}, u32[]{:S(2)}) collective-permute-start(f32[1,4,64]{2,1,0:T(4,128)S(1)} %slice.1431), channel_id=1, source_target_pairs={{2,0},{4,2},{6,4},{8,6},{10,8},{12,10},{14,12},{16,14},{18,16},{20... | collective-permute-start | bytes 3080 | tf_op jit(solution)/shard_map/ppermute | solution.py:17
  265.7 5.8 %collective-permute-start.72 = (f32[1,4,64]{2,1,0:T(4,128)S(1)}, f32[1,4,64]{2,1,0:T(4,128)S(1)}, u32[]{:S(2)}, u32[]{:S(2)}) collective-permute-start(f32[1,4,64]{2,1,0:T(4,128)S(1)} %slice.1445), channel_id=1, source_target_pairs={{0,2},{2,4},{4,6},{6,8},{8,10},{10,12},{12,14},{14,16},{16,18},{18... | collective-permute-start | bytes 3080 | tf_op jit(solution)/shard_map/ppermute | solution.py:15
  266.1 6.0 %collective-permute-start.73 = (f32[1,4,64]{2,1,0:T(4,128)S(1)}, f32[1,4,64]{2,1,0:T(4,128)S(1)}, u32[]{:S(2)}, u32[]{:S(2)}) collective-permute-start(f32[1,4,64]{2,1,0:T(4,128)S(1)} %slice.1447), channel_id=1, source_target_pairs={{2,0},{4,2},{6,4},{8,6},{10,8},{12,10},{14,12},{16,14},{18,16},{20... | collective-permute-start | bytes 3080 | tf_op jit(solution)/shard_map/ppermute | solution.py:17
  278.8 5.7 %collective-permute-start.76 = (f32[1,2,32]{2,1,0:T(2,128)S(1)}, f32[1,2,32]{2,1,0:T(2,128)S(1)}, u32[]{:S(2)}, u32[]{:S(2)}) collective-permute-start(f32[1,2,32]{2,1,0:T(2,128)S(1)} %slice.1461), channel_id=1, source_target_pairs={{0,2},{2,4},{4,6},{6,8},{8,10},{10,12},{12,14},{14,16},{16,18},{18... | collective-permute-start | bytes 776 | tf_op jit(solution)/shard_map/ppermute | solution.py:15
  279.1 5.8 %collective-permute-start.77 = (f32[1,2,32]{2,1,0:T(2,128)S(1)}, f32[1,2,32]{2,1,0:T(2,128)S(1)}, u32[]{:S(2)}, u32[]{:S(2)}) collective-permute-start(f32[1,2,32]{2,1,0:T(2,128)S(1)} %slice.1463), channel_id=1, source_target_pairs={{2,0},{4,2},{6,4},{8,6},{10,8},{12,10},{14,12},{16,14},{18,16},{20... | collective-permute-start | bytes 776 | tf_op jit(solution)/shard_map/ppermute | solution.py:17
  291.5 5.7 %collective-permute-start.80 = (f32[1,2,32]{2,1,0:T(2,128)S(1)}, f32[1,2,32]{2,1,0:T(2,128)S(1)}, u32[]{:S(2)}, u32[]{:S(2)}) collective-permute-start(f32[1,2,32]{2,1,0:T(2,128)S(1)} %slice.1477), channel_id=1, source_target_pairs={{0,2},{2,4},{4,6},{6,8},{8,10},{10,12},{12,14},{14,16},{16,18},{18... | collective-permute-start | bytes 776 | tf_op jit(solution)/shard_map/ppermute | solution.py:15
  291.7 5.8 %collective-permute-start.81 = (f32[1,2,32]{2,1,0:T(2,128)S(1)}, f32[1,2,32]{2,1,0:T(2,128)S(1)}, u32[]{:S(2)}, u32[]{:S(2)}) collective-permute-start(f32[1,2,32]{2,1,0:T(2,128)S(1)} %slice.1479), channel_id=1, source_target_pairs={{2,0},{4,2},{6,4},{8,6},{10,8},{12,10},{14,12},{16,14},{18,16},{20... | collective-permute-start | bytes 776 | tf_op jit(solution)/shard_map/ppermute | solution.py:17
  305.7 5.8 %collective-permute-start.84 = (f32[1,4,64]{2,1,0:T(4,128)S(1)}, f32[1,4,64]{2,1,0:T(4,128)S(1)}, u32[]{:S(2)}, u32[]{:S(2)}) collective-permute-start(f32[1,4,64]{2,1,0:T(4,128)S(1)} %slice.1493), channel_id=1, source_target_pairs={{0,2},{2,4},{4,6},{6,8},{8,10},{10,12},{12,14},{14,16},{16,18},{18... | collective-permute-start | bytes 3080 | tf_op jit(solution)/shard_map/ppermute | solution.py:15
  306.1 5.8 %collective-permute-start.85 = (f32[1,4,64]{2,1,0:T(4,128)S(1)}, f32[1,4,64]{2,1,0:T(4,128)S(1)}, u32[]{:S(2)}, u32[]{:S(2)}) collective-permute-start(f32[1,4,64]{2,1,0:T(4,128)S(1)} %slice.1495), channel_id=1, source_target_pairs={{2,0},{4,2},{6,4},{8,6},{10,8},{12,10},{14,12},{16,14},{18,16},{20... | collective-permute-start | bytes 3080 | tf_op jit(solution)/shard_map/ppermute | solution.py:17
  321.5 5.8 %collective-permute-start.88 = (f32[1,8,128]{2,1,0:T(8,128)S(1)}, f32[1,8,128]{2,1,0:T(8,128)S(1)}, u32[]{:S(2)}, u32[]{:S(2)}) collective-permute-start(f32[1,8,128]{2,1,0:T(8,128)S(1)} %slice.1509), channel_id=1, source_target_pairs={{0,2},{2,4},{4,6},{6,8},{8,10},{10,12},{12,14},{14,16},{16,18},{18... | collective-permute-start | bytes 12296 | tf_op jit(solution)/shard_map/ppermute | solution.py:15
  322.0 6.1 %collective-permute-start.89 = (f32[1,8,128]{2,1,0:T(8,128)S(1)}, f32[1,8,128]{2,1,0:T(8,128)S(1)}, u32[]{:S(2)}, u32[]{:S(2)}) collective-permute-start(f32[1,8,128]{2,1,0:T(8,128)S(1)} %slice.1511), channel_id=1, source_target_pairs={{2,0},{4,2},{6,4},{8,6},{10,8},{12,10},{14,12},{16,14},{18,16},{20... | collective-permute-start | bytes 12296 | tf_op jit(solution)/shard_map/ppermute | solution.py:17
  328.1 3.7 collective-permute-start.90
  341.6 5.8 %collective-permute-start.92 = (f32[1,8,128]{2,1,0:T(8,128)S(1)}, f32[1,8,128]{2,1,0:T(8,128)S(1)}, u32[]{:S(2)}, u32[]{:S(2)}) collective-permute-start(f32[1,8,128]{2,1,0:T(8,128)S(1)} %slice.1525), channel_id=1, source_target_pairs={{0,2},{2,4},{4,6},{6,8},{8,10},{10,12},{12,14},{14,16},{16,18},{18... | collective-permute-start | bytes 12296 | tf_op jit(solution)/shard_map/ppermute | solution.py:15
  342.1 5.8 %collective-permute-start.93 = (f32[1,8,128]{2,1,0:T(8,128)S(1)}, f32[1,8,128]{2,1,0:T(8,128)S(1)}, u32[]{:S(2)}, u32[]{:S(2)}) collective-permute-start(f32[1,8,128]{2,1,0:T(8,128)S(1)} %slice.1527), channel_id=1, source_target_pairs={{2,0},{4,2},{6,4},{8,6},{10,8},{12,10},{14,12},{16,14},{18,16},{20... | collective-permute-start | bytes 12296 | tf_op jit(solution)/shard_map/ppermute | solution.py:17
  348.0 3.7 collective-permute-start.94
  (44 other events, 135.7 us)
where the time goes:
time: 405 us; the launch traced here: 398 us
  starting transfers between devices  156 us (39%)
  waiting for transfers between devices  79.1 us (20%)
  matrix products  62.1 us (15%)
  local copies, waits for them, and re-layouts  40.8 us (10%)
  blocking collectives  37.5 us (9%)
  other arithmetic  13.2 us (3%)
  between operations  9.16 us (2%)
    ppermute x48, starting transfers between devices, with_halo(): lax.ppermute(head, axis, [((i + 1) % count, i) for i in range(count)])  127 us
    ppermute x48, waiting for transfers between devices, with_halo(): lax.ppermute(tail, axis, [(i, (i + 1) % count) for i in range(count)])  48.2 us
    psum x1, blocking collectives, local(): lax.psum((jnp.sum(weight * load * load), jnp.sum(weight * load * image),...  37.5 us
    ppermute x48, waiting for transfers between devices, with_halo(): lax.ppermute(head, axis, [((i + 1) % count, i) for i in range(count)])  30.9 us
    ppermute x48, starting transfers between devices, with_halo(): lax.ppermute(tail, axis, [(i, (i + 1) % count) for i in range(count)])  28.7 us
    dot_general x16, matrix products, element_apply(): third = jnp.einsum('ak,eifjgk->eifjga', deriv, block, precision=high)  28.2 us
    another operation x52, local copies, waits for them, and re-layouts  9.14 us
  transfers between devices with their start and end apart: 96, of which 83 were waited for; matrix products, arithmetic and copies ran while one was open for 11% of the time, Pallas kernels for 0%

commit v1 on v0

--- a/solution.py
+++ b/solution.py
@@ -2,6 +2,8 @@
 import jax.numpy as jnp
 import numpy as np
 from jax import lax
+from jax.experimental import pallas as pl
+from jax.experimental.pallas import tpu as pltpu
 from jax.sharding import PartitionSpec as P
 
 
@@ -165,7 +167,7 @@
     return three.reshape(blocks[0] * fine_count, blocks[1] * fine_count, blocks[2] * fine_count)
 
 
-def local(forcing, kappa, sigma):
+def distributed(forcing, kappa, sigma):
     blocks = kappa.shape
     counts = [8, 4, 2]
     tables = [lobatto(count) for count in counts]
@@ -250,7 +252,517 @@
     return (solution, residual, rel_residual)
 
 
+THETA = 1.65
+DELTA = 1.35
+RATIO = THETA / DELTA
+RHO0 = 1.0 / RATIO
+RHO1 = 1.0 / (2.0 * RATIO - RHO0)
+KEEP = RHO1 * RHO0
+PUSH = 2.0 * RHO1 / DELTA
+LANES = 128
+SUBS = 8
+
+
+def triple(first, second, third):
+    return np.kron(first, np.kron(second, third))
+
+
+def split_const(matrix):
+    high = matrix.astype(jnp.bfloat16)
+    low = (matrix - high.astype(np.float64)).astype(jnp.bfloat16)
+    return high, low
+
+
+def stacked(matrix):
+    high, low = split_const(matrix)
+    return np.concatenate([high, high, low], axis=1)
+
+
+class Tables:
+    def __init__(self):
+        self.tables = [lobatto(count) for count in (8, 4, 2)]
+        self.weights = [table[1] for table in self.tables]
+        self.stiff = [table[2].T @ np.diag(table[1]) @ table[2] for table in self.tables]
+        interps = [
+            lagrange(self.tables[level][0], self.tables[level + 1][0]) for level in range(2)
+        ]
+        order = [0, 7, 1, 2, 3, 4, 5, 6]
+        w, k = np.diag(self.weights[0]), self.stiff[0]
+        plane = np.kron(k, w) + np.kron(w, k)
+        both = np.kron(w, w)
+        flip = k[:4, ::-1][:, :4]
+        even = 0.5 * (k[:4, :4] + flip)
+        odd = 0.5 * (k[:4, :4] - flip)
+        half = 0.5 * w[:4, :4]
+        columns = np.concatenate(
+            [np.arange(8) + 64 * kk + 8 * i for kk in range(4) for i in order]
+        )
+        self.even = stacked((np.kron(even, both) + np.kron(half, plane))[:, columns])
+        self.odd = stacked((np.kron(odd, both) + np.kron(half, plane))[:, columns])
+        factor = [np.where((np.arange(n) == 0) | (np.arange(n) == n - 1), 0.5, 1.0) for n in (8, 4)]
+        down = [interps[level].T * factor[level][None, :] for level in range(2)]
+        full = np.concatenate([np.arange(8) + 64 * kk + 8 * i for kk in range(8) for i in order])
+        high, low = split_const(triple(down[0], down[0], down[0])[:, full])
+        self.down0 = np.concatenate([high, low], axis=0)
+        self.up0 = stacked(triple(interps[0], interps[0], interps[0]))
+        w, k = np.diag(self.weights[1]), self.stiff[1]
+        self.op1 = stacked(triple(k, w, w) + triple(w, k, w) + triple(w, w, k))
+        self.down1 = triple(down[1], down[1], down[1]).astype(np.float32)
+        self.up1 = triple(interps[1], interps[1], interps[1]).astype(np.float32)
+        w, k = np.diag(self.weights[2]), self.stiff[2]
+        self.op2 = (triple(k, w, w) + triple(w, k, w) + triple(w, w, k)).astype(np.float32)
+        self.squares = [
+            np.sum(table[2] * table[2] * table[1][:, None], axis=0) for table in self.tables
+        ]
+        wide = lambda column: np.repeat(np.asarray(column, np.float32)[:, None], LANES, axis=1)
+        mass, point = [], []
+        for level in (1, 2):
+            a, b = self.weights[level], self.squares[level]
+            mass.append(wide(triple(a, a, a)))
+            point.append(wide(triple(b, a, a) + triple(a, b, a) + triple(a, a, b)))
+        self.rows = np.concatenate(
+            [wide(self.weights[0]), wide(self.squares[0]), mass[0], point[0], mass[1], point[1],
+             wide(factor[0])], axis=0)
+
+
+PAIRS = ((0, 7), (1, 2), (3, 4), (5, 6))
+
+
+def kernel(nx, ny, tables, meta, near, far, even, odd, down0, up0, op1, down1, up1, op2, rows,
+           sol_ref, res_ref, rel_ref, b_ref, r_ref, d_ref, z_ref, v_ref, re_ref, ro_ref,
+           be_ref, bo_ref, c_ref, lane_ref):
+    groups = nx // SUBS
+    tiles = ny * groups
+    wide = tiles * LANES
+    own_x, own_y = meta[0], meta[1]
+    sub = lax.broadcasted_iota(jnp.int32, (SUBS, LANES), 0)
+    lane = lax.broadcasted_iota(jnp.int32, (SUBS, LANES), 1) % SUBS
+    w = [float(x) for x in tables.weights[0]]
+    q = [float(x) for x in tables.squares[0]]
+    f = [0.5 if k in (0, 7) else 1.0 for k in range(8)]
+
+    def cols(x):
+        return [x[:, t * LANES:(t + 1) * LANES] for t in range(tiles)]
+
+    def join(parts):
+        return jnp.concatenate(parts, axis=1)
+
+    def across(x):
+        return join([x] * tiles)
+
+    sub_w = across(sub)
+
+    def shift_y(parts, step):
+        return [parts[((t // groups - step) % ny) * groups + t % groups] for t in range(tiles)]
+
+    def x_up(x):
+        parts, out = cols(x), []
+        for t in range(tiles):
+            prev = parts[(t // groups) * groups + (t % groups - 1) % groups]
+            out.append(jnp.where(lane == 0, pltpu.roll(prev, LANES - SUBS + 1, 1),
+                                 pltpu.roll(parts[t], 1, 1)))
+        return join(out)
+
+    def x_down(x):
+        parts, out = cols(x), []
+        for t in range(tiles):
+            succ = parts[(t // groups) * groups + (t % groups + 1) % groups]
+            out.append(jnp.where(lane == SUBS - 1, pltpu.roll(succ, SUBS - 1, 1),
+                                 pltpu.roll(parts[t], LANES - 1, 1)))
+        return join(out)
+
+    def z_up(x):
+        return join([pltpu.roll(p, SUBS, 1) for p in cols(x)])
+
+    def z_down(x):
+        return join([pltpu.roll(p, LANES - SUBS, 1) for p in cols(x)])
+
+    def y_fold(x, first, last, low, high):
+        before = join(shift_y(cols(x), 1))
+        after = join(shift_y(cols(x), -1))
+        return x + jnp.where(first, pltpu.roll(before, low, 0),
+                             jnp.where(last, pltpu.roll(after, high, 0), 0.0))
+
+    def fold_y8(x):
+        return y_fold(x, sub_w == 0, sub_w == 7, 1, 7)
+
+    def row(k, i):
+        return pl.ds(k * 64 + i * 8, 8)
+
+    even_own = (own_x & 1) == 0
+    for t in range(tiles):
+        y_index, high = t // groups, t % groups
+        slots = []
+        for c in range(0, SUBS, 2):
+            delta = (high * SUBS + c) ^ own_x
+            slot, bit = jnp.int32(0), 0
+            if ny > 1:
+                slot, bit = y_index ^ own_y, 1
+            step = nx // 2
+            while step > 1:
+                flag = jnp.where((delta & step) != 0, 1, 0)
+                slot = slot + flag * (1 << bit)
+                bit += 1
+                step //= 2
+            slots.append(slot)
+        for i in range(8):
+            block = []
+            for slot in slots:
+                a, b = near[slot, i], far[slot, i]
+                block.append(jnp.where(even_own, a, b))
+                block.append(jnp.where(even_own, b, a))
+            for step in (1, 2, 4):
+                out = list(block)
+                for c in range(SUBS):
+                    if not c & step:
+                        a, b = block[c], block[c + step]
+                        keep = (lane & step) == 0
+                        out[c] = jnp.where(keep, a, pltpu.roll(b, step, 1))
+                        out[c + step] = jnp.where(keep, pltpu.roll(a, LANES - step, 1), b)
+                block = out
+            for k in range(7):
+                v_ref[row(k, i), t * LANES:(t + 1) * LANES] = block[k]
+            v_ref[row(7, i), t * LANES:(t + 1) * LANES] = pltpu.roll(block[0], LANES - SUBS, 1)
+            if i == 0:
+                lane_ref[0:8, t * LANES:(t + 1) * LANES] = block[7]
+    kap1 = lane_ref[0:1, :]
+    sig1 = lane_ref[1:2, :]
+    kap = jnp.broadcast_to(kap1, (SUBS, wide))
+    sig = jnp.broadcast_to(sig1, (SUBS, wide))
+    w_j = across(rows[0:8, :])
+    q_j = across(rows[8:16, :])
+    f_j = across(rows[160:168, :])
+    sig_w = sig * w_j
+
+    def store_split(kk, index, low_pair, high_pair):
+        a = jnp.concatenate(low_pair, axis=0)
+        b = jnp.concatenate(high_pair, axis=0)
+        for ref, value in ((be_ref, a + b), (bo_ref, a - b)):
+            high = value.astype(jnp.bfloat16)
+            low = (value - high.astype(jnp.float32)).astype(jnp.bfloat16)
+            at = kk * 64 + index * 16
+            ref[at:at + 16, :] = high
+            ref[256 + at:272 + at, :] = low
+            ref[512 + at:528 + at, :] = high
+
+    def fold_pairs(kk, get, index):
+        out = []
+        for i in PAIRS[index]:
+            a, b = get(kk, i), get(7 - kk, i)
+            out.append((a, b))
+        return out
+
+    def assemble_pairs(kk, index, values, with_z=True):
+        vals = [list(v) for v in values]
+        if kk == 0 and with_z:
+            for v in vals:
+                a, b = v
+                v[0] = a + z_up(b)
+                v[1] = b + z_down(a)
+        if index == 0:
+            for s in range(2):
+                a, b = vals[0][s], vals[1][s]
+                vals[0][s] = a + x_up(b)
+                vals[1][s] = b + x_down(a)
+        return [[fold_y8(x) for x in v] for v in vals]
+
+    def point(k, i):
+        s1 = q[k] * w[i] + w[k] * q[i]
+        s2 = w[k] * w[i]
+        return kap * (s1 * w_j + s2 * q_j) + s2 * sig_w
+
+    for kk in range(4):
+        for index, pair in enumerate(PAIRS):
+            diag = assemble_pairs(kk, index, fold_pairs(kk, point, index))
+            load = assemble_pairs(
+                kk, index, fold_pairs(kk, lambda k, i: v_ref[row(k, i), :], index), with_z=False)
+            dirs = []
+            for s, k in enumerate((kk, 7 - kk)):
+                group = []
+                for n, i in enumerate(pair):
+                    inverse = 1.0 / diag[n][s]
+                    b_ref[row(k, i), :] = load[n][s]
+                    r_ref[row(k, i), :] = load[n][s]
+                    first = load[n][s] * inverse * (1.0 / THETA)
+                    d_ref[row(k, i), :] = first
+                    z_ref[row(k, i), :] = jnp.zeros_like(first)
+                    group.append((first, inverse))
+                dirs.append([g[0] for g in group])
+                for n, i in enumerate(pair):
+                    v_ref[row(k, i), :] = group[n][1]
+            store_split(kk, index, dirs[0], dirs[1])
+
+    def tile_rows(x):
+        return jnp.concatenate([x] * tiles, axis=1)
+
+    def fold1(x):
+        first = x[0:16] + z_up16(x[48:64])
+        last = x[48:64] + z_down16(x[0:16])
+        pieces = [first[0:8], first[8:16], x[16:24], x[24:32], x[32:40], x[40:48],
+                  last[0:8], last[8:16]]
+        out = []
+        for k in range(4):
+            a, b = pieces[2 * k], pieces[2 * k + 1]
+            lower = sub_w < 4
+            na = a + jnp.where(lower, x_up(pltpu.roll(b, 4, 0)), 0.0)
+            nb = b + jnp.where(lower, 0.0, x_down(pltpu.roll(a, 4, 0)))
+            out += [na, nb]
+        j = sub_w % 4
+        out = [y_fold(x, j == 0, j == 3, 5, 3) for x in out]
+        return jnp.concatenate(out, axis=0)
+
+    def z_up16(x):
+        return jnp.concatenate([z_up(x[0:8]), z_up(x[8:16])], axis=0)
+
+    def z_down16(x):
+        return jnp.concatenate([z_down(x[0:8]), z_down(x[8:16])], axis=0)
+
+    def fold2(x):
+        other = pltpu.roll(x, 4, 0)
+        x = x + jnp.where(sub_w < 4, z_up(other), z_down(other))
+        i = (sub_w // 2) % 2
+        x = x + jnp.where(i == 0, x_up(pltpu.roll(x, 6, 0)), x_down(pltpu.roll(x, 2, 0)))
+        j = sub_w % 2
+        return y_fold(x, j == 0, j == 1, 7, 1)
+
+    def cat3(x):
+        high = x.astype(jnp.bfloat16)
+        low = (x - high.astype(jnp.float32)).astype(jnp.bfloat16)
+        return jnp.concatenate([high, low, high], axis=0)
+
+    def dot(a, b):
+        return jnp.dot(a, b, preferred_element_type=jnp.float32)
+
+    def dot_high(a, b):
+        return jnp.dot(a, b, preferred_element_type=jnp.float32, precision=lax.Precision.HIGHEST)
+
+    mass1 = tile_rows(rows[16:80, :])
+    point1 = tile_rows(rows[80:144, :])
+    mass2 = tile_rows(rows[144:152, :])
+    point2 = tile_rows(rows[152:160, :])
+    inv1_ref, mass1_ref = lane_ref.at[8:72, :], lane_ref.at[72:136, :]
+    inv1_ref[...] = 1.0 / fold1(kap1 * point1 + sig1 * mass1)
+    mass1_ref[...] = sig1 * mass1
+    inv2 = 1.0 / fold2(kap1 * point2 + sig1 * mass2)
+    lane_ref[136:144, :] = inv2
+    lane_ref[144:152, :] = sig1 * mass2
+
+    def apply1(v):
+        return fold1(kap1 * dot(op1[...], cat3(v)) + mass1_ref[...] * v)
+
+    def apply2(v):
+        return fold2(kap1 * dot_high(op2[...], v) + lane_ref[144:152, :] * v)
+
+    def coarse(resid):
+        inverse = inv1_ref[...]
+        d = resid * inverse * (1.0 / THETA)
+        x = d
+        resid = resid - apply1(d)
+        d = KEEP * d + PUSH * (resid * inverse)
+        x = x + d
+        resid = resid - apply1(d)
+        low = fold2(dot_high(down1[...], resid))
+        inverse2 = lane_ref[136:144, :]
+        d = low * inverse2 * (1.0 / THETA)
+        y = d
+        low = low - apply2(d)
+        y = y + KEEP * d + PUSH * (low * inverse2)
+        e = dot_high(up1[...], y)
+        x = x + e
+        resid = resid - apply1(e)
+        return x + resid * inverse * (1.0 / THETA)
+
+    def multiply():
+        re_ref[...] = dot(even[...], be_ref[...])
+        ro_ref[...] = dot(odd[...], bo_ref[...])
+
+    def image(kk, index):
+        values = []
+        for i in PAIRS[index]:
+            e = re_ref[row(kk, i), :]
+            o = ro_ref[row(kk, i), :]
+            scale = sig_w * (w[kk] * w[i])
+            values.append((kap * (e + o) + scale * d_ref[row(kk, i), :],
+                           kap * (e - o) + scale * d_ref[row(7 - kk, i), :]))
+        return assemble_pairs(kk, index, values)
+
+    def sweep(update):
+        multiply()
+        for kk in range(4):
+            for index, pair in enumerate(PAIRS):
+                out = image(kk, index)
+                dirs = []
+                for s, k in enumerate((kk, 7 - kk)):
+                    dirs.append([update(k, i, out[n][s]) for n, i in enumerate(pair)])
+                yield kk, index, dirs
+
+    def second_direction(k, i, value):
+        r = r_ref[row(k, i), :] - value
+        r_ref[row(k, i), :] = r
+        first = d_ref[row(k, i), :]
+        d = KEEP * first + PUSH * (r * v_ref[row(k, i), :])
+        z_ref[row(k, i), :] = z_ref[row(k, i), :] + (first + d)
+        return d
+
+    def residual_only(k, i, value):
+        r = r_ref[row(k, i), :] - value
+        r_ref[row(k, i), :] = r
+        return r
+
+    def last_direction(k, i, value):
+        r = r_ref[row(k, i), :] - value
+        r_ref[row(k, i), :] = r
+        d = r * v_ref[row(k, i), :] * (1.0 / THETA)
+        z_ref[row(k, i), :] = z_ref[row(k, i), :] + d
+        return d
+
+    def first_direction(k, i, value):
+        r = r_ref[row(k, i), :] - value
+        r_ref[row(k, i), :] = r
+        return r * v_ref[row(k, i), :] * (1.0 / THETA)
+
+    def run(update, keep):
+        for kk, index, dirs in sweep(update):
+            if keep:
+                for s, k in enumerate((kk, 7 - kk)):
+                    for n, i in enumerate(PAIRS[index]):
+                        d_ref[row(k, i), :] = dirs[s][n]
+                store_split(kk, index, dirs[0], dirs[1])
+            else:
+                for s, k in enumerate((kk, 7 - kk)):
+                    value = jnp.concatenate(dirs[s], axis=0)
+                    high = value.astype(jnp.bfloat16)
+                    low = (value - high.astype(jnp.float32)).astype(jnp.bfloat16)
+                    at = k * 64 + index * 16
+                    c_ref[at:at + 16, :] = high
+                    c_ref[512 + at:528 + at, :] = low
+
+    def cycle(step, carry):
+        run(second_direction, True)
+        run(residual_only, False)
+        both = dot(down0[...], c_ref[0:512, :])
+        low = both[0:64] + both[64:128] + dot(down0[0:64, :], c_ref[512:1024, :])
+        correction = coarse(fold1(low))
+        d_ref[...] = dot(up0[...], cat3(correction))
+        for kk in range(4):
+            for index, pair in enumerate(PAIRS):
+                dirs = [[d_ref[row(k, i), :] for i in pair] for k in (kk, 7 - kk)]
+                for s, k in enumerate((kk, 7 - kk)):
+                    for n, i in enumerate(pair):
+                        z_ref[row(k, i), :] = z_ref[row(k, i), :] + dirs[s][n]
+                store_split(kk, index, dirs[0], dirs[1])
+        run(last_direction, True)
+        run(first_direction, True)
+        return carry
+
+    lax.fori_loop(0, 2, cycle, 0)
+
+    zero = jnp.zeros((SUBS, wide), jnp.float32)
+    bw, ww, bb = zero, zero, zero
+    for k in range(8):
+        for i in range(8):
+            b = b_ref[row(k, i), :]
+            image_all = b - r_ref[row(k, i), :]
+            fb = b * (f[k] * f[i])
+            bw = bw + fb * image_all
+            ww = ww + image_all * image_all * (f[k] * f[i])
+            bb = bb + fb * b
+    bw, ww, bb = jnp.sum(bw * f_j), jnp.sum(ww * f_j), jnp.sum(bb * f_j)
+    coef = bw / ww
+    rr = zero
+    for k in range(8):
+        for i in range(8):
+            b = b_ref[row(k, i), :]
+            res = b - coef * (b - r_ref[row(k, i), :])
+            rr = rr + res * res * (f[k] * f[i])
+    rr = jnp.sum(rr * f_j)
+    rel_ref[...] = jnp.sqrt(jnp.full((SUBS, LANES), rr / bb, jnp.float32))
+    start = pl.multiple_of((own_y * groups + own_x // SUBS) * LANES, LANES)
+    place = own_x % SUBS
+    window = pl.ds(start, LANES)
+    for i in range(8):
+        sol = jnp.zeros((SUBS, LANES), jnp.float32)
+        res = sol
+        for k in range(8):
+            b = b_ref[row(k, i), window]
+            z = z_ref[row(k, i), window]
+            r = b - coef * (b - r_ref[row(k, i), window])
+            turn = (k - place) % LANES
+            sol = jnp.where(lane == k, pltpu.roll(z, turn, 1), sol)
+            res = jnp.where(lane == k, pltpu.roll(r, turn, 1), res)
+        sol_ref[i] = coef * sol
+        res_ref[i] = res
+
+
+def solve_all(nx, ny, meta, near, far, interpret=False):
+    tables = Tables()
+    wide = ny * nx // SUBS * LANES
+    consts = [tables.even, tables.odd, tables.down0, tables.up0, tables.op1, tables.down1,
+              tables.up1, tables.op2, tables.rows]
+    vmem = pl.BlockSpec(memory_space=pltpu.VMEM)
+    field = pltpu.VMEM((512, wide), jnp.float32)
+    return pl.pallas_call(
+        lambda *refs: kernel(nx, ny, tables, *refs),
+        in_specs=[pl.BlockSpec(memory_space=pltpu.SMEM)] + [vmem] * 11,
+        out_specs=[vmem] * 3,
+        out_shape=[
+            jax.ShapeDtypeStruct(near.shape[1:], jnp.float32),
+            jax.ShapeDtypeStruct(near.shape[1:], jnp.float32),
+            jax.ShapeDtypeStruct((SUBS, LANES), jnp.float32),
+        ],
+        scratch_shapes=[
+            field, field, field, field, field,
+            pltpu.VMEM((256, wide), jnp.float32), pltpu.VMEM((256, wide), jnp.float32),
+            pltpu.VMEM((768, wide), jnp.bfloat16), pltpu.VMEM((768, wide), jnp.bfloat16),
+            pltpu.VMEM((1024, wide), jnp.bfloat16), pltpu.VMEM((152, wide), jnp.float32),
+        ],
+        name="solve_all",
+        interpret=interpret,
+    )(meta, near, far, *[jnp.asarray(c) for c in consts])
+
+
+def packed_block(forcing, kappa, sigma):
+    field = fold_axis(forcing, 2, SUBS)
+    shape = field.shape
+    index = [lax.broadcasted_iota(jnp.int32, shape, dim) for dim in range(3)]
+    last = (index[2] % SUBS == SUBS - 1) & (index[0] == 0)
+    wide = lambda value: jnp.repeat(value.reshape(-1), SUBS)[None, None, :]
+    field = jnp.where(last & (index[1] == 0), wide(kappa), field)
+    return jnp.where(last & (index[1] == 1), wide(sigma), field)
+
+
+def gathered(forcing, kappa, sigma):
+    nx, ny = lax.axis_size("gx"), lax.axis_size("gy")
+    block = packed_block(forcing, kappa, sigma)[None]
+    if ny > 1:
+        other = lax.ppermute(block, "gy", [(i, i ^ 1) for i in range(ny)])
+        block = jnp.concatenate([block, other], axis=0)
+    step = nx // 2
+    while step:
+        other = lax.ppermute(block, "gx", [(i, i ^ step) for i in range(nx)])
+        if step > 1:
+            block = jnp.concatenate([block, other], axis=0)
+        step //= 2
+    meta = jnp.stack([lax.axis_index("gx"), lax.axis_index("gy")]).astype(jnp.int32)
+    sol, res, rel = solve_all(nx, ny, meta, block, other)
+    return sol, res, rel[0, 0]
+
+
+def fits_one_device(mesh):
+    nx, ny = mesh.shape["gx"], mesh.shape["gy"]
+    power = nx & (nx - 1) == 0
+    return power and nx % SUBS == 0 and ny <= 2 and nx * ny <= 64
+
+
 def solution(mesh):
-    in_specs = (P("gx", "gy", None), P("gx", "gy", None), P("gx", "gy", None))
-    out_specs = (P("gx", "gy", None), P("gx", "gy", None), P())
-    return jax.shard_map(local, mesh=mesh, in_specs=in_specs, out_specs=out_specs, check_vma=False)
+    spec = P("gx", "gy", None)
+    small = fits_one_device(mesh)
+
+    def local(forcing, kappa, sigma):
+        plain = forcing.shape == (SUBS, SUBS, LANES) and kappa.shape == (1, 1, LANES // SUBS)
+        return (gathered if small and plain else distributed)(forcing, kappa, sigma)
+
+    return jax.shard_map(
+        local, mesh=mesh, in_specs=(spec, spec, spec), out_specs=(spec, spec, P()),
+        check_vma=False,
+    )

time: 405 us -> 53.4 us (0.13); the launches traced: 398 us -> 53.1 us
  starting transfers between devices: 156 us -> 10.1 us
  waiting for transfers between devices: 79.1 us -> 12.9 us
  matrix products: 62.1 us -> 0 us
  blocking collectives: 37.5 us -> 0 us
  local copies, waits for them, and re-layouts: 40.8 us -> 4.67 us
  Pallas kernels: 0 us -> 23.8 us
  other arithmetic: 13.2 us -> 0.83 us
  between operations: 9.16 us -> 0.74 us
    ppermute x96 -> x5, starting transfers between devices: 156 us -> 10.1 us  [the longest x4 7.08 us: gathered(): other = lax.ppermute(block, 'gx', [(i, i ^ step) for i in range(nx)])]
    ppermute x96 -> x5, waiting for transfers between devices: 79.1 us -> 12.9 us  [the longest x4 11 us: gathered(): other = lax.ppermute(block, 'gx', [(i, i ^ step) for i in range(nx)])]
    dot_general x120 -> x0, matrix products: 62.1 us -> none  [the longest x16 28.2 us: element_apply(): third = jnp.einsum('ak,eifjgk->eifjga', deriv, block, precision=high)]
    psum x1 -> x0, blocking collectives: 37.5 us -> none  [local(): lax.psum((jnp.sum(weight * load * load), jnp.sum(weight * load * image),...]
    pallas_call x0 -> x1, Pallas kernels: none -> 23.8 us  [solve_all(): pl.pallas_call(lambda *refs: kernel(nx, ny, tables, *refs), in_specs=[pl....]
    another operation x54 -> x0, local copies, waits for them, and re-layouts: 9.14 us -> none
    reshape x48 -> x0, local copies, waits for them, and re-layouts: 8.53 us -> none  [the longest x24 4.53 us: element_apply(): block = field.reshape(ex, count, ey, count, ez, count)]
    slice x139 -> x1, local copies, waits for them, and re-layouts: 9.14 us -> 1.18 us  [gathered(): return (sol, res, rel[0, 0])]
  transfers between devices with their start and end apart: 96 -> 5, of which waited for: 83 -> 5; matrix products, arithmetic and copies ran while one was open for 11% -> 1% of each run, Pallas kernels for 0% -> 0%
where the time goes in v1:
time: 53.4 us; the launch traced here: 53.1 us
  Pallas kernels  23.8 us (45%)
  waiting for transfers between devices  12.9 us (24%)
  starting transfers between devices  10.1 us (19%)
  local copies, waits for them, and re-layouts  4.67 us (9%)
  other arithmetic  0.83 us (2%)
  between operations  0.74 us (1%)
    pallas_call x1, Pallas kernels, solve_all(): pl.pallas_call(lambda *refs: kernel(nx, ny, tables, *refs), in_specs=[pl....  23.8 us
    ppermute x4, waiting for transfers between devices, gathered(): other = lax.ppermute(block, 'gx', [(i, i ^ step) for i in range(nx)])  11 us
    ppermute x4, starting transfers between devices, gathered(): other = lax.ppermute(block, 'gx', [(i, i ^ step) for i in range(nx)])  7.08 us
    ppermute x1, starting transfers between devices, gathered(): other = lax.ppermute(block, 'gy', [(i, i ^ 1) for i in range(ny)])  3.03 us
    unnamed x13, local copies, waits for them, and re-layouts  2.15 us
    ppermute x1, waiting for transfers between devices, gathered(): other = lax.ppermute(block, 'gy', [(i, i ^ 1) for i in range(ny)])  1.89 us
    slice x1, local copies, waits for them, and re-layouts, gathered(): return (sol, res, rel[0, 0])  1.18 us
  transfers between devices with their start and end apart: 5, of which 5 were waited for; matrix products, arithmetic and copies ran while one was open for 1% of the time, Pallas kernels for 0%

profile of v1, /device:TPU:0, one launch (start us, length us, event | category | flops | bytes accessed | tf_op | source)
XLA Modules:
  0.0 53.1 jit_solution(2207662993462229384)
XLA Ops:
  0.7 0.0 copy-start
  0.7 0.9 %fusion.8 = (f32[8,8,1]{2,1,0:T(8,128)S(1)}, f32[8,8,1]{2,1,0:T(8,128)S(1)}) fusion(f32[8,8,128]{2,1,0:T(8,128)} %param.12), kind=kLoop, calls=%fused_computation.26 | loop fusion | bytes 1024 | tf_op jit(solution)/shard_map/jit(_roll_static)/slice | solution.py:122
  1.6 0.0 copy-done
  1.6 0.1 fusion.9
  1.7 0.0 copy-start.3
  1.7 0.7 %copy-done.3 = f32[1,1,16]{2,1,0:T(1,128)S(1)} copy-done((f32[1,1,16]{2,1,0:T(1,128)S(1)}, f32[1,1,16]{2,1,0:T(1,128)}, u32[]{:S(2)}) %copy-start.3) | copy-done | bytes 88
  2.4 0.1 broadcast_in_dim.47
  2.4 0.1 broadcast_in_dim.48
  2.5 0.0 copy-start.4
  2.5 0.6 %copy-done.4 = f32[1,1,16]{2,1,0:T(1,128)S(1)} copy-done((f32[1,1,16]{2,1,0:T(1,128)S(1)}, f32[1,1,16]{2,1,0:T(1,128)}, u32[]{:S(2)}) %copy-start.4) | copy-done | bytes 88
  3.2 0.1 broadcast_in_dim.44
  3.3 0.1 broadcast_in_dim.45
  3.3 0.1 constant_dynamic-update-slice_fusion.4
  3.5 3.0 %collective-permute-start = (f32[1,8,8,128]{3,2,1,0:T(8,128)S(1)}, f32[1,8,8,128]{3,2,1,0:T(8,128)S(1)}, u32[]{:S(2)}, u32[]{:S(2)}) collective-permute-start(f32[1,8,8,128]{3,2,1,0:T(8,128)S(1)} %get-tuple-element.10), channel_id=1, source_target_pairs={{0,1},{1,0},{2,3},{3,2},{4,5},{5,4},{6,7},{7,6},{8,9},{9,8},{10,11... | collective-permute-start | bytes 98312 | tf_op jit(solution)/shard_map/ppermute | solution.py:738
  6.5 1.9 %collective-permute-done = f32[1,8,8,128]{3,2,1,0:T(8,128)S(1)} collective-permute-done((f32[1,8,8,128]{3,2,1,0:T(8,128)S(1)}, f32[1,8,8,128]{3,2,1,0:T(8,128)S(1)}, u32[]{:S(2)}, u32[]{:S(2)}) %collective-permute-start) | collective-permute-done | bytes 32800 | tf_op jit(solution)/shard_map/ppermute | solution.py:738
  8.4 3.1 %collective-permute-start.1 = (f32[2,8,8,128]{3,2,1,0:T(8,128)S(1)}, f32[2,8,8,128]{3,2,1,0:T(8,128)S(1)}, u32[]{:S(2)}, u32[]{:S(2)}) collective-permute-start(f32[2,8,8,128]{3,2,1,0:T(8,128)S(1)} %pad_maximum_fusion.2), channel_id=1, source_target_pairs={{0,16},{2,18},{4,20},{6,22},{8,24},{10,26},{12,28},{14,30},{16,0},... | collective-permute-start | bytes 196616 | tf_op jit(solution)/shard_map/ppermute | solution.py:742
  11.5 2.2 %collective-permute-done.1 = f32[2,8,8,128]{3,2,1,0:T(8,128)S(1)} collective-permute-done((f32[2,8,8,128]{3,2,1,0:T(8,128)S(1)}, f32[2,8,8,128]{3,2,1,0:T(8,128)S(1)}, u32[]{:S(2)}, u32[]{:S(2)}) %collective-permute-start.1) | collective-permute-done | bytes 65568 | tf_op jit(solution)/shard_map/ppermute | solution.py:742
  13.8 2.0 %collective-permute-start.2 = (f32[4,8,8,128]{3,2,1,0:T(8,128)S(1)}, f32[4,8,8,128]{3,2,1,0:T(8,128)S(1)}, u32[]{:S(2)}, u32[]{:S(2)}) collective-permute-start(f32[4,8,8,128]{3,2,1,0:T(8,128)S(1)} %pad_maximum_fusion.1), channel_id=1, source_target_pairs={{0,8},{2,10},{4,12},{6,14},{8,0},{10,2},{12,4},{14,6},{16,24},{18,... | collective-permute-start | bytes 393224 | tf_op jit(solution)/shard_map/ppermute | solution.py:742
  15.7 3.1 %collective-permute-done.2 = f32[4,8,8,128]{3,2,1,0:T(8,128)S(1)} collective-permute-done((f32[4,8,8,128]{3,2,1,0:T(8,128)S(1)}, f32[4,8,8,128]{3,2,1,0:T(8,128)S(1)}, u32[]{:S(2)}, u32[]{:S(2)}) %collective-permute-start.2) | collective-permute-done | bytes 131104 | tf_op jit(solution)/shard_map/ppermute | solution.py:742
  18.8 1.9 %collective-permute-start.3 = (f32[8,8,8,128]{3,2,1,0:T(8,128)S(1)}, f32[8,8,8,128]{3,2,1,0:T(8,128)S(1)}, u32[]{:S(2)}, u32[]{:S(2)}) collective-permute-start(f32[8,8,8,128]{3,2,1,0:T(8,128)S(1)} %pad_maximum_fusion), channel_id=1, source_target_pairs={{0,4},{2,6},{4,0},{6,2},{8,12},{10,14},{12,8},{14,10},{16,20},{18,... | collective-permute-start | bytes 786440 | tf_op jit(solution)/shard_map/ppermute | solution.py:742
  20.8 4.5 %collective-permute-done.3 = f32[8,8,8,128]{3,2,1,0:T(8,128)S(1)} collective-permute-done((f32[8,8,8,128]{3,2,1,0:T(8,128)S(1)}, f32[8,8,8,128]{3,2,1,0:T(8,128)S(1)}, u32[]{:S(2)}, u32[]{:S(2)}) %collective-permute-start.3) | collective-permute-done | bytes 262176 | tf_op jit(solution)/shard_map/ppermute | solution.py:742
  25.3 0.0 copy-start.1
  25.3 0.1 collective-permute-start.4
  25.4 0.7 %pad_add_fusion.refs_0_ = s32[2]{0:T(128)} fusion(s32[1]{0:T(128)} %bitcast.1, s32[1]{0:T(128)} %bitcast), kind=kLoop, calls=%fused_computation.18 | loop fusion | flops 2 | bytes 16 | tf_op jit(solution)/shard_map/stack | solution.py:746
  26.0 1.2 %collective-permute-done.4.refs_2_ = f32[16,8,8,128]{3,2,1,0:T(8,128)S(1)} collective-permute-done((f32[16,8,8,128]{3,2,1,0:T(8,128)S(1)}, f32[16,8,8,128]{3,2,1,0:T(8,128)S(1)}, u32[]{:S(2)}, u32[]{:S(2)}) %collective-permute-start.4) | collective-permute-done | bytes 524320 | tf_op jit(solution)/shard_map/ppermute | solution.py:742
  27.3 0.0 copy-done.1
  27.3 0.0 copy-start.2
  27.3 0.8 %copy-done.2 = f32[16,8,8,128]{3,2,1,0:T(8,128)} copy-done((f32[16,8,8,128]{3,2,1,0:T(8,128)}, f32[16,8,8,128]{3,2,1,0:T(8,128)S(1)}, u32[]{:S(2)}) %copy-start.2) | copy-done | bytes 524312
  28.1 23.8 %solve_all.1 = (f32[8,8,128]{2,1,0:T(8,128)}, f32[8,8,128]{2,1,0:T(8,128)}, f32[8,128]{1,0:T(8,128)}) custom-call(s32[2]{0:T(128)} %pad_add_fusion.refs_0_, f32[16,8,8,128]{3,2,1,0:T(8,128)} %copy-done.1, f32[16,8,8,128]{3,2,1,0:T(8,128)} %copy-done.2, bf16[256,768]{1,0:T(8,128)(2,1)} %constant.59.clone.refs_3_, bf16[256,768]{1,0:T(8,128)(2,1)} %constant.60.clone.refs_4_, ...), custom_call_target="tpu_custom_call" | custom-call | tf_op jit(solution)/shard_map/solve_all/pallas_call | solution.py:704
  51.9 1.2 %slice.23 = f32[1,1]{1,0:T(1,128)} slice(f32[8,128]{1,0:T(8,128)} %get-tuple-element.8), slice={[0:1], [0:1]} | slice | bytes 8 | tf_op jit(solution)/shard_map/slice | solution.py:748
  (11 shorter events, 0.1 us)
Async XLA Ops:
  0.7 0.9 %copy-start = (f32[8,8,128]{2,1,0:T(8,128)S(1)}, f32[8,8,128]{2,1,0:T(8,128)}, u32[]{:S(2)}) copy-start(f32[8,8,128]{2,1,0:T(8,128)} %param.12) | copy-start | bytes 98308
  1.7 0.7 %copy-start.3 = (f32[1,1,16]{2,1,0:T(1,128)S(1)}, f32[1,1,16]{2,1,0:T(1,128)}, u32[]{:S(2)}) copy-start(f32[1,1,16]{2,1,0:T(1,128)} %param.13) | copy-start | bytes 196
  2.5 0.7 %copy-start.4 = (f32[1,1,16]{2,1,0:T(1,128)S(1)}, f32[1,1,16]{2,1,0:T(1,128)}, u32[]{:S(2)}) copy-start(f32[1,1,16]{2,1,0:T(1,128)} %param.14) | copy-start | bytes 196
  3.5 4.9 %collective-permute-start = (f32[1,8,8,128]{3,2,1,0:T(8,128)S(1)}, f32[1,8,8,128]{3,2,1,0:T(8,128)S(1)}, u32[]{:S(2)}, u32[]{:S(2)}) collective-permute-start(f32[1,8,8,128]{3,2,1,0:T(8,128)S(1)} %get-tuple-element.10), channel_id=1, source_target_pairs={{0,1},{1,0},{2,3},{3,2},{4,5},{5,4},{6,7},{7,6},{8,9},{9,8},{10,11... | collective-permute-start | bytes 98312 | tf_op jit(solution)/shard_map/ppermute | solution.py:738
  8.4 5.4 %collective-permute-start.1 = (f32[2,8,8,128]{3,2,1,0:T(8,128)S(1)}, f32[2,8,8,128]{3,2,1,0:T(8,128)S(1)}, u32[]{:S(2)}, u32[]{:S(2)}) collective-permute-start(f32[2,8,8,128]{3,2,1,0:T(8,128)S(1)} %pad_maximum_fusion.2), channel_id=1, source_target_pairs={{0,16},{2,18},{4,20},{6,22},{8,24},{10,26},{12,28},{14,30},{16,0},... | collective-permute-start | bytes 196616 | tf_op jit(solution)/shard_map/ppermute | solution.py:742
  13.8 5.0 %collective-permute-start.2 = (f32[4,8,8,128]{3,2,1,0:T(8,128)S(1)}, f32[4,8,8,128]{3,2,1,0:T(8,128)S(1)}, u32[]{:S(2)}, u32[]{:S(2)}) collective-permute-start(f32[4,8,8,128]{3,2,1,0:T(8,128)S(1)} %pad_maximum_fusion.1), channel_id=1, source_target_pairs={{0,8},{2,10},{4,12},{6,14},{8,0},{10,2},{12,4},{14,6},{16,24},{18,... | collective-permute-start | bytes 393224 | tf_op jit(solution)/shard_map/ppermute | solution.py:742
  18.8 6.4 %collective-permute-start.3 = (f32[8,8,8,128]{3,2,1,0:T(8,128)S(1)}, f32[8,8,8,128]{3,2,1,0:T(8,128)S(1)}, u32[]{:S(2)}, u32[]{:S(2)}) collective-permute-start(f32[8,8,8,128]{3,2,1,0:T(8,128)S(1)} %pad_maximum_fusion), channel_id=1, source_target_pairs={{0,4},{2,6},{4,0},{6,2},{8,12},{10,14},{12,8},{14,10},{16,20},{18,... | collective-permute-start | bytes 786440 | tf_op jit(solution)/shard_map/ppermute | solution.py:742
  25.3 2.0 %copy-start.1 = (f32[16,8,8,128]{3,2,1,0:T(8,128)}, f32[16,8,8,128]{3,2,1,0:T(8,128)S(1)}, u32[]{:S(2)}) copy-start(f32[16,8,8,128]{3,2,1,0:T(8,128)S(1)} %constant_dynamic-update-slice_fusion.refs_1_) | copy-start | bytes 1572868
  25.3 2.0 %collective-permute-start.4 = (f32[16,8,8,128]{3,2,1,0:T(8,128)S(1)}, f32[16,8,8,128]{3,2,1,0:T(8,128)S(1)}, u32[]{:S(2)}, u32[]{:S(2)}) collective-permute-start(f32[16,8,8,128]{3,2,1,0:T(8,128)S(1)} %constant_dynamic-update-slice_fusion.refs_1_), channel_id=1, source_target_pairs={{0,2},{2,0},{4,6},{6,4},{8,10},{10,8},{12,14},{14,12},{16,18},{18,... | collective-permute-start | bytes 1572872 | tf_op jit(solution)/shard_map/ppermute | solution.py:742
  27.3 0.8 %copy-start.2 = (f32[16,8,8,128]{3,2,1,0:T(8,128)}, f32[16,8,8,128]{3,2,1,0:T(8,128)S(1)}, u32[]{:S(2)}) copy-start(f32[16,8,8,128]{3,2,1,0:T(8,128)S(1)} %collective-permute-done.4.refs_2_) | copy-start | bytes 1572868

commit v2 on v1

--- a/solution.py
+++ b/solution.py
@@ -278,58 +278,68 @@
     return np.concatenate([high, high, low], axis=1)
 
 
+J_ORDER = (0, 1, 2, 3, 7, 5, 6, 4)
+PAIRS = ((0, 7), (1, 2), (3, 4), (5, 6))
+FACE = (0, 1, 3, 2)
+ROWS1 = tuple(
+    (k * 4 + FACE[2 * ih + il]) * 4 + FACE[2 * jh + jl]
+    for k in range(4) for ih in range(2) for jh in range(2) for il in range(2) for jl in range(2)
+)
+ROWS2 = tuple((k * 2 + i) * 2 + j for j in range(2) for k in range(2) for i in range(2))
+
+
+def padded(matrix, rows, columns):
+    return np.pad(matrix, ((0, rows - matrix.shape[0]), (0, columns - matrix.shape[1])))
+
+
 class Tables:
     def __init__(self):
-        self.tables = [lobatto(count) for count in (8, 4, 2)]
-        self.weights = [table[1] for table in self.tables]
-        self.stiff = [table[2].T @ np.diag(table[1]) @ table[2] for table in self.tables]
-        interps = [
-            lagrange(self.tables[level][0], self.tables[level + 1][0]) for level in range(2)
-        ]
-        order = [0, 7, 1, 2, 3, 4, 5, 6]
-        w, k = np.diag(self.weights[0]), self.stiff[0]
+        tables = [lobatto(count) for count in (8, 4, 2)]
+        self.weights = [table[1] for table in tables]
+        stiff = [table[2].T @ np.diag(table[1]) @ table[2] for table in tables]
+        self.squares = [np.sum(t[2] * t[2] * t[1][:, None], axis=0) for t in tables]
+        interps = [lagrange(tables[level][0], tables[level + 1][0]) for level in range(2)]
+        factor = [np.where((np.arange(n) == 0) | (np.arange(n) == n - 1), 0.5, 1.0) for n in (8, 4)]
+        down = [interps[level].T * factor[level][None, :] for level in range(2)]
+        flat = [i for pair in PAIRS for i in pair]
+        rows0 = [(k * 8 + i) * 8 + j for k in range(8) for i in range(8) for j in J_ORDER]
+        data0 = [(k * 8 + i) * 8 + j for k in range(8) for i in flat for j in J_ORDER]
+        rows1, rows2 = list(ROWS1), list(ROWS2)
+        w, k = np.diag(self.weights[0]), stiff[0]
         plane = np.kron(k, w) + np.kron(w, k)
         both = np.kron(w, w)
         flip = k[:4, ::-1][:, :4]
-        even = 0.5 * (k[:4, :4] + flip)
-        odd = 0.5 * (k[:4, :4] - flip)
-        half = 0.5 * w[:4, :4]
-        columns = np.concatenate(
-            [np.arange(8) + 64 * kk + 8 * i for kk in range(4) for i in order]
-        )
-        self.even = stacked((np.kron(even, both) + np.kron(half, plane))[:, columns])
-        self.odd = stacked((np.kron(odd, both) + np.kron(half, plane))[:, columns])
-        factor = [np.where((np.arange(n) == 0) | (np.arange(n) == n - 1), 0.5, 1.0) for n in (8, 4)]
-        down = [interps[level].T * factor[level][None, :] for level in range(2)]
-        full = np.concatenate([np.arange(8) + 64 * kk + 8 * i for kk in range(8) for i in order])
-        high, low = split_const(triple(down[0], down[0], down[0])[:, full])
+        half = np.kron(0.5 * w[:4, :4], plane)
+        even = np.kron(0.5 * (k[:4, :4] + flip), both) + half
+        odd = np.kron(0.5 * (k[:4, :4] - flip), both) + half
+        self.even = stacked(even[np.ix_(rows0[:256], data0[:256])])
+        self.odd = stacked(odd[np.ix_(rows0[:256], data0[:256])])
+        high, low = split_const(triple(down[0], down[0], down[0])[np.ix_(rows1, data0)])
         self.down0 = np.concatenate([high, low], axis=0)
-        self.up0 = stacked(triple(interps[0], interps[0], interps[0]))
-        w, k = np.diag(self.weights[1]), self.stiff[1]
-        self.op1 = stacked(triple(k, w, w) + triple(w, k, w) + triple(w, w, k))
-        self.down1 = triple(down[1], down[1], down[1]).astype(np.float32)
-        self.up1 = triple(interps[1], interps[1], interps[1]).astype(np.float32)
-        w, k = np.diag(self.weights[2]), self.stiff[2]
-        self.op2 = (triple(k, w, w) + triple(w, k, w) + triple(w, w, k)).astype(np.float32)
-        self.squares = [
-            np.sum(table[2] * table[2] * table[1][:, None], axis=0) for table in self.tables
-        ]
+        self.up0 = stacked(triple(interps[0], interps[0], interps[0])[np.ix_(rows0, rows1)])
+        w, k = np.diag(self.weights[1]), stiff[1]
+        self.op1 = stacked((triple(k, w, w) + triple(w, k, w) + triple(w, w, k))[np.ix_(rows1, rows1)])
+        self.down1 = padded(stacked(triple(down[1], down[1], down[1])[np.ix_(rows2, rows1)]), 16, 192)
+        self.up1 = padded(stacked(triple(interps[1], interps[1], interps[1])[np.ix_(rows1, rows2)]), 64, 32)
+        w, k = np.diag(self.weights[2]), stiff[2]
+        self.op2 = padded(
+            stacked((triple(k, w, w) + triple(w, k, w) + triple(w, w, k))[np.ix_(rows2, rows2)]), 16, 32)
         wide = lambda column: np.repeat(np.asarray(column, np.float32)[:, None], LANES, axis=1)
-        mass, point = [], []
-        for level in (1, 2):
+        blocks = [wide(self.weights[0][list(J_ORDER)]), wide(self.squares[0][list(J_ORDER)]),
+                  wide(factor[0][list(J_ORDER)])]
+        for level, order in ((1, rows1), (2, rows2)):
             a, b = self.weights[level], self.squares[level]
-            mass.append(wide(triple(a, a, a)))
-            point.append(wide(triple(b, a, a) + triple(a, b, a) + triple(a, a, b)))
-        self.rows = np.concatenate(
-            [wide(self.weights[0]), wide(self.squares[0]), mass[0], point[0], mass[1], point[1],
-             wide(factor[0])], axis=0)
-
-
-PAIRS = ((0, 7), (1, 2), (3, 4), (5, 6))
+            blocks.append(wide(triple(a, a, a)[order]))
+            blocks.append(wide((triple(b, a, a) + triple(a, b, a) + triple(a, a, b))[order]))
+        self.rows = np.concatenate(blocks, axis=0)
+
+
+def swap_rows(x, sub):
+    return jnp.where(sub == 4, pltpu.roll(x, 5, 0), jnp.where(sub == 7, pltpu.roll(x, 3, 0), x))
 
 
 def kernel(nx, ny, tables, meta, near, far, even, odd, down0, up0, op1, down1, up1, op2, rows,
-           sol_ref, res_ref, rel_ref, b_ref, r_ref, d_ref, z_ref, v_ref, re_ref, ro_ref,
+           sol_ref, res_ref, rel_ref, b_ref, r_ref, d_ref, v_ref, p_ref, z_ref, re_ref, ro_ref,
            be_ref, bo_ref, c_ref, lane_ref):
     groups = nx // SUBS
     tiles = ny * groups
@@ -352,49 +362,55 @@
 
     sub_w = across(sub)
 
-    def shift_y(parts, step):
-        return [parts[((t // groups - step) % ny) * groups + t % groups] for t in range(tiles)]
-
-    def x_up(x):
+    def x_up(x, more=0):
         parts, out = cols(x), []
         for t in range(tiles):
-            prev = parts[(t // groups) * groups + (t % groups - 1) % groups]
-            out.append(jnp.where(lane == 0, pltpu.roll(prev, LANES - SUBS + 1, 1),
-                                 pltpu.roll(parts[t], 1, 1)))
+            if t % groups:
+                prev = parts[t - 1]
+                out.append(pltpu.roll(prev, more, 1) if more else prev)
+            else:
+                prev = parts[t + groups - 1]
+                out.append(jnp.where(lane == 0, pltpu.roll(prev, (LANES - SUBS + 1 + more) % LANES, 1),
+                                     pltpu.roll(prev, 1 + more, 1)))
         return join(out)
 
-    def x_down(x):
+    def x_down(x, more=0):
         parts, out = cols(x), []
         for t in range(tiles):
-            succ = parts[(t // groups) * groups + (t % groups + 1) % groups]
-            out.append(jnp.where(lane == SUBS - 1, pltpu.roll(succ, SUBS - 1, 1),
-                                 pltpu.roll(parts[t], LANES - 1, 1)))
+            if t % groups < groups - 1:
+                succ = parts[t + 1]
+                out.append(pltpu.roll(succ, more, 1) if more else succ)
+            else:
+                succ = parts[t - groups + 1]
+                out.append(jnp.where(lane == SUBS - 1, pltpu.roll(succ, SUBS - 1 + more, 1),
+                                     pltpu.roll(succ, (LANES - 1 + more) % LANES, 1)))
         return join(out)
 
+    up, down = SUBS, LANES - SUBS
+
     def z_up(x):
-        return join([pltpu.roll(p, SUBS, 1) for p in cols(x)])
+        return join([pltpu.roll(p, up, 1) for p in cols(x)])
 
     def z_down(x):
-        return join([pltpu.roll(p, LANES - SUBS, 1) for p in cols(x)])
-
-    def y_fold(x, first, last, low, high):
-        before = join(shift_y(cols(x), 1))
-        after = join(shift_y(cols(x), -1))
-        return x + jnp.where(first, pltpu.roll(before, low, 0),
-                             jnp.where(last, pltpu.roll(after, high, 0), 0.0))
-
-    def fold_y8(x):
-        return y_fold(x, sub_w == 0, sub_w == 7, 1, 7)
+        return join([pltpu.roll(p, down, 1) for p in cols(x)])
+
+    def y_fold(x, face):
+        parts = cols(x)
+        other = join([parts[(t + groups) % tiles] for t in range(tiles)])
+        return x + jnp.where(face, pltpu.roll(other, 4, 0), 0.0)
+
+    face0 = sub_w % 4 == 0
+    face1 = sub_w % 2 == 0
 
     def row(k, i):
         return pl.ds(k * 64 + i * 8, 8)
 
-    even_own = (own_x & 1) == 0
     for t in range(tiles):
-        y_index, high = t // groups, t % groups
+        y_index, part = t // groups, t % groups
+        use_near = ((part ^ own_x) & 1) == 0
         slots = []
-        for c in range(0, SUBS, 2):
-            delta = (high * SUBS + c) ^ own_x
+        for c in range(SUBS):
+            delta = (c * groups + part) ^ own_x
             slot, bit = jnp.int32(0), 0
             if ny > 1:
                 slot, bit = y_index ^ own_y, 1
@@ -406,11 +422,7 @@
                 step //= 2
             slots.append(slot)
         for i in range(8):
-            block = []
-            for slot in slots:
-                a, b = near[slot, i], far[slot, i]
-                block.append(jnp.where(even_own, a, b))
-                block.append(jnp.where(even_own, b, a))
+            block = [jnp.where(use_near, near[slot, i], far[slot, i]) for slot in slots]
             for step in (1, 2, 4):
                 out = list(block)
                 for c in range(SUBS):
@@ -431,7 +443,7 @@
     sig = jnp.broadcast_to(sig1, (SUBS, wide))
     w_j = across(rows[0:8, :])
     q_j = across(rows[8:16, :])
-    f_j = across(rows[160:168, :])
+    f_j = across(rows[16:24, :])
     sig_w = sig * w_j
 
     def store_split(kk, index, low_pair, high_pair):
@@ -464,7 +476,7 @@
                 a, b = vals[0][s], vals[1][s]
                 vals[0][s] = a + x_up(b)
                 vals[1][s] = b + x_down(a)
-        return [[fold_y8(x) for x in v] for v in vals]
+        return [[y_fold(x, face0) for x in v] for v in vals]
 
     def point(k, i):
         s1 = q[k] * w[i] + w[k] * q[i]
@@ -483,10 +495,11 @@
                     inverse = 1.0 / diag[n][s]
                     b_ref[row(k, i), :] = load[n][s]
                     r_ref[row(k, i), :] = load[n][s]
-                    first = load[n][s] * inverse * (1.0 / THETA)
+                    scaled = inverse * (1.0 / THETA)
+                    p_ref[row(k, i), :] = inverse * PUSH
+                    first = load[n][s] * scaled
                     d_ref[row(k, i), :] = first
-                    z_ref[row(k, i), :] = jnp.zeros_like(first)
-                    group.append((first, inverse))
+                    group.append((first, scaled))
                 dirs.append([g[0] for g in group])
                 for n, i in enumerate(pair):
                     v_ref[row(k, i), :] = group[n][1]
@@ -495,51 +508,52 @@
     def tile_rows(x):
         return jnp.concatenate([x] * tiles, axis=1)
 
+    low_face = (sub_w // 2) % 2 == 0
+
     def fold1(x):
-        first = x[0:16] + z_up16(x[48:64])
-        last = x[48:64] + z_down16(x[0:16])
-        pieces = [first[0:8], first[8:16], x[16:24], x[24:32], x[32:40], x[40:48],
-                  last[0:8], last[8:16]]
+        p = [(x[16 * k:16 * k + 8], x[16 * k + 8:16 * k + 16]) for k in range(4)]
         out = []
-        for k in range(4):
-            a, b = pieces[2 * k], pieces[2 * k + 1]
-            lower = sub_w < 4
-            na = a + jnp.where(lower, x_up(pltpu.roll(b, 4, 0)), 0.0)
-            nb = b + jnp.where(lower, 0.0, x_down(pltpu.roll(a, 4, 0)))
-            out += [na, nb]
-        j = sub_w % 4
-        out = [y_fold(x, j == 0, j == 3, 5, 3) for x in out]
+        for k, (a, b) in enumerate(p):
+            na, nb = x_up(b), x_down(a)
+            if k in (0, 3):
+                c, e = p[3 - k]
+                move, amount = (z_up, up) if k == 0 else (z_down, down)
+                na = na + x_up(e, amount)
+                nb = nb + x_down(c, amount)
+                a, b = a + move(c), b + move(e)
+            out.append(y_fold(a + jnp.where(low_face, na, 0.0), face1))
+            out.append(y_fold(b + jnp.where(low_face, nb, 0.0), face1))
         return jnp.concatenate(out, axis=0)
 
-    def z_up16(x):
-        return jnp.concatenate([z_up(x[0:8]), z_up(x[8:16])], axis=0)
-
-    def z_down16(x):
-        return jnp.concatenate([z_down(x[0:8]), z_down(x[8:16])], axis=0)
+    first_k = (sub_w // 2) % 2 == 0
+    first_i = sub_w % 2 == 0
 
     def fold2(x):
-        other = pltpu.roll(x, 4, 0)
-        x = x + jnp.where(sub_w < 4, z_up(other), z_down(other))
-        i = (sub_w // 2) % 2
-        x = x + jnp.where(i == 0, x_up(pltpu.roll(x, 6, 0)), x_down(pltpu.roll(x, 2, 0)))
-        j = sub_w % 2
-        return y_fold(x, j == 0, j == 1, 7, 1)
+        other_k = jnp.where(first_k, pltpu.roll(x, 6, 0), pltpu.roll(x, 2, 0))
+        other_i = jnp.where(first_i, pltpu.roll(x, 7, 0), pltpu.roll(x, 1, 0))
+        both = jnp.where(first_i, pltpu.roll(other_k, 7, 0), pltpu.roll(other_k, 1, 0))
+        x = x + jnp.where(first_k, z_up(other_k), z_down(other_k))
+        x = x + jnp.where(first_i, x_up(other_i), x_down(other_i))
+        x = x + jnp.where(first_k, jnp.where(first_i, x_up(both, up), x_down(both, up)),
+                          jnp.where(first_i, x_up(both, down), x_down(both, down)))
+        return y_fold(x, sub_w >= 0)
 
     def cat3(x):
         high = x.astype(jnp.bfloat16)
         low = (x - high.astype(jnp.float32)).astype(jnp.bfloat16)
         return jnp.concatenate([high, low, high], axis=0)
 
+    def cat3_small(x):
+        high = x.astype(jnp.bfloat16).astype(jnp.float32)
+        return jnp.concatenate([high, x - high, high, jnp.zeros_like(x)], axis=0).astype(jnp.bfloat16)
+
     def dot(a, b):
         return jnp.dot(a, b, preferred_element_type=jnp.float32)
 
-    def dot_high(a, b):
-        return jnp.dot(a, b, preferred_element_type=jnp.float32, precision=lax.Precision.HIGHEST)
-
-    mass1 = tile_rows(rows[16:80, :])
-    point1 = tile_rows(rows[80:144, :])
-    mass2 = tile_rows(rows[144:152, :])
-    point2 = tile_rows(rows[152:160, :])
+    mass1 = tile_rows(rows[24:88, :])
+    point1 = tile_rows(rows[88:152, :])
+    mass2 = tile_rows(rows[152:160, :])
+    point2 = tile_rows(rows[160:168, :])
     inv1_ref, mass1_ref = lane_ref.at[8:72, :], lane_ref.at[72:136, :]
     inv1_ref[...] = 1.0 / fold1(kap1 * point1 + sig1 * mass1)
     mass1_ref[...] = sig1 * mass1
@@ -551,7 +565,7 @@
         return fold1(kap1 * dot(op1[...], cat3(v)) + mass1_ref[...] * v)
 
     def apply2(v):
-        return fold2(kap1 * dot_high(op2[...], v) + lane_ref[144:152, :] * v)
+        return fold2(kap1 * dot(op2[...], cat3_small(v))[0:8] + lane_ref[144:152, :] * v)
 
     def coarse(resid):
         inverse = inv1_ref[...]
@@ -561,13 +575,13 @@
         d = KEEP * d + PUSH * (resid * inverse)
         x = x + d
         resid = resid - apply1(d)
-        low = fold2(dot_high(down1[...], resid))
+        low = fold2(dot(down1[...], cat3(resid))[0:8])
         inverse2 = lane_ref[136:144, :]
         d = low * inverse2 * (1.0 / THETA)
         y = d
         low = low - apply2(d)
         y = y + KEEP * d + PUSH * (low * inverse2)
-        e = dot_high(up1[...], y)
+        e = dot(up1[...], cat3_small(y))
         x = x + e
         resid = resid - apply1(e)
         return x + resid * inverse * (1.0 / THETA)
@@ -600,26 +614,17 @@
         r = r_ref[row(k, i), :] - value
         r_ref[row(k, i), :] = r
         first = d_ref[row(k, i), :]
-        d = KEEP * first + PUSH * (r * v_ref[row(k, i), :])
-        z_ref[row(k, i), :] = z_ref[row(k, i), :] + (first + d)
-        return d
+        return KEEP * first + r * p_ref[row(k, i), :]
 
     def residual_only(k, i, value):
         r = r_ref[row(k, i), :] - value
         r_ref[row(k, i), :] = r
         return r
 
-    def last_direction(k, i, value):
+    def next_direction(k, i, value):
         r = r_ref[row(k, i), :] - value
         r_ref[row(k, i), :] = r
-        d = r * v_ref[row(k, i), :] * (1.0 / THETA)
-        z_ref[row(k, i), :] = z_ref[row(k, i), :] + d
-        return d
-
-    def first_direction(k, i, value):
-        r = r_ref[row(k, i), :] - value
-        r_ref[row(k, i), :] = r
-        return r * v_ref[row(k, i), :] * (1.0 / THETA)
+        return r * v_ref[row(k, i), :]
 
     def run(update, keep):
         for kk, index, dirs in sweep(update):
@@ -637,22 +642,29 @@
                     c_ref[at:at + 16, :] = high
                     c_ref[512 + at:528 + at, :] = low
 
+    start = pl.multiple_of((own_y * groups + own_x % groups) * LANES, LANES)
+    window = pl.ds(start, LANES)
+    z_ref[...] = jnp.zeros((512, LANES), jnp.float32)
+
+    def collect():
+        z_ref[...] = z_ref[...] + d_ref[:, window]
+
     def cycle(step, carry):
+        collect()
         run(second_direction, True)
+        collect()
         run(residual_only, False)
         both = dot(down0[...], c_ref[0:512, :])
         low = both[0:64] + both[64:128] + dot(down0[0:64, :], c_ref[512:1024, :])
         correction = coarse(fold1(low))
         d_ref[...] = dot(up0[...], cat3(correction))
+        collect()
         for kk in range(4):
             for index, pair in enumerate(PAIRS):
-                dirs = [[d_ref[row(k, i), :] for i in pair] for k in (kk, 7 - kk)]
-                for s, k in enumerate((kk, 7 - kk)):
-                    for n, i in enumerate(pair):
-                        z_ref[row(k, i), :] = z_ref[row(k, i), :] + dirs[s][n]
-                store_split(kk, index, dirs[0], dirs[1])
-        run(last_direction, True)
-        run(first_direction, True)
+                store_split(kk, index, *[[d_ref[row(k, i), :] for i in pair] for k in (kk, 7 - kk)])
+        run(next_direction, True)
+        collect()
+        run(next_direction, True)
         return carry
 
     lax.fori_loop(0, 2, cycle, 0)
@@ -676,22 +688,20 @@
             res = b - coef * (b - r_ref[row(k, i), :])
             rr = rr + res * res * (f[k] * f[i])
     rr = jnp.sum(rr * f_j)
-    rel_ref[...] = jnp.sqrt(jnp.full((SUBS, LANES), rr / bb, jnp.float32))
-    start = pl.multiple_of((own_y * groups + own_x // SUBS) * LANES, LANES)
-    place = own_x % SUBS
-    window = pl.ds(start, LANES)
+    rel_ref[0] = jnp.sqrt(rr / bb)
+    place = own_x // groups
     for i in range(8):
         sol = jnp.zeros((SUBS, LANES), jnp.float32)
         res = sol
         for k in range(8):
             b = b_ref[row(k, i), window]
-            z = z_ref[row(k, i), window]
+            z = z_ref[row(k, i), :]
             r = b - coef * (b - r_ref[row(k, i), window])
             turn = (k - place) % LANES
             sol = jnp.where(lane == k, pltpu.roll(z, turn, 1), sol)
             res = jnp.where(lane == k, pltpu.roll(r, turn, 1), res)
-        sol_ref[i] = coef * sol
-        res_ref[i] = res
+        sol_ref[i] = swap_rows(coef * sol, sub)
+        res_ref[i] = swap_rows(res, sub)
 
 
 def solve_all(nx, ny, meta, near, far, interpret=False):
@@ -704,36 +714,55 @@
     return pl.pallas_call(
         lambda *refs: kernel(nx, ny, tables, *refs),
         in_specs=[pl.BlockSpec(memory_space=pltpu.SMEM)] + [vmem] * 11,
-        out_specs=[vmem] * 3,
+        out_specs=[vmem, vmem, pl.BlockSpec(memory_space=pltpu.SMEM)],
         out_shape=[
             jax.ShapeDtypeStruct(near.shape[1:], jnp.float32),
             jax.ShapeDtypeStruct(near.shape[1:], jnp.float32),
-            jax.ShapeDtypeStruct((SUBS, LANES), jnp.float32),
+            jax.ShapeDtypeStruct((1,), jnp.float32),
         ],
         scratch_shapes=[
-            field, field, field, field, field,
+            field, field, field, field, field, pltpu.VMEM((512, LANES), jnp.float32),
             pltpu.VMEM((256, wide), jnp.float32), pltpu.VMEM((256, wide), jnp.float32),
             pltpu.VMEM((768, wide), jnp.bfloat16), pltpu.VMEM((768, wide), jnp.bfloat16),
             pltpu.VMEM((1024, wide), jnp.bfloat16), pltpu.VMEM((152, wide), jnp.float32),
         ],
         name="solve_all",
         interpret=interpret,
-    )(meta, near, far, *[jnp.asarray(c) for c in consts])
+    )(meta, *[pltpu.with_memory_space_constraint(x, pltpu.VMEM)
+             for x in (near, far, *[jnp.asarray(c) for c in consts])])
+
+
+def pack_kernel(forcing, kappa, sigma, out_ref, coef_ref):
+    sub = lax.broadcasted_iota(jnp.int32, (SUBS, LANES), 0)
+    lane = lax.broadcasted_iota(jnp.int32, (SUBS, LANES), 1)
+    count = kappa.shape[2]
+    coef_ref[...] = jnp.zeros((SUBS, LANES), jnp.float32)
+    coef_ref[0:1, 0:count] = kappa[0]
+    coef_ref[1:2, 0:count] = sigma[0]
+    spread = jnp.take_along_axis(coef_ref[...], lane // SUBS, axis=1)
+    for i in range(SUBS):
+        x = swap_rows(forcing[i], sub)
+        x = x + jnp.where(lane % SUBS == 0, pltpu.roll(x, 1, 1), 0.0)
+        if i == 0:
+            x = jnp.where(lane % SUBS == SUBS - 1, spread, x)
+        out_ref[0, i] = x
 
 
 def packed_block(forcing, kappa, sigma):
-    field = fold_axis(forcing, 2, SUBS)
-    shape = field.shape
-    index = [lax.broadcasted_iota(jnp.int32, shape, dim) for dim in range(3)]
-    last = (index[2] % SUBS == SUBS - 1) & (index[0] == 0)
-    wide = lambda value: jnp.repeat(value.reshape(-1), SUBS)[None, None, :]
-    field = jnp.where(last & (index[1] == 0), wide(kappa), field)
-    return jnp.where(last & (index[1] == 1), wide(sigma), field)
+    vmem = pl.BlockSpec(memory_space=pltpu.VMEM)
+    return pl.pallas_call(
+        pack_kernel,
+        in_specs=[vmem] * 3,
+        out_specs=vmem,
+        out_shape=jax.ShapeDtypeStruct((1, *forcing.shape), jnp.float32),
+        scratch_shapes=[pltpu.VMEM((SUBS, LANES), jnp.float32)],
+        name="pack_block",
+    )(forcing, kappa, sigma)
 
 
 def gathered(forcing, kappa, sigma):
     nx, ny = lax.axis_size("gx"), lax.axis_size("gy")
-    block = packed_block(forcing, kappa, sigma)[None]
+    block = packed_block(forcing, kappa, sigma)
     if ny > 1:
         other = lax.ppermute(block, "gy", [(i, i ^ 1) for i in range(ny)])
         block = jnp.concatenate([block, other], axis=0)
@@ -745,7 +774,7 @@
         step //= 2
     meta = jnp.stack([lax.axis_index("gx"), lax.axis_index("gy")]).astype(jnp.int32)
     sol, res, rel = solve_all(nx, ny, meta, block, other)
-    return sol, res, rel[0, 0]
+    return sol, res, rel.reshape(())
 
 
 def fits_one_device(mesh):

time: 53.4 us -> 48.2 us (0.903)
  local copies, waits for them, and re-layouts: 4.67 us -> 0.09 us
  Pallas kernels: 23.8 us -> 22.5 us
  other arithmetic: 0.83 us -> 1.44 us
    pallas_call x1, Pallas kernels: 23.8 us -> 21 us  [solve_all(): pl.pallas_call(lambda *refs: kernel(nx, ny, tables, *refs), in_specs=[pl....]
    slice x3 -> x0, local copies, waits for them, and re-layouts: 2.19 us -> none  [the longest x1 1.18 us: gathered(): return (sol, res, rel[0, 0])]
    unnamed x13 -> x24, local copies, waits for them, and re-layouts: 2.15 us -> 0.08 us
    pallas_call x0 -> x1, Pallas kernels: none -> 1.47 us  [packed_block(): pl.pallas_call(pack_kernel, in_specs=[vmem] * 3, out_specs=vmem, out_shap...]
    concatenate x3, other arithmetic: 0.03 us -> 0.79 us  [gathered(): block = jnp.concatenate([block, other], axis=0)]
where the time goes in v2:
time: 48.2 us; the launch traced here: 47.9 us
  Pallas kernels  22.5 us (47%)
  waiting for transfers between devices  13.1 us (27%)
  starting transfers between devices  9.98 us (21%)
  other arithmetic  1.44 us (3%)
  between operations  0.77 us (2%)
    pallas_call x1, Pallas kernels, solve_all(): pl.pallas_call(lambda *refs: kernel(nx, ny, tables, *refs), in_specs=[pl....  21 us
    ppermute x4, waiting for transfers between devices, gathered(): other = lax.ppermute(block, 'gx', [(i, i ^ step) for i in range(nx)])  11 us
    ppermute x4, starting transfers between devices, gathered(): other = lax.ppermute(block, 'gx', [(i, i ^ step) for i in range(nx)])  7.01 us
    ppermute x1, starting transfers between devices, gathered(): other = lax.ppermute(block, 'gy', [(i, i ^ 1) for i in range(ny)])  2.97 us
    ppermute x1, waiting for transfers between devices, gathered(): other = lax.ppermute(block, 'gy', [(i, i ^ 1) for i in range(ny)])  2.17 us
    pallas_call x1, Pallas kernels, packed_block(): pl.pallas_call(pack_kernel, in_specs=[vmem] * 3, out_specs=vmem, out_shap...  1.47 us
  transfers between devices with their start and end apart: 5, of which 5 were waited for; matrix products, arithmetic and copies ran while one was open for 1% of the time, Pallas kernels for 0%

profile of v2, /device:TPU:0, one launch (start us, length us, event | category | flops | bytes accessed | tf_op | source)
XLA Modules:
  0.0 47.9 jit_solution(10804404685321195640)
XLA Ops:
  0.6 1.5 %pack_block.1 = f32[1,8,8,128]{3,2,1,0:T(8,128)} custom-call(f32[8,8,128]{2,1,0:T(8,128)} %forcing.1, f32[1,1,16]{2,1,0:T(1,128)} %kappa.1, f32[1,1,16]{2,1,0:T(1,128)} %sigma.1), custom_call_target="tpu_custom_call" | custom-call | tf_op jit(solution)/shard_map/pack_block/pallas_call | solution.py:753
  2.1 0.0 copy-start.9
  2.1 3.0 %collective-permute-start = (f32[1,8,8,128]{3,2,1,0:T(8,128)}, f32[1,8,8,128]{3,2,1,0:T(8,128)S(1)}, u32[]{:S(2)}, u32[]{:S(2)}) collective-permute-start(f32[1,8,8,128]{3,2,1,0:T(8,128)} %pack_block.1), channel_id=1, source_target_pairs={{0,1},{1,0},{2,3},{3,2},{4,5},{5,4},{6,7},{7,6},{8,9},{9,8},{10,11... | collective-permute-start | bytes 98312 | tf_op jit(solution)/shard_map/ppermute | solution.py:767
  5.1 2.2 %collective-permute-done = f32[1,8,8,128]{3,2,1,0:T(8,128)S(1)} collective-permute-done((f32[1,8,8,128]{3,2,1,0:T(8,128)}, f32[1,8,8,128]{3,2,1,0:T(8,128)S(1)}, u32[]{:S(2)}, u32[]{:S(2)}) %collective-permute-start) | collective-permute-done | bytes 32800 | tf_op jit(solution)/shard_map/ppermute | solution.py:767
  7.2 0.8 %pad_maximum_fusion.2 = f32[2,8,8,128]{3,2,1,0:T(8,128)S(1)} fusion(f32[1,8,8,128]{3,2,1,0:T(8,128)S(1)} %collective-permute-done, f32[1,8,8,128]{3,2,1,0:T(8,128)} %pack_block.1), kind=kLoop, calls=%fused_computation.2 | loop fusion | flops 16384 | bytes 131072 | tf_op jit(solution)/shard_map/concatenate | solution.py:768
  8.0 3.0 %collective-permute-start.1 = (f32[2,8,8,128]{3,2,1,0:T(8,128)S(1)}, f32[2,8,8,128]{3,2,1,0:T(8,128)S(1)}, u32[]{:S(2)}, u32[]{:S(2)}) collective-permute-start(f32[2,8,8,128]{3,2,1,0:T(8,128)S(1)} %pad_maximum_fusion.2), channel_id=1, source_target_pairs={{0,16},{2,18},{4,20},{6,22},{8,24},{10,26},{12,28},{14,30},{16,0},... | collective-permute-start | bytes 196616 | tf_op jit(solution)/shard_map/ppermute | solution.py:771
  11.1 2.2 %collective-permute-done.1 = f32[2,8,8,128]{3,2,1,0:T(8,128)S(1)} collective-permute-done((f32[2,8,8,128]{3,2,1,0:T(8,128)S(1)}, f32[2,8,8,128]{3,2,1,0:T(8,128)S(1)}, u32[]{:S(2)}, u32[]{:S(2)}) %collective-permute-start.1) | collective-permute-done | bytes 65568 | tf_op jit(solution)/shard_map/ppermute | solution.py:771
  13.3 0.0 copy-done.9
  13.3 2.0 %collective-permute-start.2 = (f32[4,8,8,128]{3,2,1,0:T(8,128)S(1)}, f32[4,8,8,128]{3,2,1,0:T(8,128)S(1)}, u32[]{:S(2)}, u32[]{:S(2)}) collective-permute-start(f32[4,8,8,128]{3,2,1,0:T(8,128)S(1)} %pad_maximum_fusion.1), channel_id=1, source_target_pairs={{0,8},{2,10},{4,12},{6,14},{8,0},{10,2},{12,4},{14,6},{16,24},{18,... | collective-permute-start | bytes 393224 | tf_op jit(solution)/shard_map/ppermute | solution.py:771
  15.3 3.1 %collective-permute-done.2 = f32[4,8,8,128]{3,2,1,0:T(8,128)S(1)} collective-permute-done((f32[4,8,8,128]{3,2,1,0:T(8,128)S(1)}, f32[4,8,8,128]{3,2,1,0:T(8,128)S(1)}, u32[]{:S(2)}, u32[]{:S(2)}) %collective-permute-start.2) | collective-permute-done | bytes 131104 | tf_op jit(solution)/shard_map/ppermute | solution.py:771
  18.4 0.0 copy-start.2
  18.4 0.0 copy-start.4
  18.4 1.9 %collective-permute-start.3 = (f32[8,8,8,128]{3,2,1,0:T(8,128)S(1)}, f32[8,8,8,128]{3,2,1,0:T(8,128)S(1)}, u32[]{:S(2)}, u32[]{:S(2)}) collective-permute-start(f32[8,8,8,128]{3,2,1,0:T(8,128)S(1)} %pad_maximum_fusion), channel_id=1, source_target_pairs={{0,4},{2,6},{4,0},{6,2},{8,12},{10,14},{12,8},{14,10},{16,20},{18,... | collective-permute-start | bytes 786440 | tf_op jit(solution)/shard_map/ppermute | solution.py:771
  20.3 0.0 copy-start.5
  20.3 0.0 copy-start.7
  20.3 0.0 copy-start.8
  20.3 0.0 copy-start.3
  20.3 0.0 copy-start
  20.4 0.0 copy-start.1
  20.4 4.4 %collective-permute-done.3 = f32[8,8,8,128]{3,2,1,0:T(8,128)S(1)} collective-permute-done((f32[8,8,8,128]{3,2,1,0:T(8,128)S(1)}, f32[8,8,8,128]{3,2,1,0:T(8,128)S(1)}, u32[]{:S(2)}, u32[]{:S(2)}) %collective-permute-start.3) | collective-permute-done | bytes 262176 | tf_op jit(solution)/shard_map/ppermute | solution.py:771
  24.8 0.0 copy-start.6
  24.9 0.1 collective-permute-start.4
  24.9 0.6 %pad_add_fusion.refs_0_ = s32[2]{0:T(128)} fusion(s32[1]{0:T(128)} %bitcast.1, s32[1]{0:T(128)} %bitcast), kind=kLoop, calls=%fused_computation.8 | loop fusion | flops 2 | bytes 16 | tf_op jit(solution)/shard_map/stack | solution.py:775
  25.6 1.2 %collective-permute-done.4.refs_2_ = f32[16,8,8,128]{3,2,1,0:T(8,128)S(1)} collective-permute-done((f32[16,8,8,128]{3,2,1,0:T(8,128)S(1)}, f32[16,8,8,128]{3,2,1,0:T(8,128)S(1)}, u32[]{:S(2)}, u32[]{:S(2)}) %collective-permute-start.4) | collective-permute-done | bytes 524320 | tf_op jit(solution)/shard_map/ppermute | solution.py:771
  26.8 0.0 copy-done.2
  26.8 0.0 copy-done.4
  26.8 0.0 copy-done.5
  26.8 0.0 copy-done.7
  26.9 0.0 copy-done.8
  26.9 0.0 copy-done.3
  26.9 0.0 copy-done
  26.9 0.0 copy-done.1
  26.9 0.0 copy-done.6
  26.9 21.0 %solve_all.1 = (f32[8,8,128]{2,1,0:T(8,128)}, f32[8,8,128]{2,1,0:T(8,128)}, f32[1]{0:T(128)}) custom-call(s32[2]{0:T(128)} %pad_add_fusion.refs_0_, f32[16,8,8,128]{3,2,1,0:T(8,128)S(1)} %constant_dynamic-update-slice_fusion.refs_1_, f32[16,8,8,128]{3,2,1,0:T(8,128)S(1)} %collective-permute-done.4.refs_2_, bf16[256,768]{1,0:T(8,128)(2,1)S(1)} %copy-done, ...), custom_call_target="tpu_custom_call" | custom-call | tf_op jit(solution)/shard_map/solve_all/pallas_call | solution.py:714
  (7 shorter events, 0.1 us)
Async XLA Ops:
  2.1 11.2 %copy-start.9 = (f32[1,8,8,128]{3,2,1,0:T(8,128)S(1)}, f32[1,8,8,128]{3,2,1,0:T(8,128)}, u32[]{:S(2)}) copy-start(f32[1,8,8,128]{3,2,1,0:T(8,128)} %pack_block.1) | copy-start | bytes 98308
  2.1 5.1 %collective-permute-start = (f32[1,8,8,128]{3,2,1,0:T(8,128)}, f32[1,8,8,128]{3,2,1,0:T(8,128)S(1)}, u32[]{:S(2)}, u32[]{:S(2)}) collective-permute-start(f32[1,8,8,128]{3,2,1,0:T(8,128)} %pack_block.1), channel_id=1, source_target_pairs={{0,1},{1,0},{2,3},{3,2},{4,5},{5,4},{6,7},{7,6},{8,9},{9,8},{10,11... | collective-permute-start | bytes 98312 | tf_op jit(solution)/shard_map/ppermute | solution.py:767
  8.0 5.3 %collective-permute-start.1 = (f32[2,8,8,128]{3,2,1,0:T(8,128)S(1)}, f32[2,8,8,128]{3,2,1,0:T(8,128)S(1)}, u32[]{:S(2)}, u32[]{:S(2)}) collective-permute-start(f32[2,8,8,128]{3,2,1,0:T(8,128)S(1)} %pad_maximum_fusion.2), channel_id=1, source_target_pairs={{0,16},{2,18},{4,20},{6,22},{8,24},{10,26},{12,28},{14,30},{16,0},... | collective-permute-start | bytes 196616 | tf_op jit(solution)/shard_map/ppermute | solution.py:771
  13.3 5.0 %collective-permute-start.2 = (f32[4,8,8,128]{3,2,1,0:T(8,128)S(1)}, f32[4,8,8,128]{3,2,1,0:T(8,128)S(1)}, u32[]{:S(2)}, u32[]{:S(2)}) collective-permute-start(f32[4,8,8,128]{3,2,1,0:T(8,128)S(1)} %pad_maximum_fusion.1), channel_id=1, source_target_pairs={{0,8},{2,10},{4,12},{6,14},{8,0},{10,2},{12,4},{14,6},{16,24},{18,... | collective-permute-start | bytes 393224 | tf_op jit(solution)/shard_map/ppermute | solution.py:771
  18.4 8.5 %copy-start.2 = (bf16[512,192]{1,0:T(8,128)(2,1)S(1)}, bf16[512,192]{1,0:T(8,128)(2,1)}, u32[]{:S(2)}) copy-start(bf16[512,192]{1,0:T(8,128)(2,1)} %constant.29.clone.refs_6_) | copy-start | bytes 589828
  18.4 8.5 %copy-start.4 = (f32[168,128]{1,0:T(8,128)S(1)}, f32[168,128]{1,0:T(8,128)}, u32[]{:S(2)}) copy-start(f32[168,128]{1,0:T(8,128)} %constant.34.clone.refs_11_) | copy-start | bytes 258052
  18.4 6.4 %collective-permute-start.3 = (f32[8,8,8,128]{3,2,1,0:T(8,128)S(1)}, f32[8,8,8,128]{3,2,1,0:T(8,128)S(1)}, u32[]{:S(2)}, u32[]{:S(2)}) collective-permute-start(f32[8,8,8,128]{3,2,1,0:T(8,128)S(1)} %pad_maximum_fusion), channel_id=1, source_target_pairs={{0,4},{2,6},{4,0},{6,2},{8,12},{10,14},{12,8},{14,10},{16,20},{18,... | collective-permute-start | bytes 786440 | tf_op jit(solution)/shard_map/ppermute | solution.py:771
  20.3 6.5 %copy-start.5 = (bf16[64,192]{1,0:T(8,128)(2,1)S(1)}, bf16[64,192]{1,0:T(8,128)(2,1)}, u32[]{:S(2)}) copy-start(bf16[64,192]{1,0:T(8,128)(2,1)} %constant.30.clone.refs_7_) | copy-start | bytes 73732
  20.3 6.5 %copy-start.7 = (bf16[16,192]{1,0:T(8,128)(2,1)S(1)}, bf16[16,192]{1,0:T(8,128)(2,1)}, u32[]{:S(2)}) copy-start(bf16[16,192]{1,0:T(8,128)(2,1)} %constant.31.clone.refs_8_) | copy-start | bytes 18436
  20.3 6.5 %copy-start.8 = (bf16[16,32]{1,0:T(8,128)(2,1)S(1)}, bf16[16,32]{1,0:T(8,128)(2,1)}, u32[]{:S(2)}) copy-start(bf16[16,32]{1,0:T(8,128)(2,1)} %constant.33.clone.refs_10_) | copy-start | bytes 3076
  20.3 6.5 %copy-start.3 = (bf16[128,512]{1,0:T(8,128)(2,1)S(1)}, bf16[128,512]{1,0:T(8,128)(2,1)}, u32[]{:S(2)}) copy-start(bf16[128,512]{1,0:T(8,128)(2,1)} %constant.28.clone.refs_5_) | copy-start | bytes 393220
  20.3 6.5 %copy-start = (bf16[256,768]{1,0:T(8,128)(2,1)S(1)}, bf16[256,768]{1,0:T(8,128)(2,1)}, u32[]{:S(2)}) copy-start(bf16[256,768]{1,0:T(8,128)(2,1)} %constant.26.clone.refs_3_) | copy-start | bytes 1179652
  20.4 6.5 %copy-start.1 = (bf16[256,768]{1,0:T(8,128)(2,1)S(1)}, bf16[256,768]{1,0:T(8,128)(2,1)}, u32[]{:S(2)}) copy-start(bf16[256,768]{1,0:T(8,128)(2,1)} %constant.27.clone.refs_4_) | copy-start | bytes 1179652
  24.8 2.1 %copy-start.6 = (bf16[64,32]{1,0:T(8,128)(2,1)S(1)}, bf16[64,32]{1,0:T(8,128)(2,1)}, u32[]{:S(2)}) copy-start(bf16[64,32]{1,0:T(8,128)(2,1)} %constant.32.clone.refs_9_) | copy-start | bytes 12292
  24.9 2.0 %collective-permute-start.4 = (f32[16,8,8,128]{3,2,1,0:T(8,128)S(1)}, f32[16,8,8,128]{3,2,1,0:T(8,128)S(1)}, u32[]{:S(2)}, u32[]{:S(2)}) collective-permute-start(f32[16,8,8,128]{3,2,1,0:T(8,128)S(1)} %constant_dynamic-update-slice_fusion.refs_1_), channel_id=1, source_target_pairs={{0,2},{2,0},{4,6},{6,4},{8,10},{10,8},{12,14},{14,12},{16,18},{18,... | collective-permute-start | bytes 1572872 | tf_op jit(solution)/shard_map/ppermute | solution.py:771

commit v3 on v2

--- a/solution.py
+++ b/solution.py
@@ -338,13 +338,13 @@
     return jnp.where(sub == 4, pltpu.roll(x, 5, 0), jnp.where(sub == 7, pltpu.roll(x, 3, 0), x))
 
 
-def kernel(nx, ny, tables, meta, near, far, even, odd, down0, up0, op1, down1, up1, op2, rows,
+def kernel(nx, ny, tables, near, far, even, odd, down0, up0, op1, down1, up1, op2, rows,
            sol_ref, res_ref, rel_ref, b_ref, r_ref, d_ref, v_ref, p_ref, z_ref, re_ref, ro_ref,
            be_ref, bo_ref, c_ref, lane_ref):
     groups = nx // SUBS
     tiles = ny * groups
     wide = tiles * LANES
-    own_x, own_y = meta[0], meta[1]
+    own_x, own_y = lax.axis_index("gx"), lax.axis_index("gy")
     sub = lax.broadcasted_iota(jnp.int32, (SUBS, LANES), 0)
     lane = lax.broadcasted_iota(jnp.int32, (SUBS, LANES), 1) % SUBS
     w = [float(x) for x in tables.weights[0]]
@@ -649,7 +649,7 @@
     def collect():
         z_ref[...] = z_ref[...] + d_ref[:, window]
 
-    def cycle(step, carry):
+    def cycle():
         collect()
         run(second_direction, True)
         collect()
@@ -665,9 +665,9 @@
         run(next_direction, True)
         collect()
         run(next_direction, True)
-        return carry
-
-    lax.fori_loop(0, 2, cycle, 0)
+
+    cycle()
+    cycle()
 
     zero = jnp.zeros((SUBS, wide), jnp.float32)
     bw, ww, bb = zero, zero, zero
@@ -704,7 +704,7 @@
         res_ref[i] = swap_rows(res, sub)
 
 
-def solve_all(nx, ny, meta, near, far, interpret=False):
+def solve_all(nx, ny, near, far):
     tables = Tables()
     wide = ny * nx // SUBS * LANES
     consts = [tables.even, tables.odd, tables.down0, tables.up0, tables.op1, tables.down1,
@@ -713,7 +713,7 @@
     field = pltpu.VMEM((512, wide), jnp.float32)
     return pl.pallas_call(
         lambda *refs: kernel(nx, ny, tables, *refs),
-        in_specs=[pl.BlockSpec(memory_space=pltpu.SMEM)] + [vmem] * 11,
+        in_specs=[vmem] * 11,
         out_specs=[vmem, vmem, pl.BlockSpec(memory_space=pltpu.SMEM)],
         out_shape=[
             jax.ShapeDtypeStruct(near.shape[1:], jnp.float32),
@@ -727,8 +727,7 @@
             pltpu.VMEM((1024, wide), jnp.bfloat16), pltpu.VMEM((152, wide), jnp.float32),
         ],
         name="solve_all",
-        interpret=interpret,
-    )(meta, *[pltpu.with_memory_space_constraint(x, pltpu.VMEM)
+    )(*[pltpu.with_memory_space_constraint(x, pltpu.VMEM)
              for x in (near, far, *[jnp.asarray(c) for c in consts])])
 
 
@@ -754,7 +753,7 @@
         pack_kernel,
         in_specs=[vmem] * 3,
         out_specs=vmem,
-        out_shape=jax.ShapeDtypeStruct((1, *forcing.shape), jnp.float32),
+        out_shape=pltpu.VMEM((1, *forcing.shape), jnp.float32),
         scratch_shapes=[pltpu.VMEM((SUBS, LANES), jnp.float32)],
         name="pack_block",
     )(forcing, kappa, sigma)
@@ -772,8 +771,7 @@
         if step > 1:
             block = jnp.concatenate([block, other], axis=0)
         step //= 2
-    meta = jnp.stack([lax.axis_index("gx"), lax.axis_index("gy")]).astype(jnp.int32)
-    sol, res, rel = solve_all(nx, ny, meta, block, other)
+    sol, res, rel = solve_all(nx, ny, block, other)
     return sol, res, rel.reshape(())
 
 

time: 48.2 us -> 40.3 us (0.84)
  Pallas kernels: 22.5 us -> 15.7 us
  other arithmetic: 1.44 us -> 0.03 us
    pallas_call x1, Pallas kernels: 21 us -> 14.8 us  [solve_all(): pl.pallas_call(lambda *refs: kernel(nx, ny, tables, *refs), in_specs=[vme...]
    concatenate x3, other arithmetic: 0.79 us -> 0.03 us  [gathered(): block = jnp.concatenate([block, other], axis=0)]
    another operation x1 -> x0, other arithmetic: 0.65 us -> none  [gathered(): jnp.stack([lax.axis_index('gx'), lax.axis_index('gy')]).astype(jnp.int32)]
    ppermute x4, waiting for transfers between devices: 11 us -> 11.6 us  [gathered(): other = lax.ppermute(block, 'gx', [(i, i ^ step) for i in range(nx)])]
    pallas_call x1, Pallas kernels: 1.47 us -> 0.86 us  [packed_block(): pl.pallas_call(pack_kernel, in_specs=[vmem] * 3, out_specs=vmem, out_shap...]
  transfers between devices with their start and end apart: 5 -> 5, of which waited for: 5 -> 5; matrix products, arithmetic and copies ran while one was open for 1% -> 0% of each run, Pallas kernels for 0% -> 0%
where the time goes in v3:
time: 40.3 us; the launch traced here: 40.2 us
  Pallas kernels  15.7 us (39%)
  waiting for transfers between devices  13.5 us (33%)
  starting transfers between devices  10.1 us (25%)
  between operations  0.76 us (2%)
    pallas_call x1, Pallas kernels, solve_all(): pl.pallas_call(lambda *refs: kernel(nx, ny, tables, *refs), in_specs=[vme...  14.8 us
    ppermute x4, waiting for transfers between devices, gathered(): other = lax.ppermute(block, 'gx', [(i, i ^ step) for i in range(nx)])  11.6 us
    ppermute x4, starting transfers between devices, gathered(): other = lax.ppermute(block, 'gx', [(i, i ^ step) for i in range(nx)])  7.08 us
    ppermute x1, starting transfers between devices, gathered(): other = lax.ppermute(block, 'gy', [(i, i ^ 1) for i in range(ny)])  3.01 us
    ppermute x1, waiting for transfers between devices, gathered(): other = lax.ppermute(block, 'gy', [(i, i ^ 1) for i in range(ny)])  1.89 us
    pallas_call x1, Pallas kernels, packed_block(): pl.pallas_call(pack_kernel, in_specs=[vmem] * 3, out_specs=vmem, out_shap...  0.86 us
  transfers between devices with their start and end apart: 5, of which 5 were waited for; matrix products, arithmetic and copies ran while one was open for 0% of the time, Pallas kernels for 0%

profile of v3, /device:TPU:0, one launch (start us, length us, event | category | flops | bytes accessed | tf_op | source)
XLA Modules:
  0.0 40.2 jit_solution(9610060126584697)
XLA Ops:
  0.6 0.9 %pack_block.1 = f32[1,8,8,128]{3,2,1,0:T(8,128)S(1)} custom-call(f32[8,8,128]{2,1,0:T(8,128)} %forcing.1, f32[1,1,16]{2,1,0:T(1,128)} %kappa.1, f32[1,1,16]{2,1,0:T(1,128)} %sigma.1), custom_call_target="tpu_custom_call" | custom-call | tf_op jit(solution)/shard_map/pack_block/pallas_call | solution.py:752
  1.5 3.0 %collective-permute-start = (f32[1,8,8,128]{3,2,1,0:T(8,128)S(1)}, f32[1,8,8,128]{3,2,1,0:T(8,128)S(1)}, u32[]{:S(2)}, u32[]{:S(2)}) collective-permute-start(f32[1,8,8,128]{3,2,1,0:T(8,128)S(1)} %pack_block.1), channel_id=1, source_target_pairs={{0,1},{1,0},{2,3},{3,2},{4,5},{5,4},{6,7},{7,6},{8,9},{9,8},{10,11... | collective-permute-start | bytes 98312 | tf_op jit(solution)/shard_map/ppermute | solution.py:766
  4.5 1.9 %collective-permute-done = f32[1,8,8,128]{3,2,1,0:T(8,128)S(1)} collective-permute-done((f32[1,8,8,128]{3,2,1,0:T(8,128)S(1)}, f32[1,8,8,128]{3,2,1,0:T(8,128)S(1)}, u32[]{:S(2)}, u32[]{:S(2)}) %collective-permute-start) | collective-permute-done | bytes 32800 | tf_op jit(solution)/shard_map/ppermute | solution.py:766
  6.4 3.1 %collective-permute-start.1 = (f32[2,8,8,128]{3,2,1,0:T(8,128)S(1)}, f32[2,8,8,128]{3,2,1,0:T(8,128)S(1)}, u32[]{:S(2)}, u32[]{:S(2)}) collective-permute-start(f32[2,8,8,128]{3,2,1,0:T(8,128)S(1)} %pad_maximum_fusion.2), channel_id=1, source_target_pairs={{0,16},{2,18},{4,20},{6,22},{8,24},{10,26},{12,28},{14,30},{16,0},... | collective-permute-start | bytes 196616 | tf_op jit(solution)/shard_map/ppermute | solution.py:770
  9.5 2.2 %collective-permute-done.1 = f32[2,8,8,128]{3,2,1,0:T(8,128)S(1)} collective-permute-done((f32[2,8,8,128]{3,2,1,0:T(8,128)S(1)}, f32[2,8,8,128]{3,2,1,0:T(8,128)S(1)}, u32[]{:S(2)}, u32[]{:S(2)}) %collective-permute-start.1) | collective-permute-done | bytes 65568 | tf_op jit(solution)/shard_map/ppermute | solution.py:770
  11.8 2.0 %collective-permute-start.2 = (f32[4,8,8,128]{3,2,1,0:T(8,128)S(1)}, f32[4,8,8,128]{3,2,1,0:T(8,128)S(1)}, u32[]{:S(2)}, u32[]{:S(2)}) collective-permute-start(f32[4,8,8,128]{3,2,1,0:T(8,128)S(1)} %pad_maximum_fusion.1), channel_id=1, source_target_pairs={{0,8},{2,10},{4,12},{6,14},{8,0},{10,2},{12,4},{14,6},{16,24},{18,... | collective-permute-start | bytes 393224 | tf_op jit(solution)/shard_map/ppermute | solution.py:770
  13.8 3.1 %collective-permute-done.2 = f32[4,8,8,128]{3,2,1,0:T(8,128)S(1)} collective-permute-done((f32[4,8,8,128]{3,2,1,0:T(8,128)S(1)}, f32[4,8,8,128]{3,2,1,0:T(8,128)S(1)}, u32[]{:S(2)}, u32[]{:S(2)}) %collective-permute-start.2) | collective-permute-done | bytes 131104 | tf_op jit(solution)/shard_map/ppermute | solution.py:770
  16.8 0.0 copy-start.2
  16.8 0.0 copy-start.4
  16.8 1.9 %collective-permute-start.3 = (f32[8,8,8,128]{3,2,1,0:T(8,128)S(1)}, f32[8,8,8,128]{3,2,1,0:T(8,128)S(1)}, u32[]{:S(2)}, u32[]{:S(2)}) collective-permute-start(f32[8,8,8,128]{3,2,1,0:T(8,128)S(1)} %pad_maximum_fusion), channel_id=1, source_target_pairs={{0,4},{2,6},{4,0},{6,2},{8,12},{10,14},{12,8},{14,10},{16,20},{18,... | collective-permute-start | bytes 786440 | tf_op jit(solution)/shard_map/ppermute | solution.py:770
  18.8 0.0 copy-start.5
  18.8 0.0 copy-start.6
  18.8 0.0 copy-start.7
  18.8 0.0 copy-start.8
  18.8 0.0 copy-start.3
  18.8 0.0 copy-start
  18.8 0.0 copy-start.1
  18.8 4.4 %collective-permute-done.3 = f32[8,8,8,128]{3,2,1,0:T(8,128)S(1)} collective-permute-done((f32[8,8,8,128]{3,2,1,0:T(8,128)S(1)}, f32[8,8,8,128]{3,2,1,0:T(8,128)S(1)}, u32[]{:S(2)}, u32[]{:S(2)}) %collective-permute-start.3) | collective-permute-done | bytes 262176 | tf_op jit(solution)/shard_map/ppermute | solution.py:770
  23.3 0.1 collective-permute-start.4
  23.4 1.9 %collective-permute-done.4.refs_1_ = f32[16,8,8,128]{3,2,1,0:T(8,128)S(1)} collective-permute-done((f32[16,8,8,128]{3,2,1,0:T(8,128)S(1)}, f32[16,8,8,128]{3,2,1,0:T(8,128)S(1)}, u32[]{:S(2)}, u32[]{:S(2)}) %collective-permute-start.4) | collective-permute-done | bytes 524320 | tf_op jit(solution)/shard_map/ppermute | solution.py:770
  25.3 0.0 copy-done.2
  25.3 0.0 copy-done.4
  25.3 0.0 copy-done.5
  25.3 0.0 copy-done.6
  25.3 0.0 copy-done.7
  25.3 0.0 copy-done.8
  25.3 0.0 copy-done.3
  25.3 0.0 copy-done
  25.3 0.0 copy-done.1
  25.3 14.8 %solve_all.1 = (f32[8,8,128]{2,1,0:T(8,128)}, f32[8,8,128]{2,1,0:T(8,128)}, f32[1]{0:T(128)}) custom-call(f32[16,8,8,128]{3,2,1,0:T(8,128)S(1)} %constant_dynamic-update-slice_fusion.refs_0_, f32[16,8,8,128]{3,2,1,0:T(8,128)S(1)} %collective-permute-done.4.refs_1_, bf16[256,768]{1,0:T(8,128)(2,1)S(1)} %copy-done, bf16[256,768]{1,0:T(8,128)(2,1)S(1)} %copy-done.1, ...), custom_call_target="tpu_custom_call" | custom-call | tf_op jit(solution)/shard_map/solve_all/pallas_call | solution.py:714
  (8 shorter events, 0.1 us)
Async XLA Ops:
  1.5 4.9 %collective-permute-start = (f32[1,8,8,128]{3,2,1,0:T(8,128)S(1)}, f32[1,8,8,128]{3,2,1,0:T(8,128)S(1)}, u32[]{:S(2)}, u32[]{:S(2)}) collective-permute-start(f32[1,8,8,128]{3,2,1,0:T(8,128)S(1)} %pack_block.1), channel_id=1, source_target_pairs={{0,1},{1,0},{2,3},{3,2},{4,5},{5,4},{6,7},{7,6},{8,9},{9,8},{10,11... | collective-permute-start | bytes 98312 | tf_op jit(solution)/shard_map/ppermute | solution.py:766
  6.4 5.4 %collective-permute-start.1 = (f32[2,8,8,128]{3,2,1,0:T(8,128)S(1)}, f32[2,8,8,128]{3,2,1,0:T(8,128)S(1)}, u32[]{:S(2)}, u32[]{:S(2)}) collective-permute-start(f32[2,8,8,128]{3,2,1,0:T(8,128)S(1)} %pad_maximum_fusion.2), channel_id=1, source_target_pairs={{0,16},{2,18},{4,20},{6,22},{8,24},{10,26},{12,28},{14,30},{16,0},... | collective-permute-start | bytes 196616 | tf_op jit(solution)/shard_map/ppermute | solution.py:770
  11.8 5.0 %collective-permute-start.2 = (f32[4,8,8,128]{3,2,1,0:T(8,128)S(1)}, f32[4,8,8,128]{3,2,1,0:T(8,128)S(1)}, u32[]{:S(2)}, u32[]{:S(2)}) collective-permute-start(f32[4,8,8,128]{3,2,1,0:T(8,128)S(1)} %pad_maximum_fusion.1), channel_id=1, source_target_pairs={{0,8},{2,10},{4,12},{6,14},{8,0},{10,2},{12,4},{14,6},{16,24},{18,... | collective-permute-start | bytes 393224 | tf_op jit(solution)/shard_map/ppermute | solution.py:770
  16.8 8.5 %copy-start.2 = (bf16[512,192]{1,0:T(8,128)(2,1)S(1)}, bf16[512,192]{1,0:T(8,128)(2,1)}, u32[]{:S(2)}) copy-start(bf16[512,192]{1,0:T(8,128)(2,1)} %constant.21.clone.refs_5_) | copy-start | bytes 589828
  16.8 8.5 %copy-start.4 = (f32[168,128]{1,0:T(8,128)S(1)}, f32[168,128]{1,0:T(8,128)}, u32[]{:S(2)}) copy-start(f32[168,128]{1,0:T(8,128)} %constant.26.clone.refs_10_) | copy-start | bytes 258052
  16.8 6.4 %collective-permute-start.3 = (f32[8,8,8,128]{3,2,1,0:T(8,128)S(1)}, f32[8,8,8,128]{3,2,1,0:T(8,128)S(1)}, u32[]{:S(2)}, u32[]{:S(2)}) collective-permute-start(f32[8,8,8,128]{3,2,1,0:T(8,128)S(1)} %pad_maximum_fusion), channel_id=1, source_target_pairs={{0,4},{2,6},{4,0},{6,2},{8,12},{10,14},{12,8},{14,10},{16,20},{18,... | collective-permute-start | bytes 786440 | tf_op jit(solution)/shard_map/ppermute | solution.py:770
  18.8 6.5 %copy-start.5 = (bf16[64,192]{1,0:T(8,128)(2,1)S(1)}, bf16[64,192]{1,0:T(8,128)(2,1)}, u32[]{:S(2)}) copy-start(bf16[64,192]{1,0:T(8,128)(2,1)} %constant.22.clone.refs_6_) | copy-start | bytes 73732
  18.8 6.5 %copy-start.6 = (bf16[64,32]{1,0:T(8,128)(2,1)S(1)}, bf16[64,32]{1,0:T(8,128)(2,1)}, u32[]{:S(2)}) copy-start(bf16[64,32]{1,0:T(8,128)(2,1)} %constant.24.clone.refs_8_) | copy-start | bytes 12292
  18.8 6.5 %copy-start.7 = (bf16[16,192]{1,0:T(8,128)(2,1)S(1)}, bf16[16,192]{1,0:T(8,128)(2,1)}, u32[]{:S(2)}) copy-start(bf16[16,192]{1,0:T(8,128)(2,1)} %constant.23.clone.refs_7_) | copy-start | bytes 18436
  18.8 6.5 %copy-start.8 = (bf16[16,32]{1,0:T(8,128)(2,1)S(1)}, bf16[16,32]{1,0:T(8,128)(2,1)}, u32[]{:S(2)}) copy-start(bf16[16,32]{1,0:T(8,128)(2,1)} %constant.25.clone.refs_9_) | copy-start | bytes 3076
  18.8 6.5 %copy-start.3 = (bf16[128,512]{1,0:T(8,128)(2,1)S(1)}, bf16[128,512]{1,0:T(8,128)(2,1)}, u32[]{:S(2)}) copy-start(bf16[128,512]{1,0:T(8,128)(2,1)} %constant.20.clone.refs_4_) | copy-start | bytes 393220
  18.8 6.5 %copy-start = (bf16[256,768]{1,0:T(8,128)(2,1)S(1)}, bf16[256,768]{1,0:T(8,128)(2,1)}, u32[]{:S(2)}) copy-start(bf16[256,768]{1,0:T(8,128)(2,1)} %constant.18.clone.refs_2_) | copy-start | bytes 1179652
  18.8 6.5 %copy-start.1 = (bf16[256,768]{1,0:T(8,128)(2,1)S(1)}, bf16[256,768]{1,0:T(8,128)(2,1)}, u32[]{:S(2)}) copy-start(bf16[256,768]{1,0:T(8,128)(2,1)} %constant.19.clone.refs_3_) | copy-start | bytes 1179652
  23.3 2.0 %collective-permute-start.4 = (f32[16,8,8,128]{3,2,1,0:T(8,128)S(1)}, f32[16,8,8,128]{3,2,1,0:T(8,128)S(1)}, u32[]{:S(2)}, u32[]{:S(2)}) collective-permute-start(f32[16,8,8,128]{3,2,1,0:T(8,128)S(1)} %constant_dynamic-update-slice_fusion.refs_0_), channel_id=1, source_target_pairs={{0,2},{2,0},{4,6},{6,4},{8,10},{10,8},{12,14},{14,12},{16,18},{18,... | collective-permute-start | bytes 1572872 | tf_op jit(solution)/shard_map/ppermute | solution.py:770

commit v4 on v3

--- a/solution.py
+++ b/solution.py
@@ -316,11 +316,16 @@
         self.odd = stacked(odd[np.ix_(rows0[:256], data0[:256])])
         high, low = split_const(triple(down[0], down[0], down[0])[np.ix_(rows1, data0)])
         self.down0 = np.concatenate([high, low], axis=0)
-        self.up0 = stacked(triple(interps[0], interps[0], interps[0])[np.ix_(rows0, rows1)])
+        up = triple(interps[0], interps[0], interps[0])
+        stiffness = np.kron(k, both) + np.kron(w, plane)
+        self.up0 = stacked(np.concatenate([up[np.ix_(rows0, rows1)], (stiffness @ up)[np.ix_(rows0, rows1)]]))
         w, k = np.diag(self.weights[1]), stiff[1]
-        self.op1 = stacked((triple(k, w, w) + triple(w, k, w) + triple(w, w, k))[np.ix_(rows1, rows1)])
+        stiffness = triple(k, w, w) + triple(w, k, w) + triple(w, w, k)
+        up = triple(interps[1], interps[1], interps[1])
+        self.op1 = stacked(stiffness[np.ix_(rows1, rows1)])
         self.down1 = padded(stacked(triple(down[1], down[1], down[1])[np.ix_(rows2, rows1)]), 16, 192)
-        self.up1 = padded(stacked(triple(interps[1], interps[1], interps[1])[np.ix_(rows1, rows2)]), 64, 32)
+        self.up1 = padded(stacked(
+            np.concatenate([up[np.ix_(rows1, rows2)], (stiffness @ up)[np.ix_(rows1, rows2)]])), 128, 32)
         w, k = np.diag(self.weights[2]), stiff[2]
         self.op2 = padded(
             stacked((triple(k, w, w) + triple(w, k, w) + triple(w, w, k))[np.ix_(rows2, rows2)]), 16, 32)
@@ -339,74 +344,73 @@
 
 
 def kernel(nx, ny, tables, near, far, even, odd, down0, up0, op1, down1, up1, op2, rows,
-           sol_ref, res_ref, rel_ref, b_ref, r_ref, d_ref, v_ref, p_ref, z_ref, re_ref, ro_ref,
+           sol_ref, res_ref, rel_ref, b_ref, r_ref, d_ref, v_ref, p_ref, t_ref, a_ref, z_ref,
            be_ref, bo_ref, c_ref, lane_ref):
     groups = nx // SUBS
     tiles = ny * groups
+    part_wide = ny * LANES
     wide = tiles * LANES
     own_x, own_y = lax.axis_index("gx"), lax.axis_index("gy")
     sub = lax.broadcasted_iota(jnp.int32, (SUBS, LANES), 0)
-    lane = lax.broadcasted_iota(jnp.int32, (SUBS, LANES), 1) % SUBS
+    lanes = lax.broadcasted_iota(jnp.int32, (SUBS, LANES), 1)
+    lane = lanes % SUBS
     w = [float(x) for x in tables.weights[0]]
     q = [float(x) for x in tables.squares[0]]
     f = [0.5 if k in (0, 7) else 1.0 for k in range(8)]
-
-    def cols(x):
-        return [x[:, t * LANES:(t + 1) * LANES] for t in range(tiles)]
-
-    def join(parts):
-        return jnp.concatenate(parts, axis=1)
-
-    def across(x):
-        return join([x] * tiles)
-
-    sub_w = across(sub)
-
-    def x_up(x, more=0):
-        parts, out = cols(x), []
-        for t in range(tiles):
-            if t % groups:
-                prev = parts[t - 1]
-                out.append(pltpu.roll(prev, more, 1) if more else prev)
-            else:
-                prev = parts[t + groups - 1]
-                out.append(jnp.where(lane == 0, pltpu.roll(prev, (LANES - SUBS + 1 + more) % LANES, 1),
-                                     pltpu.roll(prev, 1 + more, 1)))
-        return join(out)
-
-    def x_down(x, more=0):
-        parts, out = cols(x), []
-        for t in range(tiles):
-            if t % groups < groups - 1:
-                succ = parts[t + 1]
-                out.append(pltpu.roll(succ, more, 1) if more else succ)
-            else:
-                succ = parts[t - groups + 1]
-                out.append(jnp.where(lane == SUBS - 1, pltpu.roll(succ, SUBS - 1 + more, 1),
-                                     pltpu.roll(succ, (LANES - 1 + more) % LANES, 1)))
-        return join(out)
+    parts = range(groups)
+
+    def cut(x):
+        return [x[:, t * LANES:(t + 1) * LANES] for t in range(x.shape[1] // LANES)]
+
+    def join(pieces):
+        return jnp.concatenate(pieces, axis=1)
+
+    def ls(p):
+        return slice(p * part_wide, (p + 1) * part_wide)
+
+    def split_parts(x):
+        return [x[:, ls(p)] for p in parts]
+
+    def across(x, count):
+        return join([x] * count)
+
+    sub_w = across(sub, tiles)
+    sub_p = across(sub, ny)
+
+    def move(x, amount):
+        amount %= LANES
+        return join([pltpu.roll(t, amount, 1) for t in cut(x)]) if amount else x
+
+    def x_up(x, p, more=0):
+        if p:
+            return move(x[p - 1], more)
+        prev = cut(x[groups - 1])
+        return join([jnp.where(lane == 0, pltpu.roll(t, (LANES - SUBS + 1 + more) % LANES, 1),
+                               pltpu.roll(t, 1 + more, 1)) for t in prev])
+
+    def x_down(x, p, more=0):
+        if p < groups - 1:
+            return move(x[p + 1], more)
+        succ = cut(x[0])
+        return join([jnp.where(lane == SUBS - 1, pltpu.roll(t, SUBS - 1 + more, 1),
+                               pltpu.roll(t, (LANES - 1 + more) % LANES, 1)) for t in succ])
 
     up, down = SUBS, LANES - SUBS
 
-    def z_up(x):
-        return join([pltpu.roll(p, up, 1) for p in cols(x)])
-
-    def z_down(x):
-        return join([pltpu.roll(p, down, 1) for p in cols(x)])
-
     def y_fold(x, face):
-        parts = cols(x)
-        other = join([parts[(t + groups) % tiles] for t in range(tiles)])
+        t = cut(x)
+        other = join([t[(n // ny) * ny + (n + 1) % ny] for n in range(len(t))])
         return x + jnp.where(face, pltpu.roll(other, 4, 0), 0.0)
 
-    face0 = sub_w % 4 == 0
+    face0 = sub_p % 4 == 0
     face1 = sub_w % 2 == 0
 
     def row(k, i):
         return pl.ds(k * 64 + i * 8, 8)
 
     for t in range(tiles):
-        y_index, part = t // groups, t % groups
+        part, y_index = t // ny, t % ny
+        at = slice(t * LANES, (t + 1) * LANES)
         use_near = ((part ^ own_x) & 1) == 0
         slots = []
         for c in range(SUBS):
@@ -421,106 +425,145 @@
                 bit += 1
                 step //= 2
             slots.append(slot)
-        for i in range(8):
-            block = [jnp.where(use_near, near[slot, i], far[slot, i]) for slot in slots]
-            for step in (1, 2, 4):
-                out = list(block)
-                for c in range(SUBS):
-                    if not c & step:
-                        a, b = block[c], block[c + step]
-                        keep = (lane & step) == 0
-                        out[c] = jnp.where(keep, a, pltpu.roll(b, step, 1))
-                        out[c + step] = jnp.where(keep, pltpu.roll(a, LANES - step, 1), b)
-                block = out
+        blocks = [[jnp.where(use_near, near[slot, i], far[slot, i]) for slot in slots]
+                  for i in range(8)]
+        for step in (1, 2, 4):
+            keep = (lane & step) == 0
+            low = [c for c in range(SUBS) if not c & step]
+            turned = [[jnp.take_along_axis(jnp.where(keep, b[c + step], b[c]), lanes ^ step, axis=1)
+                       for c in low] for b in blocks]
+            fresh = []
+            for b, turn in zip(blocks, turned):
+                out = list(b)
+                for c, x in zip(low, turn):
+                    out[c] = jnp.where(keep, b[c], x)
+                    out[c + step] = jnp.where(keep, x, b[c + step])
+                fresh.append(out)
+            blocks = fresh
+        for i, b in enumerate(blocks):
             for k in range(7):
-                v_ref[row(k, i), t * LANES:(t + 1) * LANES] = block[k]
-            v_ref[row(7, i), t * LANES:(t + 1) * LANES] = pltpu.roll(block[0], LANES - SUBS, 1)
-            if i == 0:
-                lane_ref[0:8, t * LANES:(t + 1) * LANES] = block[7]
+                v_ref[row(k, i), at] = b[k]
+            v_ref[row(7, i), at] = pltpu.roll(b[0], down, 1)
+        lane_ref[0:8, at] = blocks[0][7]
     kap1 = lane_ref[0:1, :]
     sig1 = lane_ref[1:2, :]
-    kap = jnp.broadcast_to(kap1, (SUBS, wide))
-    sig = jnp.broadcast_to(sig1, (SUBS, wide))
-    w_j = across(rows[0:8, :])
-    q_j = across(rows[8:16, :])
-    f_j = across(rows[16:24, :])
-    sig_w = sig * w_j
-
-    def store_split(kk, index, low_pair, high_pair):
+    w_j = across(rows[0:8, :], ny)
+    q_j = across(rows[8:16, :], ny)
+    f_j = across(rows[16:24, :], tiles)
+    kap = [jnp.broadcast_to(kap1[:, ls(p)], (SUBS, part_wide)) for p in parts]
+    sig_w = [jnp.broadcast_to(sig1[:, ls(p)], (SUBS, part_wide)) * w_j for p in parts]
+
+    def split(value):
+        high = value.astype(jnp.bfloat16)
+        return high, (value - high.astype(jnp.float32)).astype(jnp.bfloat16)
+
+    def store_split(kk, index, p, low_pair, high_pair):
         a = jnp.concatenate(low_pair, axis=0)
         b = jnp.concatenate(high_pair, axis=0)
         for ref, value in ((be_ref, a + b), (bo_ref, a - b)):
-            high = value.astype(jnp.bfloat16)
-            low = (value - high.astype(jnp.float32)).astype(jnp.bfloat16)
+            high, low = split(value)
             at = kk * 64 + index * 16
-            ref[at:at + 16, :] = high
-            ref[256 + at:272 + at, :] = low
-            ref[512 + at:528 + at, :] = high
-
-    def fold_pairs(kk, get, index):
+            ref[at:at + 16, ls(p)] = high
+            ref[256 + at:272 + at, ls(p)] = low
+            ref[512 + at:528 + at, ls(p)] = high
+
+    def fold_z(kk, pair):
+        a, b = pair
+        return (a + move(b, up), b + move(a, down)) if kk == 0 else (a, b)
+
+    def inner(p, kk, index, get, with_z=True):
         out = []
         for i in PAIRS[index]:
-            a, b = get(kk, i), get(7 - kk, i)
-            out.append((a, b))
+            pair = get(p, kk, i)
+            pair = fold_z(kk, pair) if with_z else pair
+            out.append([y_fold(x, face0) for x in pair])
         return out
 
-    def assemble_pairs(kk, index, values, with_z=True):
-        vals = [list(v) for v in values]
-        if kk == 0 and with_z:
-            for v in vals:
-                a, b = v
-                v[0] = a + z_up(b)
-                v[1] = b + z_down(a)
-        if index == 0:
+    def faces(kk, get, with_z=True):
+        first, last = [], []
+        for p in parts:
+            a, b = get(p, kk, 0), get(p, kk, 7)
+            first.append(fold_z(kk, a) if with_z else a)
+            last.append(fold_z(kk, b) if with_z else b)
+        out = []
+        for p in parts:
+            a, b = [], []
             for s in range(2):
-                a, b = vals[0][s], vals[1][s]
-                vals[0][s] = a + x_up(b)
-                vals[1][s] = b + x_down(a)
-        return [[y_fold(x, face0) for x in v] for v in vals]
-
-    def point(k, i):
-        s1 = q[k] * w[i] + w[k] * q[i]
-        s2 = w[k] * w[i]
-        return kap * (s1 * w_j + s2 * q_j) + s2 * sig_w
-
-    for kk in range(4):
-        for index, pair in enumerate(PAIRS):
-            diag = assemble_pairs(kk, index, fold_pairs(kk, point, index))
-            load = assemble_pairs(
-                kk, index, fold_pairs(kk, lambda k, i: v_ref[row(k, i), :], index), with_z=False)
-            dirs = []
-            for s, k in enumerate((kk, 7 - kk)):
-                group = []
-                for n, i in enumerate(pair):
-                    inverse = 1.0 / diag[n][s]
-                    b_ref[row(k, i), :] = load[n][s]
-                    r_ref[row(k, i), :] = load[n][s]
-                    scaled = inverse * (1.0 / THETA)
-                    p_ref[row(k, i), :] = inverse * PUSH
-                    first = load[n][s] * scaled
-                    d_ref[row(k, i), :] = first
-                    group.append((first, scaled))
-                dirs.append([g[0] for g in group])
-                for n, i in enumerate(pair):
-                    v_ref[row(k, i), :] = group[n][1]
-            store_split(kk, index, dirs[0], dirs[1])
-
-    def tile_rows(x):
-        return jnp.concatenate([x] * tiles, axis=1)
+                firsts, lasts = [x[s] for x in first], [x[s] for x in last]
+                a.append(y_fold(firsts[p] + x_up(lasts, p), face0))
+                b.append(y_fold(lasts[p] + x_down(firsts, p), face0))
+            out.append([a, b])
+        return out
+
+    def walk(get, handle, after, with_z=True):
+        for p in parts:
+            for kk in range(4):
+                for index in (1, 2, 3):
+                    handle(p, kk, index, inner(p, kk, index, get, with_z))
+            if p == 0:
+                for kk in range(4):
+                    for n, values in enumerate(faces(kk, get, with_z)):
+                        handle(n, kk, 0, values)
+            after(p)
+
+    def dot(a, b):
+        return jnp.dot(a, b, preferred_element_type=jnp.float32)
+
+    def multiply(p):
+        a_ref[0:256, ls(p)] = dot(even[...], be_ref[:, ls(p)])
+        a_ref[256:512, ls(p)] = dot(odd[...], bo_ref[:, ls(p)])
+
+    def point(p, kk, i):
+        out = []
+        for k in (kk, 7 - kk):
+            s1 = q[k] * w[i] + w[k] * q[i]
+            s2 = w[k] * w[i]
+            out.append(kap[p] * (s1 * w_j + s2 * q_j) + s2 * sig_w[p])
+        return out
+
+    def put_diag(p, kk, index, values):
+        for s, k in enumerate((kk, 7 - kk)):
+            for n, i in enumerate(PAIRS[index]):
+                inverse = 1.0 / values[n][s]
+                p_ref[row(k, i), ls(p)] = inverse * PUSH
+                t_ref[row(k, i), ls(p)] = inverse * (1.0 / THETA)
+
+    def put_load(p, kk, index, values):
+        dirs = []
+        for s, k in enumerate((kk, 7 - kk)):
+            group = []
+            for n, i in enumerate(PAIRS[index]):
+                at = (row(k, i), ls(p))
+                b_ref[at] = values[n][s]
+                r_ref[at] = values[n][s]
+                group.append(values[n][s] * t_ref[at])
+                d_ref[at] = group[-1]
+            dirs.append(group)
+        store_split(kk, index, p, dirs[0], dirs[1])
+
+    walk(point, put_diag, lambda p: None)
+    walk(lambda p, kk, i: (v_ref[row(kk, i), ls(p)], v_ref[row(7 - kk, i), ls(p)]),
+         put_load, multiply, with_z=False)
 
     low_face = (sub_w // 2) % 2 == 0
 
+    def x_up_all(x, more=0):
+        return join([x_up(split_parts(x), p, more) for p in parts])
+
+    def x_down_all(x, more=0):
+        return join([x_down(split_parts(x), p, more) for p in parts])
+
     def fold1(x):
-        p = [(x[16 * k:16 * k + 8], x[16 * k + 8:16 * k + 16]) for k in range(4)]
+        c = [(x[16 * k:16 * k + 8], x[16 * k + 8:16 * k + 16]) for k in range(4)]
         out = []
-        for k, (a, b) in enumerate(p):
-            na, nb = x_up(b), x_down(a)
+        for k, (a, b) in enumerate(c):
+            na, nb = x_up_all(b), x_down_all(a)
             if k in (0, 3):
-                c, e = p[3 - k]
-                move, amount = (z_up, up) if k == 0 else (z_down, down)
-                na = na + x_up(e, amount)
-                nb = nb + x_down(c, amount)
-                a, b = a + move(c), b + move(e)
+                g, h = c[3 - k]
+                amount = up if k == 0 else down
+                na = na + x_up_all(h, amount)
+                nb = nb + x_down_all(g, amount)
+                a, b = a + move(g, amount), b + move(h, amount)
             out.append(y_fold(a + jnp.where(low_face, na, 0.0), face1))
             out.append(y_fold(b + jnp.where(low_face, nb, 0.0), face1))
         return jnp.concatenate(out, axis=0)
@@ -532,33 +575,28 @@
         other_k = jnp.where(first_k, pltpu.roll(x, 6, 0), pltpu.roll(x, 2, 0))
         other_i = jnp.where(first_i, pltpu.roll(x, 7, 0), pltpu.roll(x, 1, 0))
         both = jnp.where(first_i, pltpu.roll(other_k, 7, 0), pltpu.roll(other_k, 1, 0))
-        x = x + jnp.where(first_k, z_up(other_k), z_down(other_k))
-        x = x + jnp.where(first_i, x_up(other_i), x_down(other_i))
-        x = x + jnp.where(first_k, jnp.where(first_i, x_up(both, up), x_down(both, up)),
-                          jnp.where(first_i, x_up(both, down), x_down(both, down)))
+        x = x + jnp.where(first_k, move(other_k, up), move(other_k, down))
+        x = x + jnp.where(first_i, x_up_all(other_i), x_down_all(other_i))
+        x = x + jnp.where(first_k, jnp.where(first_i, x_up_all(both, up), x_down_all(both, up)),
+                          jnp.where(first_i, x_up_all(both, down), x_down_all(both, down)))
         return y_fold(x, sub_w >= 0)
 
     def cat3(x):
-        high = x.astype(jnp.bfloat16)
-        low = (x - high.astype(jnp.float32)).astype(jnp.bfloat16)
+        high, low = split(x)
         return jnp.concatenate([high, low, high], axis=0)
 
     def cat3_small(x):
         high = x.astype(jnp.bfloat16).astype(jnp.float32)
         return jnp.concatenate([high, x - high, high, jnp.zeros_like(x)], axis=0).astype(jnp.bfloat16)
 
-    def dot(a, b):
-        return jnp.dot(a, b, preferred_element_type=jnp.float32)
-
-    mass1 = tile_rows(rows[24:88, :])
-    point1 = tile_rows(rows[88:152, :])
-    mass2 = tile_rows(rows[152:160, :])
-    point2 = tile_rows(rows[160:168, :])
+    mass1 = across(rows[24:88, :], tiles)
+    point1 = across(rows[88:152, :], tiles)
+    mass2 = across(rows[152:160, :], tiles)
+    point2 = across(rows[160:168, :], tiles)
     inv1_ref, mass1_ref = lane_ref.at[8:72, :], lane_ref.at[72:136, :]
     inv1_ref[...] = 1.0 / fold1(kap1 * point1 + sig1 * mass1)
     mass1_ref[...] = sig1 * mass1
-    inv2 = 1.0 / fold2(kap1 * point2 + sig1 * mass2)
-    lane_ref[136:144, :] = inv2
+    lane_ref[136:144, :] = 1.0 / fold2(kap1 * point2 + sig1 * mass2)
     lane_ref[144:152, :] = sig1 * mass2
 
     def apply1(v):
@@ -581,93 +619,90 @@
         y = d
         low = low - apply2(d)
         y = y + KEEP * d + PUSH * (low * inverse2)
-        e = dot(up1[...], cat3_small(y))
+        both = dot(up1[...], cat3_small(y))
+        e = both[0:64]
         x = x + e
-        resid = resid - apply1(e)
+        resid = resid - fold1(kap1 * both[64:128] + mass1_ref[...] * e)
         return x + resid * inverse * (1.0 / THETA)
 
-    def multiply():
-        re_ref[...] = dot(even[...], be_ref[...])
-        ro_ref[...] = dot(odd[...], bo_ref[...])
-
-    def image(kk, index):
-        values = []
-        for i in PAIRS[index]:
-            e = re_ref[row(kk, i), :]
-            o = ro_ref[row(kk, i), :]
-            scale = sig_w * (w[kk] * w[i])
-            values.append((kap * (e + o) + scale * d_ref[row(kk, i), :],
-                           kap * (e - o) + scale * d_ref[row(7 - kk, i), :]))
-        return assemble_pairs(kk, index, values)
-
-    def sweep(update):
-        multiply()
-        for kk in range(4):
-            for index, pair in enumerate(PAIRS):
-                out = image(kk, index)
-                dirs = []
-                for s, k in enumerate((kk, 7 - kk)):
-                    dirs.append([update(k, i, out[n][s]) for n, i in enumerate(pair)])
-                yield kk, index, dirs
-
-    def second_direction(k, i, value):
-        r = r_ref[row(k, i), :] - value
-        r_ref[row(k, i), :] = r
-        first = d_ref[row(k, i), :]
-        return KEEP * first + r * p_ref[row(k, i), :]
-
-    def residual_only(k, i, value):
-        r = r_ref[row(k, i), :] - value
-        r_ref[row(k, i), :] = r
+    def weighted(p, kk, i, a, b):
+        scale = sig_w[p] * (w[kk] * w[i])
+        return (kap[p] * a + scale * d_ref[row(kk, i), ls(p)],
+                kap[p] * b + scale * d_ref[row(7 - kk, i), ls(p)])
+
+    def from_halves(p, kk, i):
+        e = a_ref[row(kk, i), ls(p)]
+        o = a_ref[row(4 + kk, i), ls(p)]
+        return weighted(p, kk, i, e + o, e - o)
+
+    def from_whole(p, kk, i):
+        return weighted(p, kk, i, a_ref[row(kk, i), ls(p)], a_ref[row(7 - kk, i), ls(p)])
+
+    def lower(at, value):
+        r = r_ref[at] - value
+        r_ref[at] = r
         return r
 
-    def next_direction(k, i, value):
-        r = r_ref[row(k, i), :] - value
-        r_ref[row(k, i), :] = r
-        return r * v_ref[row(k, i), :]
-
-    def run(update, keep):
-        for kk, index, dirs in sweep(update):
-            if keep:
-                for s, k in enumerate((kk, 7 - kk)):
-                    for n, i in enumerate(PAIRS[index]):
-                        d_ref[row(k, i), :] = dirs[s][n]
-                store_split(kk, index, dirs[0], dirs[1])
-            else:
-                for s, k in enumerate((kk, 7 - kk)):
-                    value = jnp.concatenate(dirs[s], axis=0)
-                    high = value.astype(jnp.bfloat16)
-                    low = (value - high.astype(jnp.float32)).astype(jnp.bfloat16)
-                    at = k * 64 + index * 16
-                    c_ref[at:at + 16, :] = high
-                    c_ref[512 + at:528 + at, :] = low
-
-    start = pl.multiple_of((own_y * groups + own_x % groups) * LANES, LANES)
-    window = pl.ds(start, LANES)
+    def second_direction(at, value):
+        return KEEP * d_ref[at] + lower(at, value) * p_ref[at]
+
+    def next_direction(at, value):
+        return lower(at, value) * t_ref[at]
+
+    def put(update):
+        def handle(p, kk, index, values):
+            dirs = []
+            for s, k in enumerate((kk, 7 - kk)):
+                group = []
+                for n, i in enumerate(PAIRS[index]):
+                    at = (row(k, i), ls(p))
+                    group.append(update(at, values[n][s]))
+                    d_ref[at] = group[-1]
+                dirs.append(group)
+            store_split(kk, index, p, dirs[0], dirs[1])
+        return handle
+
+    def put_resid(p, kk, index, values):
+        for s, k in enumerate((kk, 7 - kk)):
+            pair = [lower((row(k, i), ls(p)), values[n][s]) for n, i in enumerate(PAIRS[index])]
+            high, low = split(jnp.concatenate(pair, axis=0))
+            at = k * 64 + index * 16
+            c_ref[at:at + 16, ls(p)] = high
+            c_ref[512 + at:528 + at, ls(p)] = low
+
+    def put_last(p, kk, index, values):
+        for s, k in enumerate((kk, 7 - kk)):
+            for n, i in enumerate(PAIRS[index]):
+                lower((row(k, i), ls(p)), values[n][s])
+
+    window = pl.ds(pl.multiple_of((own_x % groups * ny + own_y) * LANES, LANES), LANES)
     z_ref[...] = jnp.zeros((512, LANES), jnp.float32)
 
     def collect():
         z_ref[...] = z_ref[...] + d_ref[:, window]
 
-    def cycle():
+    for step in range(2):
         collect()
-        run(second_direction, True)
+        walk(from_halves, put(second_direction), multiply)
         collect()
-        run(residual_only, False)
-        both = dot(down0[...], c_ref[0:512, :])
-        low = both[0:64] + both[64:128] + dot(down0[0:64, :], c_ref[512:1024, :])
-        correction = coarse(fold1(low))
-        d_ref[...] = dot(up0[...], cat3(correction))
+        low = {}
+
+        def reduce(p):
+            both = dot(down0[...], c_ref[0:512, ls(p)])
+            low[p] = both[0:64] + both[64:128] + dot(down0[0:64, :], c_ref[512:1024, ls(p)])
+
+        walk(from_halves, put_resid, reduce)
+        correction = cat3(coarse(fold1(join([low[p] for p in parts]))))
+        for p in parts:
+            d_ref[:, ls(p)] = dot(up0[0:512, :], correction[:, ls(p)])
+            a_ref[:, ls(p)] = dot(up0[512:1024, :], correction[:, ls(p)])
         collect()
-        for kk in range(4):
-            for index, pair in enumerate(PAIRS):
-                store_split(kk, index, *[[d_ref[row(k, i), :] for i in pair] for k in (kk, 7 - kk)])
-        run(next_direction, True)
+        walk(from_whole, put(next_direction), multiply)
         collect()
-        run(next_direction, True)
-
-    cycle()
-    cycle()
+        if step == 0:
+            walk(from_halves, put(next_direction), multiply)
+        else:
+            walk(from_halves, put_last, lambda p: None)
 
     zero = jnp.zeros((SUBS, wide), jnp.float32)
     bw, ww, bb = zero, zero, zero
@@ -695,10 +730,9 @@
         res = sol
         for k in range(8):
             b = b_ref[row(k, i), window]
-            z = z_ref[row(k, i), :]
             r = b - coef * (b - r_ref[row(k, i), window])
             turn = (k - place) % LANES
-            sol = jnp.where(lane == k, pltpu.roll(z, turn, 1), sol)
+            sol = jnp.where(lane == k, pltpu.roll(z_ref[row(k, i), :], turn, 1), sol)
             res = jnp.where(lane == k, pltpu.roll(r, turn, 1), res)
         sol_ref[i] = swap_rows(coef * sol, sub)
         res_ref[i] = swap_rows(res, sub)
@@ -721,8 +755,8 @@
             jax.ShapeDtypeStruct((1,), jnp.float32),
         ],
         scratch_shapes=[
-            field, field, field, field, field, pltpu.VMEM((512, LANES), jnp.float32),
-            pltpu.VMEM((256, wide), jnp.float32), pltpu.VMEM((256, wide), jnp.float32),
+            field, field, field, field, field, field, field,
+            pltpu.VMEM((512, LANES), jnp.float32),
             pltpu.VMEM((768, wide), jnp.bfloat16), pltpu.VMEM((768, wide), jnp.bfloat16),
             pltpu.VMEM((1024, wide), jnp.bfloat16), pltpu.VMEM((152, wide), jnp.float32),
         ],

time: 40.3 us -> 38 us (0.943)
  Pallas kernels: 15.7 us -> 13.3 us
    pallas_call x1, Pallas kernels: 14.8 us -> 12.5 us  [solve_all(): pl.pallas_call(lambda *refs: kernel(nx, ny, tables, *refs), in_specs=[vme...]
where the time goes in v4:
time: 38 us; the launch traced here: 37.8 us
  waiting for transfers between devices  13.5 us (36%)
  Pallas kernels  13.3 us (35%)
  starting transfers between devices  10.1 us (27%)
  between operations  0.76 us (2%)
    pallas_call x1, Pallas kernels, solve_all(): pl.pallas_call(lambda *refs: kernel(nx, ny, tables, *refs), in_specs=[vme...  12.5 us
    ppermute x4, waiting for transfers between devices, gathered(): other = lax.ppermute(block, 'gx', [(i, i ^ step) for i in range(nx)])  11.6 us
    ppermute x4, starting transfers between devices, gathered(): other = lax.ppermute(block, 'gx', [(i, i ^ step) for i in range(nx)])  7.08 us
    ppermute x1, starting transfers between devices, gathered(): other = lax.ppermute(block, 'gy', [(i, i ^ 1) for i in range(ny)])  3.01 us
    ppermute x1, waiting for transfers between devices, gathered(): other = lax.ppermute(block, 'gy', [(i, i ^ 1) for i in range(ny)])  1.89 us
    pallas_call x1, Pallas kernels, packed_block(): pl.pallas_call(pack_kernel, in_specs=[vmem] * 3, out_specs=vmem, out_shap...  0.86 us
  transfers between devices with their start and end apart: 5, of which 5 were waited for; matrix products, arithmetic and copies ran while one was open for 0% of the time, Pallas kernels for 0%

profile of v4, /device:TPU:0, one launch (start us, length us, event | category | flops | bytes accessed | tf_op | source)
XLA Modules:
  0.0 37.8 jit_solution(17633772243931363574)
XLA Ops:
  0.6 0.9 %pack_block.1 = f32[1,8,8,128]{3,2,1,0:T(8,128)S(1)} custom-call(f32[8,8,128]{2,1,0:T(8,128)} %forcing.1, f32[1,1,16]{2,1,0:T(1,128)} %kappa.1, f32[1,1,16]{2,1,0:T(1,128)} %sigma.1), custom_call_target="tpu_custom_call" | custom-call | tf_op jit(solution)/shard_map/pack_block/pallas_call | solution.py:786
  1.5 3.0 %collective-permute-start = (f32[1,8,8,128]{3,2,1,0:T(8,128)S(1)}, f32[1,8,8,128]{3,2,1,0:T(8,128)S(1)}, u32[]{:S(2)}, u32[]{:S(2)}) collective-permute-start(f32[1,8,8,128]{3,2,1,0:T(8,128)S(1)} %pack_block.1), channel_id=1, source_target_pairs={{0,1},{1,0},{2,3},{3,2},{4,5},{5,4},{6,7},{7,6},{8,9},{9,8},{10,11... | collective-permute-start | bytes 98312 | tf_op jit(solution)/shard_map/ppermute | solution.py:800
  4.5 1.9 %collective-permute-done = f32[1,8,8,128]{3,2,1,0:T(8,128)S(1)} collective-permute-done((f32[1,8,8,128]{3,2,1,0:T(8,128)S(1)}, f32[1,8,8,128]{3,2,1,0:T(8,128)S(1)}, u32[]{:S(2)}, u32[]{:S(2)}) %collective-permute-start) | collective-permute-done | bytes 32800 | tf_op jit(solution)/shard_map/ppermute | solution.py:800
  6.4 3.1 %collective-permute-start.1 = (f32[2,8,8,128]{3,2,1,0:T(8,128)S(1)}, f32[2,8,8,128]{3,2,1,0:T(8,128)S(1)}, u32[]{:S(2)}, u32[]{:S(2)}) collective-permute-start(f32[2,8,8,128]{3,2,1,0:T(8,128)S(1)} %pad_maximum_fusion.2), channel_id=1, source_target_pairs={{0,16},{2,18},{4,20},{6,22},{8,24},{10,26},{12,28},{14,30},{16,0},... | collective-permute-start | bytes 196616 | tf_op jit(solution)/shard_map/ppermute | solution.py:804
  9.5 2.2 %collective-permute-done.1 = f32[2,8,8,128]{3,2,1,0:T(8,128)S(1)} collective-permute-done((f32[2,8,8,128]{3,2,1,0:T(8,128)S(1)}, f32[2,8,8,128]{3,2,1,0:T(8,128)S(1)}, u32[]{:S(2)}, u32[]{:S(2)}) %collective-permute-start.1) | collective-permute-done | bytes 65568 | tf_op jit(solution)/shard_map/ppermute | solution.py:804
  11.8 0.0 copy-start.6
  11.8 2.0 %collective-permute-start.2 = (f32[4,8,8,128]{3,2,1,0:T(8,128)S(1)}, f32[4,8,8,128]{3,2,1,0:T(8,128)S(1)}, u32[]{:S(2)}, u32[]{:S(2)}) collective-permute-start(f32[4,8,8,128]{3,2,1,0:T(8,128)S(1)} %pad_maximum_fusion.1), channel_id=1, source_target_pairs={{0,8},{2,10},{4,12},{6,14},{8,0},{10,2},{12,4},{14,6},{16,24},{18,... | collective-permute-start | bytes 393224 | tf_op jit(solution)/shard_map/ppermute | solution.py:804
  13.8 0.0 copy-start.4
  13.8 3.1 %collective-permute-done.2 = f32[4,8,8,128]{3,2,1,0:T(8,128)S(1)} collective-permute-done((f32[4,8,8,128]{3,2,1,0:T(8,128)S(1)}, f32[4,8,8,128]{3,2,1,0:T(8,128)S(1)}, u32[]{:S(2)}, u32[]{:S(2)}) %collective-permute-start.2) | collective-permute-done | bytes 131104 | tf_op jit(solution)/shard_map/ppermute | solution.py:804
  16.8 0.0 copy-start.2
  16.8 0.0 copy-start.3
  16.8 0.0 copy-start
  16.8 1.9 %collective-permute-start.3 = (f32[8,8,8,128]{3,2,1,0:T(8,128)S(1)}, f32[8,8,8,128]{3,2,1,0:T(8,128)S(1)}, u32[]{:S(2)}, u32[]{:S(2)}) collective-permute-start(f32[8,8,8,128]{3,2,1,0:T(8,128)S(1)} %pad_maximum_fusion), channel_id=1, source_target_pairs={{0,4},{2,6},{4,0},{6,2},{8,12},{10,14},{12,8},{14,10},{16,20},{18,... | collective-permute-start | bytes 786440 | tf_op jit(solution)/shard_map/ppermute | solution.py:804
  18.8 0.0 copy-start.1
  18.8 0.0 copy-start.5
  18.8 0.0 copy-start.7
  18.8 0.0 copy-start.8
  18.9 4.4 %collective-permute-done.3 = f32[8,8,8,128]{3,2,1,0:T(8,128)S(1)} collective-permute-done((f32[8,8,8,128]{3,2,1,0:T(8,128)S(1)}, f32[8,8,8,128]{3,2,1,0:T(8,128)S(1)}, u32[]{:S(2)}, u32[]{:S(2)}) %collective-permute-start.3) | collective-permute-done | bytes 262176 | tf_op jit(solution)/shard_map/ppermute | solution.py:804
  23.3 0.1 collective-permute-start.4
  23.4 1.9 %collective-permute-done.4.refs_1_ = f32[16,8,8,128]{3,2,1,0:T(8,128)S(1)} collective-permute-done((f32[16,8,8,128]{3,2,1,0:T(8,128)S(1)}, f32[16,8,8,128]{3,2,1,0:T(8,128)S(1)}, u32[]{:S(2)}, u32[]{:S(2)}) %collective-permute-start.4) | collective-permute-done | bytes 524320 | tf_op jit(solution)/shard_map/ppermute | solution.py:804
  25.3 0.0 copy-done.6
  25.3 0.0 copy-done.4
  25.3 0.0 copy-done.2
  25.3 0.0 copy-done.3
  25.3 0.0 copy-done
  25.3 0.0 copy-done.1
  25.3 0.0 copy-done.5
  25.3 0.0 copy-done.7
  25.3 0.0 copy-done.8
  25.4 12.5 %solve_all.1 = (f32[8,8,128]{2,1,0:T(8,128)}, f32[8,8,128]{2,1,0:T(8,128)}, f32[1]{0:T(128)}) custom-call(f32[16,8,8,128]{3,2,1,0:T(8,128)S(1)} %constant_dynamic-update-slice_fusion.refs_0_, f32[16,8,8,128]{3,2,1,0:T(8,128)S(1)} %collective-permute-done.4.refs_1_, bf16[256,768]{1,0:T(8,128)(2,1)S(1)} %copy-done.1, bf16[256,768]{1,0:T(8,128)(2,1)S(1)} %copy-done.2, ...), custom_call_target="tpu_custom_call" | custom-call | tf_op jit(solution)/shard_map/solve_all/pallas_call | solution.py:748
  (8 shorter events, 0.1 us)
Async XLA Ops:
  1.5 4.9 %collective-permute-start = (f32[1,8,8,128]{3,2,1,0:T(8,128)S(1)}, f32[1,8,8,128]{3,2,1,0:T(8,128)S(1)}, u32[]{:S(2)}, u32[]{:S(2)}) collective-permute-start(f32[1,8,8,128]{3,2,1,0:T(8,128)S(1)} %pack_block.1), channel_id=1, source_target_pairs={{0,1},{1,0},{2,3},{3,2},{4,5},{5,4},{6,7},{7,6},{8,9},{9,8},{10,11... | collective-permute-start | bytes 98312 | tf_op jit(solution)/shard_map/ppermute | solution.py:800
  6.4 5.4 %collective-permute-start.1 = (f32[2,8,8,128]{3,2,1,0:T(8,128)S(1)}, f32[2,8,8,128]{3,2,1,0:T(8,128)S(1)}, u32[]{:S(2)}, u32[]{:S(2)}) collective-permute-start(f32[2,8,8,128]{3,2,1,0:T(8,128)S(1)} %pad_maximum_fusion.2), channel_id=1, source_target_pairs={{0,16},{2,18},{4,20},{6,22},{8,24},{10,26},{12,28},{14,30},{16,0},... | collective-permute-start | bytes 196616 | tf_op jit(solution)/shard_map/ppermute | solution.py:804
  11.8 13.5 %copy-start.6 = (bf16[128,32]{1,0:T(8,128)(2,1)S(1)}, bf16[128,32]{1,0:T(8,128)(2,1)}, u32[]{:S(2)}) copy-start(bf16[128,32]{1,0:T(8,128)(2,1)} %constant.24.clone.refs_8_) | copy-start | bytes 24580
  11.8 5.0 %collective-permute-start.2 = (f32[4,8,8,128]{3,2,1,0:T(8,128)S(1)}, f32[4,8,8,128]{3,2,1,0:T(8,128)S(1)}, u32[]{:S(2)}, u32[]{:S(2)}) collective-permute-start(f32[4,8,8,128]{3,2,1,0:T(8,128)S(1)} %pad_maximum_fusion.1), channel_id=1, source_target_pairs={{0,8},{2,10},{4,12},{6,14},{8,0},{10,2},{12,4},{14,6},{16,24},{18,... | collective-permute-start | bytes 393224 | tf_op jit(solution)/shard_map/ppermute | solution.py:804
  13.8 11.5 %copy-start.4 = (f32[168,128]{1,0:T(8,128)S(1)}, f32[168,128]{1,0:T(8,128)}, u32[]{:S(2)}) copy-start(f32[168,128]{1,0:T(8,128)} %constant.26.clone.refs_10_) | copy-start | bytes 258052
  16.8 8.5 %copy-start.2 = (bf16[256,768]{1,0:T(8,128)(2,1)S(1)}, bf16[256,768]{1,0:T(8,128)(2,1)}, u32[]{:S(2)}) copy-start(bf16[256,768]{1,0:T(8,128)(2,1)} %constant.19.clone.refs_3_) | copy-start | bytes 1179652
  16.8 8.5 %copy-start.3 = (bf16[128,512]{1,0:T(8,128)(2,1)S(1)}, bf16[128,512]{1,0:T(8,128)(2,1)}, u32[]{:S(2)}) copy-start(bf16[128,512]{1,0:T(8,128)(2,1)} %constant.20.clone.refs_4_) | copy-start | bytes 393220
  16.8 8.5 %copy-start = (bf16[1024,192]{1,0:T(8,128)(2,1)S(1)}, bf16[1024,192]{1,0:T(8,128)(2,1)}, u32[]{:S(2)}) copy-start(bf16[1024,192]{1,0:T(8,128)(2,1)} %constant.21.clone.refs_5_) | copy-start | bytes 1179652
  16.8 6.4 %collective-permute-start.3 = (f32[8,8,8,128]{3,2,1,0:T(8,128)S(1)}, f32[8,8,8,128]{3,2,1,0:T(8,128)S(1)}, u32[]{:S(2)}, u32[]{:S(2)}) collective-permute-start(f32[8,8,8,128]{3,2,1,0:T(8,128)S(1)} %pad_maximum_fusion), channel_id=1, source_target_pairs={{0,4},{2,6},{4,0},{6,2},{8,12},{10,14},{12,8},{14,10},{16,20},{18,... | collective-permute-start | bytes 786440 | tf_op jit(solution)/shard_map/ppermute | solution.py:804
  18.8 6.5 %copy-start.1 = (bf16[256,768]{1,0:T(8,128)(2,1)S(1)}, bf16[256,768]{1,0:T(8,128)(2,1)}, u32[]{:S(2)}) copy-start(bf16[256,768]{1,0:T(8,128)(2,1)} %constant.18.clone.refs_2_) | copy-start | bytes 1179652
  18.8 6.5 %copy-start.5 = (bf16[64,192]{1,0:T(8,128)(2,1)S(1)}, bf16[64,192]{1,0:T(8,128)(2,1)}, u32[]{:S(2)}) copy-start(bf16[64,192]{1,0:T(8,128)(2,1)} %constant.22.clone.refs_6_) | copy-start | bytes 73732
  18.8 6.5 %copy-start.7 = (bf16[16,192]{1,0:T(8,128)(2,1)S(1)}, bf16[16,192]{1,0:T(8,128)(2,1)}, u32[]{:S(2)}) copy-start(bf16[16,192]{1,0:T(8,128)(2,1)} %constant.23.clone.refs_7_) | copy-start | bytes 18436
  18.8 6.5 %copy-start.8 = (bf16[16,32]{1,0:T(8,128)(2,1)S(1)}, bf16[16,32]{1,0:T(8,128)(2,1)}, u32[]{:S(2)}) copy-start(bf16[16,32]{1,0:T(8,128)(2,1)} %constant.25.clone.refs_9_) | copy-start | bytes 3076
  23.3 2.0 %collective-permute-start.4 = (f32[16,8,8,128]{3,2,1,0:T(8,128)S(1)}, f32[16,8,8,128]{3,2,1,0:T(8,128)S(1)}, u32[]{:S(2)}, u32[]{:S(2)}) collective-permute-start(f32[16,8,8,128]{3,2,1,0:T(8,128)S(1)} %constant_dynamic-update-slice_fusion.refs_0_), channel_id=1, source_target_pairs={{0,2},{2,0},{4,6},{6,4},{8,10},{10,8},{12,14},{14,12},{16,18},{18,... | collective-permute-start | bytes 1572872 | tf_op jit(solution)/shard_map/ppermute | solution.py:804

commit v5 on v4

--- a/solution.py
+++ b/solution.py
@@ -279,6 +279,7 @@
 
 
 J_ORDER = (0, 1, 2, 3, 7, 5, 6, 4)
+SPLIT_AT = ((0, 1), (2, 1))
 PAIRS = ((0, 7), (1, 2), (3, 4), (5, 6))
 FACE = (0, 1, 3, 2)
 ROWS1 = tuple(
@@ -327,8 +328,7 @@
         self.up1 = padded(stacked(
             np.concatenate([up[np.ix_(rows1, rows2)], (stiffness @ up)[np.ix_(rows1, rows2)]])), 128, 32)
         w, k = np.diag(self.weights[2]), stiff[2]
-        self.op2 = padded(
-            stacked((triple(k, w, w) + triple(w, k, w) + triple(w, w, k))[np.ix_(rows2, rows2)]), 16, 32)
+        op2 = (triple(k, w, w) + triple(w, k, w) + triple(w, w, k))[np.ix_(rows2, rows2)]
         wide = lambda column: np.repeat(np.asarray(column, np.float32)[:, None], LANES, axis=1)
         blocks = [wide(self.weights[0][list(J_ORDER)]), wide(self.squares[0][list(J_ORDER)]),
                   wide(factor[0][list(J_ORDER)])]
@@ -336,6 +336,8 @@
             a, b = self.weights[level], self.squares[level]
             blocks.append(wide(triple(a, a, a)[order]))
             blocks.append(wide((triple(b, a, a) + triple(a, b, a) + triple(a, a, b))[order]))
+        at = np.arange(SUBS)
+        self.op2 = np.concatenate([wide(op2[at, (at - turn) % SUBS]) for turn in range(SUBS)], axis=0)
         self.rows = np.concatenate(blocks, axis=0)
 
 
@@ -344,8 +346,8 @@
 
 
 def kernel(nx, ny, tables, near, far, even, odd, down0, up0, op1, down1, up1, op2, rows,
-           sol_ref, res_ref, rel_ref, b_ref, r_ref, d_ref, v_ref, p_ref, t_ref, a_ref, z_ref,
-           be_ref, bo_ref, c_ref, lane_ref):
+           sol_ref, res_ref, rel_ref, b_ref, r_ref, d_ref, other_ref, v_ref, p_ref, t_ref, a_ref, z_ref,
+           be_ref, bo_ref, c_ref, lane_ref, low_ref, cor_ref):
     groups = nx // SUBS
     tiles = ny * groups
     part_wide = ny * LANES
@@ -356,7 +358,6 @@
     lane = lanes % SUBS
     w = [float(x) for x in tables.weights[0]]
     q = [float(x) for x in tables.squares[0]]
-    f = [0.5 if k in (0, 7) else 1.0 for k in range(8)]
     parts = range(groups)
 
     def cut(x):
@@ -465,7 +466,6 @@
             at = kk * 64 + index * 16
             ref[at:at + 16, ls(p)] = high
             ref[256 + at:272 + at, ls(p)] = low
-            ref[512 + at:528 + at, ls(p)] = high
 
     def fold_z(kk, pair):
         a, b = pair
@@ -495,23 +495,40 @@
             out.append([a, b])
         return out
 
+    pending = []
+
+    def flush():
+        while pending:
+            pending.pop(0)()
+
     def walk(get, handle, after, with_z=True):
         for p in parts:
             for kk in range(4):
                 for index in (1, 2, 3):
+                    if pending and (kk, index) in SPLIT_AT:
+                        pending.pop(0)()
                     handle(p, kk, index, inner(p, kk, index, get, with_z))
+            flush()
             if p == 0:
                 for kk in range(4):
                     for n, values in enumerate(faces(kk, get, with_z)):
                         handle(n, kk, 0, values)
-            after(p)
+            pending.extend(after(p))
 
     def dot(a, b):
         return jnp.dot(a, b, preferred_element_type=jnp.float32)
 
+    def rows_of(ref, p):
+        return jnp.concatenate([ref[:, ls(p)], ref[0:256, ls(p)]], axis=0)
+
     def multiply(p):
-        a_ref[0:256, ls(p)] = dot(even[...], be_ref[:, ls(p)])
-        a_ref[256:512, ls(p)] = dot(odd[...], bo_ref[:, ls(p)])
+        def first():
+            a_ref[0:256, ls(p)] = dot(even[...], rows_of(be_ref, p))
+
+        def second():
+            a_ref[256:512, ls(p)] = dot(odd[...], rows_of(bo_ref, p))
+
+        return first, second
 
     def point(p, kk, i):
         out = []
@@ -541,7 +558,7 @@
             dirs.append(group)
         store_split(kk, index, p, dirs[0], dirs[1])
 
-    walk(point, put_diag, lambda p: None)
+    walk(point, put_diag, lambda p: ())
     walk(lambda p, kk, i: (v_ref[row(kk, i), ls(p)], v_ref[row(7 - kk, i), ls(p)]),
          put_load, multiply, with_z=False)
 
@@ -603,7 +620,11 @@
         return fold1(kap1 * dot(op1[...], cat3(v)) + mass1_ref[...] * v)
 
     def apply2(v):
-        return fold2(kap1 * dot(op2[...], cat3_small(v))[0:8] + lane_ref[144:152, :] * v)
+        terms = [across(op2[8 * n:8 * n + 8, :], tiles) * (pltpu.roll(v, n, 0) if n else v)
+                 for n in range(SUBS)]
+        while len(terms) > 1:
+            terms = [x + y for x, y in zip(terms[::2], terms[1::2])]
+        return fold2(kap1 * terms[0] + lane_ref[144:152, :] * v)
 
     def coarse(resid):
         inverse = inv1_ref[...]
@@ -625,10 +646,15 @@
         resid = resid - fold1(kap1 * both[64:128] + mass1_ref[...] * e)
         return x + resid * inverse * (1.0 / THETA)
 
+    d_refs = [d_ref, other_ref]
+
+    def turn_over():
+        d_refs.reverse()
+
     def weighted(p, kk, i, a, b):
         scale = sig_w[p] * (w[kk] * w[i])
-        return (kap[p] * a + scale * d_ref[row(kk, i), ls(p)],
-                kap[p] * b + scale * d_ref[row(7 - kk, i), ls(p)])
+        return (kap[p] * a + scale * d_refs[0][row(kk, i), ls(p)],
+                kap[p] * b + scale * d_refs[0][row(7 - kk, i), ls(p)])
 
     def from_halves(p, kk, i):
         e = a_ref[row(kk, i), ls(p)]
@@ -644,7 +670,7 @@
         return r
 
     def second_direction(at, value):
-        return KEEP * d_ref[at] + lower(at, value) * p_ref[at]
+        return KEEP * d_refs[0][at] + lower(at, value) * p_ref[at]
 
     def next_direction(at, value):
         return lower(at, value) * t_ref[at]
@@ -657,7 +683,7 @@
                 for n, i in enumerate(PAIRS[index]):
                     at = (row(k, i), ls(p))
                     group.append(update(at, values[n][s]))
-                    d_ref[at] = group[-1]
+                    d_refs[1][at] = group[-1]
                 dirs.append(group)
             store_split(kk, index, p, dirs[0], dirs[1])
         return handle
@@ -679,58 +705,62 @@
     z_ref[...] = jnp.zeros((512, LANES), jnp.float32)
 
     def collect():
-        z_ref[...] = z_ref[...] + d_ref[:, window]
+        z_ref[...] = z_ref[...] + d_refs[0][:, window]
 
     for step in range(2):
         collect()
         walk(from_halves, put(second_direction), multiply)
+        turn_over()
         collect()
-        low = {}
-
         def reduce(p):
-            both = dot(down0[...], c_ref[0:512, ls(p)])
-            low[p] = both[0:64] + both[64:128] + dot(down0[0:64, :], c_ref[512:1024, ls(p)])
+            def first():
+                both = dot(down0[...], c_ref[0:512, ls(p)])
+                low_ref[:, ls(p)] = both[0:64] + both[64:128]
+
+            def second():
+                low_ref[:, ls(p)] = low_ref[:, ls(p)] + dot(down0[0:64, :], c_ref[512:1024, ls(p)])
+
+            return first, second
 
         walk(from_halves, put_resid, reduce)
-        correction = cat3(coarse(fold1(join([low[p] for p in parts]))))
+        flush()
+        cor_ref[...] = cat3(coarse(fold1(low_ref[...])))
+        turn_over()
         for p in parts:
-            d_ref[:, ls(p)] = dot(up0[0:512, :], correction[:, ls(p)])
-            a_ref[:, ls(p)] = dot(up0[512:1024, :], correction[:, ls(p)])
+            d_refs[0][:, ls(p)] = dot(up0[0:512, :], cor_ref[:, ls(p)])
+            a_ref[:, ls(p)] = dot(up0[512:1024, :], cor_ref[:, ls(p)])
         collect()
         walk(from_whole, put(next_direction), multiply)
+        turn_over()
         collect()
         if step == 0:
             walk(from_halves, put(next_direction), multiply)
+            turn_over()
         else:
-            walk(from_halves, put_last, lambda p: None)
+            walk(from_halves, put_last, lambda p: ())
 
     zero = jnp.zeros((SUBS, wide), jnp.float32)
-    bw, ww, bb = zero, zero, zero
+    sums = [[zero] * 4 for weight in range(3)]
     for k in range(8):
         for i in range(8):
             b = b_ref[row(k, i), :]
-            image_all = b - r_ref[row(k, i), :]
-            fb = b * (f[k] * f[i])
-            bw = bw + fb * image_all
-            ww = ww + image_all * image_all * (f[k] * f[i])
-            bb = bb + fb * b
-    bw, ww, bb = jnp.sum(bw * f_j), jnp.sum(ww * f_j), jnp.sum(bb * f_j)
-    coef = bw / ww
-    rr = zero
-    for k in range(8):
-        for i in range(8):
-            b = b_ref[row(k, i), :]
-            res = b - coef * (b - r_ref[row(k, i), :])
-            rr = rr + res * res * (f[k] * f[i])
-    rr = jnp.sum(rr * f_j)
+            r = r_ref[row(k, i), :]
+            image_all = b - r
+            group = sums[(k in (0, 7)) + (i in (0, 7))]
+            for n, (x, y) in enumerate(((r, image_all), (image_all, image_all), (r, r), (b, b))):
+                group[n] = group[n] + x * y
+    rw, ww, rr, bb = [jnp.sum((a + 0.5 * b + 0.25 * c) * f_j) for a, b, c in zip(*sums)]
+    excess = rw / ww
+    coef = 1.0 + excess
+    rr = rr - rw * excess
     rel_ref[0] = jnp.sqrt(rr / bb)
     place = own_x // groups
     for i in range(8):
         sol = jnp.zeros((SUBS, LANES), jnp.float32)
         res = sol
         for k in range(8):
-            b = b_ref[row(k, i), window]
-            r = b - coef * (b - r_ref[row(k, i), window])
+            r = r_ref[row(k, i), window]
+            r = r - excess * (b_ref[row(k, i), window] - r)
             turn = (k - place) % LANES
             sol = jnp.where(lane == k, pltpu.roll(z_ref[row(k, i), :], turn, 1), sol)
             res = jnp.where(lane == k, pltpu.roll(r, turn, 1), res)
@@ -755,10 +785,11 @@
             jax.ShapeDtypeStruct((1,), jnp.float32),
         ],
         scratch_shapes=[
-            field, field, field, field, field, field, field,
+            field, field, field, field, field, field, field, field,
             pltpu.VMEM((512, LANES), jnp.float32),
-            pltpu.VMEM((768, wide), jnp.bfloat16), pltpu.VMEM((768, wide), jnp.bfloat16),
+            pltpu.VMEM((512, wide), jnp.bfloat16), pltpu.VMEM((512, wide), jnp.bfloat16),
             pltpu.VMEM((1024, wide), jnp.bfloat16), pltpu.VMEM((152, wide), jnp.float32),
+            pltpu.VMEM((64, wide), jnp.float32), pltpu.VMEM((192, wide), jnp.bfloat16),
         ],
         name="solve_all",
     )(*[pltpu.with_memory_space_constraint(x, pltpu.VMEM)

time: 38 us -> 37.4 us (0.984)
  Pallas kernels: 13.3 us -> 12.7 us
    pallas_call x1, Pallas kernels: 12.5 us -> 11.9 us  [solve_all(): pl.pallas_call(lambda *refs: kernel(nx, ny, tables, *refs), in_specs=[vme...]
where the time goes in v5:
time: 37.4 us; the launch traced here: 37.3 us
  waiting for transfers between devices  13.5 us (36%)
  Pallas kernels  12.7 us (34%)
  starting transfers between devices  10.1 us (27%)
  between operations  0.75 us (2%)
    pallas_call x1, Pallas kernels, solve_all(): pl.pallas_call(lambda *refs: kernel(nx, ny, tables, *refs), in_specs=[vme...  11.9 us
    ppermute x4, waiting for transfers between devices, gathered(): other = lax.ppermute(block, 'gx', [(i, i ^ step) for i in range(nx)])  11.6 us
    ppermute x4, starting transfers between devices, gathered(): other = lax.ppermute(block, 'gx', [(i, i ^ step) for i in range(nx)])  7.08 us
    ppermute x1, starting transfers between devices, gathered(): other = lax.ppermute(block, 'gy', [(i, i ^ 1) for i in range(ny)])  3.01 us
    ppermute x1, waiting for transfers between devices, gathered(): other = lax.ppermute(block, 'gy', [(i, i ^ 1) for i in range(ny)])  1.89 us
    pallas_call x1, Pallas kernels, packed_block(): pl.pallas_call(pack_kernel, in_specs=[vmem] * 3, out_specs=vmem, out_shap...  0.86 us
  transfers between devices with their start and end apart: 5, of which 5 were waited for; matrix products, arithmetic and copies ran while one was open for 0% of the time, Pallas kernels for 0%

profile of v5, /device:TPU:0, one launch (start us, length us, event | category | flops | bytes accessed | tf_op | source)
XLA Modules:
  0.0 37.3 jit_solution(13214337119501402468)
XLA Ops:
  0.6 0.9 %pack_block.1 = f32[1,8,8,128]{3,2,1,0:T(8,128)S(1)} custom-call(f32[8,8,128]{2,1,0:T(8,128)} %forcing.1, f32[1,1,16]{2,1,0:T(1,128)} %kappa.1, f32[1,1,16]{2,1,0:T(1,128)} %sigma.1), custom_call_target="tpu_custom_call" | custom-call | tf_op jit(solution)/shard_map/pack_block/pallas_call | solution.py:817
  1.5 3.0 %collective-permute-start = (f32[1,8,8,128]{3,2,1,0:T(8,128)S(1)}, f32[1,8,8,128]{3,2,1,0:T(8,128)S(1)}, u32[]{:S(2)}, u32[]{:S(2)}) collective-permute-start(f32[1,8,8,128]{3,2,1,0:T(8,128)S(1)} %pack_block.1), channel_id=1, source_target_pairs={{0,1},{1,0},{2,3},{3,2},{4,5},{5,4},{6,7},{7,6},{8,9},{9,8},{10,11... | collective-permute-start | bytes 98312 | tf_op jit(solution)/shard_map/ppermute | solution.py:831
  4.5 1.9 %collective-permute-done = f32[1,8,8,128]{3,2,1,0:T(8,128)S(1)} collective-permute-done((f32[1,8,8,128]{3,2,1,0:T(8,128)S(1)}, f32[1,8,8,128]{3,2,1,0:T(8,128)S(1)}, u32[]{:S(2)}, u32[]{:S(2)}) %collective-permute-start) | collective-permute-done | bytes 32800 | tf_op jit(solution)/shard_map/ppermute | solution.py:831
  6.4 3.1 %collective-permute-start.1 = (f32[2,8,8,128]{3,2,1,0:T(8,128)S(1)}, f32[2,8,8,128]{3,2,1,0:T(8,128)S(1)}, u32[]{:S(2)}, u32[]{:S(2)}) collective-permute-start(f32[2,8,8,128]{3,2,1,0:T(8,128)S(1)} %pad_maximum_fusion.2), channel_id=1, source_target_pairs={{0,16},{2,18},{4,20},{6,22},{8,24},{10,26},{12,28},{14,30},{16,0},... | collective-permute-start | bytes 196616 | tf_op jit(solution)/shard_map/ppermute | solution.py:835
  9.5 2.2 %collective-permute-done.1 = f32[2,8,8,128]{3,2,1,0:T(8,128)S(1)} collective-permute-done((f32[2,8,8,128]{3,2,1,0:T(8,128)S(1)}, f32[2,8,8,128]{3,2,1,0:T(8,128)S(1)}, u32[]{:S(2)}, u32[]{:S(2)}) %collective-permute-start.1) | collective-permute-done | bytes 65568 | tf_op jit(solution)/shard_map/ppermute | solution.py:835
  11.8 0.0 copy-start.6
  11.8 0.0 copy-start.7
  11.8 2.0 %collective-permute-start.2 = (f32[4,8,8,128]{3,2,1,0:T(8,128)S(1)}, f32[4,8,8,128]{3,2,1,0:T(8,128)S(1)}, u32[]{:S(2)}, u32[]{:S(2)}) collective-permute-start(f32[4,8,8,128]{3,2,1,0:T(8,128)S(1)} %pad_maximum_fusion.1), channel_id=1, source_target_pairs={{0,8},{2,10},{4,12},{6,14},{8,0},{10,2},{12,4},{14,6},{16,24},{18,... | collective-permute-start | bytes 393224 | tf_op jit(solution)/shard_map/ppermute | solution.py:835
  13.8 0.0 copy-start.4
  13.8 3.1 %collective-permute-done.2 = f32[4,8,8,128]{3,2,1,0:T(8,128)S(1)} collective-permute-done((f32[4,8,8,128]{3,2,1,0:T(8,128)S(1)}, f32[4,8,8,128]{3,2,1,0:T(8,128)S(1)}, u32[]{:S(2)}, u32[]{:S(2)}) %collective-permute-start.2) | collective-permute-done | bytes 131104 | tf_op jit(solution)/shard_map/ppermute | solution.py:835
  16.8 0.0 copy-start.2
  16.8 0.0 copy-start.3
  16.8 0.0 copy-start
  16.9 1.9 %collective-permute-start.3 = (f32[8,8,8,128]{3,2,1,0:T(8,128)S(1)}, f32[8,8,8,128]{3,2,1,0:T(8,128)S(1)}, u32[]{:S(2)}, u32[]{:S(2)}) collective-permute-start(f32[8,8,8,128]{3,2,1,0:T(8,128)S(1)} %pad_maximum_fusion), channel_id=1, source_target_pairs={{0,4},{2,6},{4,0},{6,2},{8,12},{10,14},{12,8},{14,10},{16,20},{18,... | collective-permute-start | bytes 786440 | tf_op jit(solution)/shard_map/ppermute | solution.py:835
  18.8 0.0 copy-start.1
  18.8 0.0 copy-start.5
  18.8 0.0 copy-start.8
  18.8 4.4 %collective-permute-done.3 = f32[8,8,8,128]{3,2,1,0:T(8,128)S(1)} collective-permute-done((f32[8,8,8,128]{3,2,1,0:T(8,128)S(1)}, f32[8,8,8,128]{3,2,1,0:T(8,128)S(1)}, u32[]{:S(2)}, u32[]{:S(2)}) %collective-permute-start.3) | collective-permute-done | bytes 262176 | tf_op jit(solution)/shard_map/ppermute | solution.py:835
  23.3 0.1 collective-permute-start.4
  23.4 1.9 %collective-permute-done.4.refs_1_ = f32[16,8,8,128]{3,2,1,0:T(8,128)S(1)} collective-permute-done((f32[16,8,8,128]{3,2,1,0:T(8,128)S(1)}, f32[16,8,8,128]{3,2,1,0:T(8,128)S(1)}, u32[]{:S(2)}, u32[]{:S(2)}) %collective-permute-start.4) | collective-permute-done | bytes 524320 | tf_op jit(solution)/shard_map/ppermute | solution.py:835
  25.3 0.0 copy-done.6
  25.3 0.0 copy-done.7
  25.3 0.0 copy-done.4
  25.3 0.0 copy-done.2
  25.3 0.0 copy-done.3
  25.3 0.0 copy-done
  25.3 0.0 copy-done.1
  25.3 0.0 copy-done.5
  25.3 0.0 copy-done.8
  25.4 11.9 %solve_all.1 = (f32[8,8,128]{2,1,0:T(8,128)}, f32[8,8,128]{2,1,0:T(8,128)}, f32[1]{0:T(128)}) custom-call(f32[16,8,8,128]{3,2,1,0:T(8,128)S(1)} %constant_dynamic-update-slice_fusion.refs_0_, f32[16,8,8,128]{3,2,1,0:T(8,128)S(1)} %collective-permute-done.4.refs_1_, bf16[256,768]{1,0:T(8,128)(2,1)S(1)} %copy-done.1, bf16[256,768]{1,0:T(8,128)(2,1)S(1)} %copy-done.2, ...), custom_call_target="tpu_custom_call" | custom-call | tf_op jit(solution)/shard_map/solve_all/pallas_call | solution.py:778
  (8 shorter events, 0.1 us)
Async XLA Ops:
  1.5 4.9 %collective-permute-start = (f32[1,8,8,128]{3,2,1,0:T(8,128)S(1)}, f32[1,8,8,128]{3,2,1,0:T(8,128)S(1)}, u32[]{:S(2)}, u32[]{:S(2)}) collective-permute-start(f32[1,8,8,128]{3,2,1,0:T(8,128)S(1)} %pack_block.1), channel_id=1, source_target_pairs={{0,1},{1,0},{2,3},{3,2},{4,5},{5,4},{6,7},{7,6},{8,9},{9,8},{10,11... | collective-permute-start | bytes 98312 | tf_op jit(solution)/shard_map/ppermute | solution.py:831
  6.4 5.4 %collective-permute-start.1 = (f32[2,8,8,128]{3,2,1,0:T(8,128)S(1)}, f32[2,8,8,128]{3,2,1,0:T(8,128)S(1)}, u32[]{:S(2)}, u32[]{:S(2)}) collective-permute-start(f32[2,8,8,128]{3,2,1,0:T(8,128)S(1)} %pad_maximum_fusion.2), channel_id=1, source_target_pairs={{0,16},{2,18},{4,20},{6,22},{8,24},{10,26},{12,28},{14,30},{16,0},... | collective-permute-start | bytes 196616 | tf_op jit(solution)/shard_map/ppermute | solution.py:835
  11.8 13.5 %copy-start.6 = (bf16[128,32]{1,0:T(8,128)(2,1)S(1)}, bf16[128,32]{1,0:T(8,128)(2,1)}, u32[]{:S(2)}) copy-start(bf16[128,32]{1,0:T(8,128)(2,1)} %constant.24.clone.refs_8_) | copy-start | bytes 24580
  11.8 13.5 %copy-start.7 = (f32[64,128]{1,0:T(8,128)S(1)}, f32[64,128]{1,0:T(8,128)}, u32[]{:S(2)}) copy-start(f32[64,128]{1,0:T(8,128)} %constant.25.clone.refs_9_) | copy-start | bytes 98308
  11.8 5.0 %collective-permute-start.2 = (f32[4,8,8,128]{3,2,1,0:T(8,128)S(1)}, f32[4,8,8,128]{3,2,1,0:T(8,128)S(1)}, u32[]{:S(2)}, u32[]{:S(2)}) collective-permute-start(f32[4,8,8,128]{3,2,1,0:T(8,128)S(1)} %pad_maximum_fusion.1), channel_id=1, source_target_pairs={{0,8},{2,10},{4,12},{6,14},{8,0},{10,2},{12,4},{14,6},{16,24},{18,... | collective-permute-start | bytes 393224 | tf_op jit(solution)/shard_map/ppermute | solution.py:835
  13.8 11.5 %copy-start.4 = (f32[168,128]{1,0:T(8,128)S(1)}, f32[168,128]{1,0:T(8,128)}, u32[]{:S(2)}) copy-start(f32[168,128]{1,0:T(8,128)} %constant.26.clone.refs_10_) | copy-start | bytes 258052
  16.8 8.5 %copy-start.2 = (bf16[256,768]{1,0:T(8,128)(2,1)S(1)}, bf16[256,768]{1,0:T(8,128)(2,1)}, u32[]{:S(2)}) copy-start(bf16[256,768]{1,0:T(8,128)(2,1)} %constant.19.clone.refs_3_) | copy-start | bytes 1179652
  16.8 8.5 %copy-start.3 = (bf16[128,512]{1,0:T(8,128)(2,1)S(1)}, bf16[128,512]{1,0:T(8,128)(2,1)}, u32[]{:S(2)}) copy-start(bf16[128,512]{1,0:T(8,128)(2,1)} %constant.20.clone.refs_4_) | copy-start | bytes 393220
  16.8 8.5 %copy-start = (bf16[1024,192]{1,0:T(8,128)(2,1)S(1)}, bf16[1024,192]{1,0:T(8,128)(2,1)}, u32[]{:S(2)}) copy-start(bf16[1024,192]{1,0:T(8,128)(2,1)} %constant.21.clone.refs_5_) | copy-start | bytes 1179652
  16.9 6.4 %collective-permute-start.3 = (f32[8,8,8,128]{3,2,1,0:T(8,128)S(1)}, f32[8,8,8,128]{3,2,1,0:T(8,128)S(1)}, u32[]{:S(2)}, u32[]{:S(2)}) collective-permute-start(f32[8,8,8,128]{3,2,1,0:T(8,128)S(1)} %pad_maximum_fusion), channel_id=1, source_target_pairs={{0,4},{2,6},{4,0},{6,2},{8,12},{10,14},{12,8},{14,10},{16,20},{18,... | collective-permute-start | bytes 786440 | tf_op jit(solution)/shard_map/ppermute | solution.py:835
  18.8 6.5 %copy-start.1 = (bf16[256,768]{1,0:T(8,128)(2,1)S(1)}, bf16[256,768]{1,0:T(8,128)(2,1)}, u32[]{:S(2)}) copy-start(bf16[256,768]{1,0:T(8,128)(2,1)} %constant.18.clone.refs_2_) | copy-start | bytes 1179652
  18.8 6.5 %copy-start.5 = (bf16[64,192]{1,0:T(8,128)(2,1)S(1)}, bf16[64,192]{1,0:T(8,128)(2,1)}, u32[]{:S(2)}) copy-start(bf16[64,192]{1,0:T(8,128)(2,1)} %constant.22.clone.refs_6_) | copy-start | bytes 73732
  18.8 6.5 %copy-start.8 = (bf16[16,192]{1,0:T(8,128)(2,1)S(1)}, bf16[16,192]{1,0:T(8,128)(2,1)}, u32[]{:S(2)}) copy-start(bf16[16,192]{1,0:T(8,128)(2,1)} %constant.23.clone.refs_7_) | copy-start | bytes 18436
  23.3 2.0 %collective-permute-start.4 = (f32[16,8,8,128]{3,2,1,0:T(8,128)S(1)}, f32[16,8,8,128]{3,2,1,0:T(8,128)S(1)}, u32[]{:S(2)}, u32[]{:S(2)}) collective-permute-start(f32[16,8,8,128]{3,2,1,0:T(8,128)S(1)} %constant_dynamic-update-slice_fusion.refs_0_), channel_id=1, source_target_pairs={{0,2},{2,0},{4,6},{6,4},{8,10},{10,8},{12,14},{14,12},{16,18},{18,... | collective-permute-start | bytes 1572872 | tf_op jit(solution)/shard_map/ppermute | solution.py:835

commit v6 on v5

--- a/solution.py
+++ b/solution.py
@@ -341,6 +341,17 @@
         self.rows = np.concatenate(blocks, axis=0)
 
 
+def gather_rounds(nx, ny):
+    dims = []
+    step = nx // 2
+    while step > 1:
+        dims.append((step, 0))
+        step //= 2
+    if ny > 1:
+        dims.insert(len(dims) - 1, (0, 1))
+    return [dims[n:n + 2] for n in range(0, len(dims), 2)]
+
+
 def swap_rows(x, sub):
     return jnp.where(sub == 4, pltpu.roll(x, 5, 0), jnp.where(sub == 7, pltpu.roll(x, 3, 0), x))
 
@@ -416,15 +427,16 @@
         slots = []
         for c in range(SUBS):
             delta = (c * groups + part) ^ own_x
-            slot, bit = jnp.int32(0), 0
-            if ny > 1:
-                slot, bit = y_index ^ own_y, 1
-            step = nx // 2
-            while step > 1:
-                flag = jnp.where((delta & step) != 0, 1, 0)
-                slot = slot + flag * (1 << bit)
-                bit += 1
-                step //= 2
+            slot, size = jnp.int32(0), 1
+            for dims in gather_rounds(nx, ny):
+                flags = [y_index ^ own_y if along_y else jnp.where((delta & along_x) != 0, 1, 0)
+                         for along_x, along_y in dims]
+                if len(dims) == 2:
+                    place = flags[0] * 2 + flags[1] * 3 - flags[0] * flags[1] * 4
+                else:
+                    place = flags[0]
+                slot = slot + place * size
+                size *= 1 << len(dims)
             slots.append(slot)
         blocks = [[jnp.where(use_near, near[slot, i], far[slot, i]) for slot in slots]
                   for i in range(8)]
@@ -826,17 +838,20 @@
 
 def gathered(forcing, kappa, sigma):
     nx, ny = lax.axis_size("gx"), lax.axis_size("gy")
+
+    def swap(block, along_x, along_y):
+        pairs = [(a * ny + b, (a ^ along_x) * ny + (b ^ along_y)) for a in range(nx) for b in range(ny)]
+        return lax.ppermute(block, ("gx", "gy"), pairs)
+
     block = packed_block(forcing, kappa, sigma)
-    if ny > 1:
-        other = lax.ppermute(block, "gy", [(i, i ^ 1) for i in range(ny)])
-        block = jnp.concatenate([block, other], axis=0)
-    step = nx // 2
-    while step:
-        other = lax.ppermute(block, "gx", [(i, i ^ step) for i in range(nx)])
-        if step > 1:
-            block = jnp.concatenate([block, other], axis=0)
-        step //= 2
-    sol, res, rel = solve_all(nx, ny, block, other)
+    for dims in gather_rounds(nx, ny):
+        if len(dims) == 2:
+            (x0, y0), (x1, y1) = dims
+            masks = [(x0 ^ x1, y0 ^ y1), dims[0], dims[1]]
+        else:
+            masks = dims
+        block = jnp.concatenate([block] + [swap(block, *mask) for mask in masks], axis=0)
+    sol, res, rel = solve_all(nx, ny, block, swap(block, 1, 0))
     return sol, res, rel.reshape(())
 
 

time: 37.4 us -> 37 us (0.989)
  local copies, waits for them, and re-layouts: 0.09 us -> 3.32 us
  waiting for transfers between devices: 13.5 us -> 10.4 us
  starting transfers between devices: 10.1 us -> 9.39 us
    unnamed x22 -> x24, local copies, waits for them, and re-layouts: 0.07 us -> 3.31 us
    ppermute x5 -> x7, waiting for transfers between devices: 13.5 us -> 10.4 us  [swap(): return lax.ppermute(block, ('gx', 'gy'), pairs)]
    ppermute x5 -> x7, starting transfers between devices: 10.1 us -> 9.39 us  [swap(): return lax.ppermute(block, ('gx', 'gy'), pairs)]
  transfers between devices with their start and end apart: 5 -> 7, of which waited for: 5 -> 6; matrix products, arithmetic and copies ran while one was open for 0% -> 0% of each run, Pallas kernels for 0% -> 0%
where the time goes in v6:
time: 37 us; the launch traced here: 36.7 us
  Pallas kernels  12.8 us (35%)
  waiting for transfers between devices  10.4 us (28%)
  starting transfers between devices  9.39 us (25%)
  local copies, waits for them, and re-layouts  3.32 us (9%)
  between operations  0.74 us (2%)
    pallas_call x1, Pallas kernels, solve_all(): pl.pallas_call(lambda *refs: kernel(nx, ny, tables, *refs), in_specs=[vme...  11.9 us
    ppermute x7, waiting for transfers between devices, swap(): return lax.ppermute(block, ('gx', 'gy'), pairs)  10.4 us
    ppermute x7, starting transfers between devices, swap(): return lax.ppermute(block, ('gx', 'gy'), pairs)  9.39 us
    unnamed x24, local copies, waits for them, and re-layouts  3.31 us
    pallas_call x1, Pallas kernels, packed_block(): pl.pallas_call(pack_kernel, in_specs=[vmem] * 3, out_specs=vmem, out_shap...  0.9 us
  transfers between devices with their start and end apart: 7, of which 6 were waited for; matrix products, arithmetic and copies ran while one was open for 0% of the time, Pallas kernels for 0%

profile of v6, /device:TPU:0, one launch (start us, length us, event | category | flops | bytes accessed | tf_op | source)
XLA Modules:
  0.0 36.7 jit_solution(14913428771996098834)
XLA Ops:
  0.6 0.0 copy-start.2
  0.6 0.9 %pack_block.1 = f32[1,8,8,128]{3,2,1,0:T(8,128)S(1)} custom-call(f32[8,8,128]{2,1,0:T(8,128)} %forcing.1, f32[1,1,16]{2,1,0:T(1,128)} %kappa.1, f32[1,1,16]{2,1,0:T(1,128)} %sigma.1), custom_call_target="tpu_custom_call" | custom-call | tf_op jit(solution)/shard_map/pack_block/pallas_call | solution.py:829
  1.5 5.1 %collective-permute-start = (f32[1,8,8,128]{3,2,1,0:T(8,128)S(1)}, f32[1,8,8,128]{3,2,1,0:T(8,128)S(1)}, u32[]{:S(2)}, u32[]{:S(2)}) collective-permute-start(f32[1,8,8,128]{3,2,1,0:T(8,128)S(1)} %pack_block.1), channel_id=1, source_target_pairs={{0,24},{1,25},{2,26},{3,27},{4,28},{5,29},{6,30},{7,31},{8,16},{9,... | collective-permute-start | bytes 98312 | tf_op jit(solution)/shard_map/ppermute | solution.py:844
  6.7 0.0 collective-permute-start.1
  6.7 0.6 %collective-permute-start.2 = (f32[1,8,8,128]{3,2,1,0:T(8,128)S(1)}, f32[1,8,8,128]{3,2,1,0:T(8,128)S(1)}, u32[]{:S(2)}, u32[]{:S(2)}) collective-permute-start(f32[1,8,8,128]{3,2,1,0:T(8,128)S(1)} %pack_block.1), channel_id=1, source_target_pairs={{0,8},{1,9},{2,10},{3,11},{4,12},{5,13},{6,14},{7,15},{8,0},{9,1},... | collective-permute-start | bytes 98312 | tf_op jit(solution)/shard_map/ppermute | solution.py:844
  7.3 1.2 %collective-permute-done = f32[1,8,8,128]{3,2,1,0:T(8,128)S(1)} collective-permute-done((f32[1,8,8,128]{3,2,1,0:T(8,128)S(1)}, f32[1,8,8,128]{3,2,1,0:T(8,128)S(1)}, u32[]{:S(2)}, u32[]{:S(2)}) %collective-permute-start) | collective-permute-done | bytes 32800 | tf_op jit(solution)/shard_map/ppermute | solution.py:844
  8.6 2.9 %collective-permute-done.1 = f32[1,8,8,128]{3,2,1,0:T(8,128)S(1)} collective-permute-done((f32[1,8,8,128]{3,2,1,0:T(8,128)S(1)}, f32[1,8,8,128]{3,2,1,0:T(8,128)S(1)}, u32[]{:S(2)}, u32[]{:S(2)}) %collective-permute-start.1) | collective-permute-done | bytes 32800 | tf_op jit(solution)/shard_map/ppermute | solution.py:844
  11.5 0.0 collective-permute-done.2
  11.5 0.0 copy-start.6
  11.5 0.0 copy-start
  11.5 2.5 %collective-permute-start.3 = (f32[4,8,8,128]{3,2,1,0:T(8,128)S(1)}, f32[4,8,8,128]{3,2,1,0:T(8,128)S(1)}, u32[]{:S(2)}, u32[]{:S(2)}) collective-permute-start(f32[4,8,8,128]{3,2,1,0:T(8,128)S(1)} %pad_maximum_fusion), channel_id=1, source_target_pairs={{0,5},{1,4},{2,7},{3,6},{4,1},{5,0},{6,3},{7,2},{8,13},{9,12},{10,... | collective-permute-start | bytes 393224 | tf_op jit(solution)/shard_map/ppermute | solution.py:844
  14.0 0.5 %collective-permute-start.4 = (f32[4,8,8,128]{3,2,1,0:T(8,128)S(1)}, f32[4,8,8,128]{3,2,1,0:T(8,128)S(1)}, u32[]{:S(2)}, u32[]{:S(2)}) collective-permute-start(f32[4,8,8,128]{3,2,1,0:T(8,128)S(1)} %pad_maximum_fusion), channel_id=1, source_target_pairs={{0,1},{1,0},{2,3},{3,2},{4,5},{5,4},{6,7},{7,6},{8,9},{9,8},{10,11... | collective-permute-start | bytes 393224 | tf_op jit(solution)/shard_map/ppermute | solution.py:844
  14.6 0.5 %collective-permute-start.5 = (f32[4,8,8,128]{3,2,1,0:T(8,128)S(1)}, f32[4,8,8,128]{3,2,1,0:T(8,128)S(1)}, u32[]{:S(2)}, u32[]{:S(2)}) collective-permute-start(f32[4,8,8,128]{3,2,1,0:T(8,128)S(1)} %pad_maximum_fusion), channel_id=1, source_target_pairs={{0,4},{1,5},{2,6},{3,7},{4,0},{5,1},{6,2},{7,3},{8,12},{9,13},{10,... | collective-permute-start | bytes 393224 | tf_op jit(solution)/shard_map/ppermute | solution.py:844
  15.1 0.0 copy-start.1
  15.1 2.7 %collective-permute-done.3 = f32[4,8,8,128]{3,2,1,0:T(8,128)S(1)} collective-permute-done((f32[4,8,8,128]{3,2,1,0:T(8,128)S(1)}, f32[4,8,8,128]{3,2,1,0:T(8,128)S(1)}, u32[]{:S(2)}, u32[]{:S(2)}) %collective-permute-start.3) | collective-permute-done | bytes 131104 | tf_op jit(solution)/shard_map/ppermute | solution.py:844
  17.8 1.3 %collective-permute-done.4 = f32[4,8,8,128]{3,2,1,0:T(8,128)S(1)} collective-permute-done((f32[4,8,8,128]{3,2,1,0:T(8,128)S(1)}, f32[4,8,8,128]{3,2,1,0:T(8,128)S(1)}, u32[]{:S(2)}, u32[]{:S(2)}) %collective-permute-start.4) | collective-permute-done | bytes 131104 | tf_op jit(solution)/shard_map/ppermute | solution.py:844
  19.2 0.0 copy-start.5
  19.2 0.4 collective-permute-done.5
  19.5 0.1 collective-permute-start.6
  19.6 1.9 %collective-permute-done.6.refs_1_ = f32[16,8,8,128]{3,2,1,0:T(8,128)S(1)} collective-permute-done((f32[16,8,8,128]{3,2,1,0:T(8,128)S(1)}, f32[16,8,8,128]{3,2,1,0:T(8,128)S(1)}, u32[]{:S(2)}, u32[]{:S(2)}) %collective-permute-start.6) | collective-permute-done | bytes 524320 | tf_op jit(solution)/shard_map/ppermute | solution.py:844
  21.5 0.0 copy-done.2
  21.5 0.0 copy-done.6
  21.5 0.0 copy-done
  21.5 0.0 copy-done.1
  21.5 0.0 copy-done.5
  21.6 0.0 copy-start.3
  21.6 0.9 %copy-done.3 = bf16[128,512]{1,0:T(8,128)(2,1)S(1)} copy-done((bf16[128,512]{1,0:T(8,128)(2,1)S(1)}, bf16[128,512]{1,0:T(8,128)(2,1)}, u32[]{:S(2)}) %copy-start.3) | copy-done | bytes 131096
  22.5 0.0 copy-start.4
  22.5 0.9 %copy-done.4 = f32[168,128]{1,0:T(8,128)S(1)} copy-done((f32[168,128]{1,0:T(8,128)S(1)}, f32[168,128]{1,0:T(8,128)}, u32[]{:S(2)}) %copy-start.4) | copy-done | bytes 86040
  23.4 0.0 copy-start.7
  23.4 0.8 %copy-done.7 = f32[64,128]{1,0:T(8,128)S(1)} copy-done((f32[64,128]{1,0:T(8,128)S(1)}, f32[64,128]{1,0:T(8,128)}, u32[]{:S(2)}) %copy-start.7) | copy-done | bytes 32792
  24.1 0.0 copy-start.8
  24.1 0.7 %copy-done.8 = bf16[16,192]{1,0:T(8,128)(2,1)S(1)} copy-done((bf16[16,192]{1,0:T(8,128)(2,1)S(1)}, bf16[16,192]{1,0:T(8,128)(2,1)}, u32[]{:S(2)}) %copy-start.8) | copy-done | bytes 6168
  24.8 11.9 %solve_all.1 = (f32[8,8,128]{2,1,0:T(8,128)}, f32[8,8,128]{2,1,0:T(8,128)}, f32[1]{0:T(128)}) custom-call(f32[16,8,8,128]{3,2,1,0:T(8,128)S(1)} %constant_dynamic-update-slice_fusion.refs_0_, f32[16,8,8,128]{3,2,1,0:T(8,128)S(1)} %collective-permute-done.6.refs_1_, bf16[256,768]{1,0:T(8,128)(2,1)S(1)} %copy-done.1, bf16[256,768]{1,0:T(8,128)(2,1)S(1)} %copy-done.2, ...), custom_call_target="tpu_custom_call" | custom-call | tf_op jit(solution)/shard_map/solve_all/pallas_call | solution.py:790
  (8 shorter events, 0.1 us)
Async XLA Ops:
  0.6 20.9 %copy-start.2 = (bf16[256,768]{1,0:T(8,128)(2,1)S(1)}, bf16[256,768]{1,0:T(8,128)(2,1)}, u32[]{:S(2)}) copy-start(bf16[256,768]{1,0:T(8,128)(2,1)} %constant.19.clone.refs_3_) | copy-start | bytes 1179652
  1.5 7.0 %collective-permute-start = (f32[1,8,8,128]{3,2,1,0:T(8,128)S(1)}, f32[1,8,8,128]{3,2,1,0:T(8,128)S(1)}, u32[]{:S(2)}, u32[]{:S(2)}) collective-permute-start(f32[1,8,8,128]{3,2,1,0:T(8,128)S(1)} %pack_block.1), channel_id=1, source_target_pairs={{0,24},{1,25},{2,26},{3,27},{4,28},{5,29},{6,30},{7,31},{8,16},{9,... | collective-permute-start | bytes 98312 | tf_op jit(solution)/shard_map/ppermute | solution.py:844
  6.7 4.8 %collective-permute-start.1 = (f32[1,8,8,128]{3,2,1,0:T(8,128)S(1)}, f32[1,8,8,128]{3,2,1,0:T(8,128)S(1)}, u32[]{:S(2)}, u32[]{:S(2)}) collective-permute-start(f32[1,8,8,128]{3,2,1,0:T(8,128)S(1)} %pack_block.1), channel_id=1, source_target_pairs={{0,16},{1,17},{2,18},{3,19},{4,20},{5,21},{6,22},{7,23},{8,24},{9,... | collective-permute-start | bytes 98312 | tf_op jit(solution)/shard_map/ppermute | solution.py:844
  6.7 4.8 %collective-permute-start.2 = (f32[1,8,8,128]{3,2,1,0:T(8,128)S(1)}, f32[1,8,8,128]{3,2,1,0:T(8,128)S(1)}, u32[]{:S(2)}, u32[]{:S(2)}) collective-permute-start(f32[1,8,8,128]{3,2,1,0:T(8,128)S(1)} %pack_block.1), channel_id=1, source_target_pairs={{0,8},{1,9},{2,10},{3,11},{4,12},{5,13},{6,14},{7,15},{8,0},{9,1},... | collective-permute-start | bytes 98312 | tf_op jit(solution)/shard_map/ppermute | solution.py:844
  11.5 10.0 %copy-start.6 = (bf16[128,32]{1,0:T(8,128)(2,1)S(1)}, bf16[128,32]{1,0:T(8,128)(2,1)}, u32[]{:S(2)}) copy-start(bf16[128,32]{1,0:T(8,128)(2,1)} %constant.24.clone.refs_8_) | copy-start | bytes 24580
  11.5 10.0 %copy-start = (bf16[1024,192]{1,0:T(8,128)(2,1)S(1)}, bf16[1024,192]{1,0:T(8,128)(2,1)}, u32[]{:S(2)}) copy-start(bf16[1024,192]{1,0:T(8,128)(2,1)} %constant.21.clone.refs_5_) | copy-start | bytes 1179652
  11.5 6.3 %collective-permute-start.3 = (f32[4,8,8,128]{3,2,1,0:T(8,128)S(1)}, f32[4,8,8,128]{3,2,1,0:T(8,128)S(1)}, u32[]{:S(2)}, u32[]{:S(2)}) collective-permute-start(f32[4,8,8,128]{3,2,1,0:T(8,128)S(1)} %pad_maximum_fusion), channel_id=1, source_target_pairs={{0,5},{1,4},{2,7},{3,6},{4,1},{5,0},{6,3},{7,2},{8,13},{9,12},{10,... | collective-permute-start | bytes 393224 | tf_op jit(solution)/shard_map/ppermute | solution.py:844
  14.0 5.1 %collective-permute-start.4 = (f32[4,8,8,128]{3,2,1,0:T(8,128)S(1)}, f32[4,8,8,128]{3,2,1,0:T(8,128)S(1)}, u32[]{:S(2)}, u32[]{:S(2)}) collective-permute-start(f32[4,8,8,128]{3,2,1,0:T(8,128)S(1)} %pad_maximum_fusion), channel_id=1, source_target_pairs={{0,1},{1,0},{2,3},{3,2},{4,5},{5,4},{6,7},{7,6},{8,9},{9,8},{10,11... | collective-permute-start | bytes 393224 | tf_op jit(solution)/shard_map/ppermute | solution.py:844
  14.6 5.0 %collective-permute-start.5 = (f32[4,8,8,128]{3,2,1,0:T(8,128)S(1)}, f32[4,8,8,128]{3,2,1,0:T(8,128)S(1)}, u32[]{:S(2)}, u32[]{:S(2)}) collective-permute-start(f32[4,8,8,128]{3,2,1,0:T(8,128)S(1)} %pad_maximum_fusion), channel_id=1, source_target_pairs={{0,4},{1,5},{2,6},{3,7},{4,0},{5,1},{6,2},{7,3},{8,12},{9,13},{10,... | collective-permute-start | bytes 393224 | tf_op jit(solution)/shard_map/ppermute | solution.py:844
  15.1 6.4 %copy-start.1 = (bf16[256,768]{1,0:T(8,128)(2,1)S(1)}, bf16[256,768]{1,0:T(8,128)(2,1)}, u32[]{:S(2)}) copy-start(bf16[256,768]{1,0:T(8,128)(2,1)} %constant.18.clone.refs_2_) | copy-start | bytes 1179652
  19.2 2.4 %copy-start.5 = (bf16[64,192]{1,0:T(8,128)(2,1)S(1)}, bf16[64,192]{1,0:T(8,128)(2,1)}, u32[]{:S(2)}) copy-start(bf16[64,192]{1,0:T(8,128)(2,1)} %constant.22.clone.refs_6_) | copy-start | bytes 73732
  19.5 2.0 %collective-permute-start.6 = (f32[16,8,8,128]{3,2,1,0:T(8,128)S(1)}, f32[16,8,8,128]{3,2,1,0:T(8,128)S(1)}, u32[]{:S(2)}, u32[]{:S(2)}) collective-permute-start(f32[16,8,8,128]{3,2,1,0:T(8,128)S(1)} %constant_dynamic-update-slice_fusion.refs_0_), channel_id=1, source_target_pairs={{0,2},{1,3},{2,0},{3,1},{4,6},{5,7},{6,4},{7,5},{8,10},{9,11},{10,... | collective-permute-start | bytes 1572872 | tf_op jit(solution)/shard_map/ppermute | solution.py:844
  21.6 0.9 %copy-start.3 = (bf16[128,512]{1,0:T(8,128)(2,1)S(1)}, bf16[128,512]{1,0:T(8,128)(2,1)}, u32[]{:S(2)}) copy-start(bf16[128,512]{1,0:T(8,128)(2,1)} %constant.20.clone.refs_4_) | copy-start | bytes 393220
  22.5 0.9 %copy-start.4 = (f32[168,128]{1,0:T(8,128)S(1)}, f32[168,128]{1,0:T(8,128)}, u32[]{:S(2)}) copy-start(f32[168,128]{1,0:T(8,128)} %constant.26.clone.refs_10_) | copy-start | bytes 258052
  23.4 0.8 %copy-start.7 = (f32[64,128]{1,0:T(8,128)S(1)}, f32[64,128]{1,0:T(8,128)}, u32[]{:S(2)}) copy-start(f32[64,128]{1,0:T(8,128)} %constant.25.clone.refs_9_) | copy-start | bytes 98308
  24.1 0.7 %copy-start.8 = (bf16[16,192]{1,0:T(8,128)(2,1)S(1)}, bf16[16,192]{1,0:T(8,128)(2,1)}, u32[]{:S(2)}) copy-start(bf16[16,192]{1,0:T(8,128)(2,1)} %constant.23.clone.refs_7_) | copy-start | bytes 18436

commit v7 on v6

--- a/solution.py
+++ b/solution.py
@@ -356,7 +356,17 @@
     return jnp.where(sub == 4, pltpu.roll(x, 5, 0), jnp.where(sub == 7, pltpu.roll(x, 3, 0), x))
 
 
-def kernel(nx, ny, tables, near, far, even, odd, down0, up0, op1, down1, up1, op2, rows,
+def kernel(nx, ny, tables, near, far, *refs):
+    count = (len(refs) - 19) // 2
+    sources, rest = refs[:count], refs[count:]
+    copies = [pltpu.make_async_copy(source, place, rest[-1].at[n])
+              for n, (source, place) in enumerate(zip(sources, rest[-1 - count:-1]))]
+    for copy in reversed(copies):
+        copy.start()
+    solve(nx, ny, tables, near, far, copies, *rest[-1 - count:-1], *rest[:-1 - count])
+
+
+def solve(nx, ny, tables, near, far, copies, even, odd, down0, up0, op1, down1, up1, op2, rows,
            sol_ref, res_ref, rel_ref, b_ref, r_ref, d_ref, other_ref, v_ref, p_ref, t_ref, a_ref, z_ref,
            be_ref, bo_ref, c_ref, lane_ref, low_ref, cor_ref):
     groups = nx // SUBS
@@ -458,6 +468,7 @@
                 v_ref[row(k, i), at] = b[k]
             v_ref[row(7, i), at] = pltpu.roll(b[0], down, 1)
         lane_ref[0:8, at] = blocks[0][7]
+    copies[-1].wait()
     kap1 = lane_ref[0:1, :]
     sig1 = lane_ref[1:2, :]
     w_j = across(rows[0:8, :], ny)
@@ -571,6 +582,8 @@
         store_split(kk, index, p, dirs[0], dirs[1])
 
     walk(point, put_diag, lambda p: ())
+    for copy in copies[:-1]:
+        copy.wait()
     walk(lambda p, kk, i: (v_ref[row(kk, i), ls(p)], v_ref[row(7 - kk, i), ls(p)]),
          put_load, multiply, with_z=False)
 
@@ -789,7 +802,7 @@
     field = pltpu.VMEM((512, wide), jnp.float32)
     return pl.pallas_call(
         lambda *refs: kernel(nx, ny, tables, *refs),
-        in_specs=[vmem] * 11,
+        in_specs=[vmem] * 2 + [pl.BlockSpec(memory_space=pltpu.HBM)] * len(consts),
         out_specs=[vmem, vmem, pl.BlockSpec(memory_space=pltpu.SMEM)],
         out_shape=[
             jax.ShapeDtypeStruct(near.shape[1:], jnp.float32),
@@ -802,10 +815,12 @@
             pltpu.VMEM((512, wide), jnp.bfloat16), pltpu.VMEM((512, wide), jnp.bfloat16),
             pltpu.VMEM((1024, wide), jnp.bfloat16), pltpu.VMEM((152, wide), jnp.float32),
             pltpu.VMEM((64, wide), jnp.float32), pltpu.VMEM((192, wide), jnp.bfloat16),
+            *[pltpu.VMEM(c.shape, c.dtype) for c in consts],
+            pltpu.SemaphoreType.DMA((len(consts),)),
         ],
         name="solve_all",
-    )(*[pltpu.with_memory_space_constraint(x, pltpu.VMEM)
-             for x in (near, far, *[jnp.asarray(c) for c in consts])])
+    )(*[pltpu.with_memory_space_constraint(x, pltpu.VMEM) for x in (near, far)],
+      *[jnp.asarray(c) for c in consts])
 
 
 def pack_kernel(forcing, kappa, sigma, out_ref, coef_ref):

time: 37 us -> 34.8 us (0.941)
  local copies, waits for them, and re-layouts: 3.32 us -> 0.05 us
  Pallas kernels: 12.8 us -> 14 us
    unnamed x24 -> x6, local copies, waits for them, and re-layouts: 3.31 us -> 0.04 us
    pallas_call x1, Pallas kernels: 11.9 us -> 13.2 us  [solve_all(): pl.pallas_call(lambda *refs: kernel(nx, ny, tables, *refs), in_specs=[vme...]
where the time goes in v7:
time: 34.8 us; the launch traced here: 34.6 us
  Pallas kernels  14 us (40%)
  waiting for transfers between devices  10.5 us (30%)
  starting transfers between devices  9.39 us (27%)
  between operations  0.67 us (2%)
    pallas_call x1, Pallas kernels, solve_all(): pl.pallas_call(lambda *refs: kernel(nx, ny, tables, *refs), in_specs=[vme...  13.2 us
    ppermute x7, waiting for transfers between devices, swap(): return lax.ppermute(block, ('gx', 'gy'), pairs)  10.5 us
    ppermute x7, starting transfers between devices, swap(): return lax.ppermute(block, ('gx', 'gy'), pairs)  9.39 us
    pallas_call x1, Pallas kernels, packed_block(): pl.pallas_call(pack_kernel, in_specs=[vmem] * 3, out_specs=vmem, out_shap...  0.86 us
  transfers between devices with their start and end apart: 7, of which 6 were waited for; matrix products, arithmetic and copies ran while one was open for 0% of the time, Pallas kernels for 0%

profile of v7, /device:TPU:0, one launch (start us, length us, event | category | flops | bytes accessed | tf_op | source)
XLA Modules:
  0.0 34.6 jit_solution(5006784773717153207)
XLA Ops:
  0.6 0.9 %pack_block.1 = f32[1,8,8,128]{3,2,1,0:T(8,128)S(1)} custom-call(f32[8,8,128]{2,1,0:T(8,128)} %forcing.1, f32[1,1,16]{2,1,0:T(1,128)} %kappa.1, f32[1,1,16]{2,1,0:T(1,128)} %sigma.1), custom_call_target="tpu_custom_call" | custom-call | tf_op jit(solution)/shard_map/pack_block/pallas_call | solution.py:844
  1.5 5.1 %collective-permute-start = (f32[1,8,8,128]{3,2,1,0:T(8,128)S(1)}, f32[1,8,8,128]{3,2,1,0:T(8,128)S(1)}, u32[]{:S(2)}, u32[]{:S(2)}) collective-permute-start(f32[1,8,8,128]{3,2,1,0:T(8,128)S(1)} %pack_block.1), channel_id=1, source_target_pairs={{0,24},{1,25},{2,26},{3,27},{4,28},{5,29},{6,30},{7,31},{8,16},{9,... | collective-permute-start | bytes 98312 | tf_op jit(solution)/shard_map/ppermute | solution.py:859
  6.6 0.0 collective-permute-start.1
  6.6 0.6 %collective-permute-start.2 = (f32[1,8,8,128]{3,2,1,0:T(8,128)S(1)}, f32[1,8,8,128]{3,2,1,0:T(8,128)S(1)}, u32[]{:S(2)}, u32[]{:S(2)}) collective-permute-start(f32[1,8,8,128]{3,2,1,0:T(8,128)S(1)} %pack_block.1), channel_id=1, source_target_pairs={{0,8},{1,9},{2,10},{3,11},{4,12},{5,13},{6,14},{7,15},{8,0},{9,1},... | collective-permute-start | bytes 98312 | tf_op jit(solution)/shard_map/ppermute | solution.py:859
  7.3 1.2 %collective-permute-done = f32[1,8,8,128]{3,2,1,0:T(8,128)S(1)} collective-permute-done((f32[1,8,8,128]{3,2,1,0:T(8,128)S(1)}, f32[1,8,8,128]{3,2,1,0:T(8,128)S(1)}, u32[]{:S(2)}, u32[]{:S(2)}) %collective-permute-start) | collective-permute-done | bytes 32800 | tf_op jit(solution)/shard_map/ppermute | solution.py:859
  8.5 2.9 %collective-permute-done.1 = f32[1,8,8,128]{3,2,1,0:T(8,128)S(1)} collective-permute-done((f32[1,8,8,128]{3,2,1,0:T(8,128)S(1)}, f32[1,8,8,128]{3,2,1,0:T(8,128)S(1)}, u32[]{:S(2)}, u32[]{:S(2)}) %collective-permute-start.1) | collective-permute-done | bytes 32800 | tf_op jit(solution)/shard_map/ppermute | solution.py:859
  11.4 0.0 collective-permute-done.2
  11.4 2.5 %collective-permute-start.3 = (f32[4,8,8,128]{3,2,1,0:T(8,128)S(1)}, f32[4,8,8,128]{3,2,1,0:T(8,128)S(1)}, u32[]{:S(2)}, u32[]{:S(2)}) collective-permute-start(f32[4,8,8,128]{3,2,1,0:T(8,128)S(1)} %pad_maximum_fusion), channel_id=1, source_target_pairs={{0,5},{1,4},{2,7},{3,6},{4,1},{5,0},{6,3},{7,2},{8,13},{9,12},{10,... | collective-permute-start | bytes 393224 | tf_op jit(solution)/shard_map/ppermute | solution.py:859
  14.0 0.5 %collective-permute-start.4 = (f32[4,8,8,128]{3,2,1,0:T(8,128)S(1)}, f32[4,8,8,128]{3,2,1,0:T(8,128)S(1)}, u32[]{:S(2)}, u32[]{:S(2)}) collective-permute-start(f32[4,8,8,128]{3,2,1,0:T(8,128)S(1)} %pad_maximum_fusion), channel_id=1, source_target_pairs={{0,1},{1,0},{2,3},{3,2},{4,5},{5,4},{6,7},{7,6},{8,9},{9,8},{10,11... | collective-permute-start | bytes 393224 | tf_op jit(solution)/shard_map/ppermute | solution.py:859
  14.5 0.5 %collective-permute-start.5 = (f32[4,8,8,128]{3,2,1,0:T(8,128)S(1)}, f32[4,8,8,128]{3,2,1,0:T(8,128)S(1)}, u32[]{:S(2)}, u32[]{:S(2)}) collective-permute-start(f32[4,8,8,128]{3,2,1,0:T(8,128)S(1)} %pad_maximum_fusion), channel_id=1, source_target_pairs={{0,4},{1,5},{2,6},{3,7},{4,0},{5,1},{6,2},{7,3},{8,12},{9,13},{10,... | collective-permute-start | bytes 393224 | tf_op jit(solution)/shard_map/ppermute | solution.py:859
  15.0 2.7 %collective-permute-done.3 = f32[4,8,8,128]{3,2,1,0:T(8,128)S(1)} collective-permute-done((f32[4,8,8,128]{3,2,1,0:T(8,128)S(1)}, f32[4,8,8,128]{3,2,1,0:T(8,128)S(1)}, u32[]{:S(2)}, u32[]{:S(2)}) %collective-permute-start.3) | collective-permute-done | bytes 131104 | tf_op jit(solution)/shard_map/ppermute | solution.py:859
  17.7 1.3 %collective-permute-done.4 = f32[4,8,8,128]{3,2,1,0:T(8,128)S(1)} collective-permute-done((f32[4,8,8,128]{3,2,1,0:T(8,128)S(1)}, f32[4,8,8,128]{3,2,1,0:T(8,128)S(1)}, u32[]{:S(2)}, u32[]{:S(2)}) %collective-permute-start.4) | collective-permute-done | bytes 131104 | tf_op jit(solution)/shard_map/ppermute | solution.py:859
  19.1 0.4 %collective-permute-done.5 = f32[4,8,8,128]{3,2,1,0:T(8,128)S(1)} collective-permute-done((f32[4,8,8,128]{3,2,1,0:T(8,128)S(1)}, f32[4,8,8,128]{3,2,1,0:T(8,128)S(1)}, u32[]{:S(2)}, u32[]{:S(2)}) %collective-permute-start.5) | collective-permute-done | bytes 131104 | tf_op jit(solution)/shard_map/ppermute | solution.py:859
  19.5 0.1 collective-permute-start.6
  19.6 1.9 %collective-permute-done.6.refs_1_ = f32[16,8,8,128]{3,2,1,0:T(8,128)S(1)} collective-permute-done((f32[16,8,8,128]{3,2,1,0:T(8,128)S(1)}, f32[16,8,8,128]{3,2,1,0:T(8,128)S(1)}, u32[]{:S(2)}, u32[]{:S(2)}) %collective-permute-start.6) | collective-permute-done | bytes 524320 | tf_op jit(solution)/shard_map/ppermute | solution.py:859
  21.4 13.2 %solve_all.1 = (f32[8,8,128]{2,1,0:T(8,128)}, f32[8,8,128]{2,1,0:T(8,128)}, f32[1]{0:T(128)}) custom-call(f32[16,8,8,128]{3,2,1,0:T(8,128)S(1)} %constant_dynamic-update-slice_fusion.refs_0_, f32[16,8,8,128]{3,2,1,0:T(8,128)S(1)} %collective-permute-done.6.refs_1_, bf16[256,768]{1,0:T(8,128)(2,1)} %constant.18.clone.refs_2_, ...), custom_call_target="tpu_custom_call" | custom-call | tf_op jit(solution)/shard_map/solve_all/pallas_call | solution.py:803
  (8 shorter events, 0.1 us)
Async XLA Ops:
  1.5 7.0 %collective-permute-start = (f32[1,8,8,128]{3,2,1,0:T(8,128)S(1)}, f32[1,8,8,128]{3,2,1,0:T(8,128)S(1)}, u32[]{:S(2)}, u32[]{:S(2)}) collective-permute-start(f32[1,8,8,128]{3,2,1,0:T(8,128)S(1)} %pack_block.1), channel_id=1, source_target_pairs={{0,24},{1,25},{2,26},{3,27},{4,28},{5,29},{6,30},{7,31},{8,16},{9,... | collective-permute-start | bytes 98312 | tf_op jit(solution)/shard_map/ppermute | solution.py:859
  6.6 4.8 %collective-permute-start.1 = (f32[1,8,8,128]{3,2,1,0:T(8,128)S(1)}, f32[1,8,8,128]{3,2,1,0:T(8,128)S(1)}, u32[]{:S(2)}, u32[]{:S(2)}) collective-permute-start(f32[1,8,8,128]{3,2,1,0:T(8,128)S(1)} %pack_block.1), channel_id=1, source_target_pairs={{0,16},{1,17},{2,18},{3,19},{4,20},{5,21},{6,22},{7,23},{8,24},{9,... | collective-permute-start | bytes 98312 | tf_op jit(solution)/shard_map/ppermute | solution.py:859
  6.6 4.8 %collective-permute-start.2 = (f32[1,8,8,128]{3,2,1,0:T(8,128)S(1)}, f32[1,8,8,128]{3,2,1,0:T(8,128)S(1)}, u32[]{:S(2)}, u32[]{:S(2)}) collective-permute-start(f32[1,8,8,128]{3,2,1,0:T(8,128)S(1)} %pack_block.1), channel_id=1, source_target_pairs={{0,8},{1,9},{2,10},{3,11},{4,12},{5,13},{6,14},{7,15},{8,0},{9,1},... | collective-permute-start | bytes 98312 | tf_op jit(solution)/shard_map/ppermute | solution.py:859
  11.4 6.3 %collective-permute-start.3 = (f32[4,8,8,128]{3,2,1,0:T(8,128)S(1)}, f32[4,8,8,128]{3,2,1,0:T(8,128)S(1)}, u32[]{:S(2)}, u32[]{:S(2)}) collective-permute-start(f32[4,8,8,128]{3,2,1,0:T(8,128)S(1)} %pad_maximum_fusion), channel_id=1, source_target_pairs={{0,5},{1,4},{2,7},{3,6},{4,1},{5,0},{6,3},{7,2},{8,13},{9,12},{10,... | collective-permute-start | bytes 393224 | tf_op jit(solution)/shard_map/ppermute | solution.py:859
  14.0 5.1 %collective-permute-start.4 = (f32[4,8,8,128]{3,2,1,0:T(8,128)S(1)}, f32[4,8,8,128]{3,2,1,0:T(8,128)S(1)}, u32[]{:S(2)}, u32[]{:S(2)}) collective-permute-start(f32[4,8,8,128]{3,2,1,0:T(8,128)S(1)} %pad_maximum_fusion), channel_id=1, source_target_pairs={{0,1},{1,0},{2,3},{3,2},{4,5},{5,4},{6,7},{7,6},{8,9},{9,8},{10,11... | collective-permute-start | bytes 393224 | tf_op jit(solution)/shard_map/ppermute | solution.py:859
  14.5 5.0 %collective-permute-start.5 = (f32[4,8,8,128]{3,2,1,0:T(8,128)S(1)}, f32[4,8,8,128]{3,2,1,0:T(8,128)S(1)}, u32[]{:S(2)}, u32[]{:S(2)}) collective-permute-start(f32[4,8,8,128]{3,2,1,0:T(8,128)S(1)} %pad_maximum_fusion), channel_id=1, source_target_pairs={{0,4},{1,5},{2,6},{3,7},{4,0},{5,1},{6,2},{7,3},{8,12},{9,13},{10,... | collective-permute-start | bytes 393224 | tf_op jit(solution)/shard_map/ppermute | solution.py:859
  19.5 2.0 %collective-permute-start.6 = (f32[16,8,8,128]{3,2,1,0:T(8,128)S(1)}, f32[16,8,8,128]{3,2,1,0:T(8,128)S(1)}, u32[]{:S(2)}, u32[]{:S(2)}) collective-permute-start(f32[16,8,8,128]{3,2,1,0:T(8,128)S(1)} %constant_dynamic-update-slice_fusion.refs_0_), channel_id=1, source_target_pairs={{0,2},{1,3},{2,0},{3,1},{4,6},{5,7},{6,4},{7,5},{8,10},{9,11},{10,... | collective-permute-start | bytes 1572872 | tf_op jit(solution)/shard_map/ppermute | solution.py:859
